TPU v7x, 32 devices: a whole 2x2x4 slice. The times are simulated.
32 devices in a mesh: segment: 8 (over z, x), dp: 4 (over y, core).
Axes of the slice: x: 2, y: 2, z: 4, core: 2. Of those that a mesh axis runs over, the one named last changes fastest.
Arguments:
- src_embed: bfloat16 [16, 128, 2048], P('dp', None, 'segment'), parts along dimension 0, may hold values from -6 to 6
- tgt_embed: bfloat16 [16, 128, 2048], P('dp', None, 'segment'), parts along dimension 0, may hold values from -6 to 6
- src_lengths: int32 [16], P('dp'), parts along dimension 0, may hold values from 32 to 128
- tgt_lengths: int32 [16], P('dp'), parts along dimension 0, may hold values from 32 to 128
- attn_in: bfloat16 [8, 2048, 3072], P('segment'), may hold values from -0.125 to 0.125
- attn_out: bfloat16 [8, 1024, 2048], P('segment'), may hold values from -0.375 to 0.375
- norm_gain: float32 [4, 2048], replicated, may hold values from 0.25 to 1.75
- final_gain: float32 [2048], replicated, may hold values from 0.25 to 1.75
Outputs:
- decoded: bfloat16 [16, 128, 2048], P('dp', None, 'segment'), parts along dimension 0
There are 4 independent parts, one for each index of `dp`. A program takes and returns all parts, laid end to end along the dimension named above; an argument that names none is the same for every part. Nothing has to cross between parts.
Inputs may be any that keep to these rules, and one draw needn't show every extreme that they name: `src_lengths`: keys at positions below a sequence's length are its real tokens. `tgt_lengths`: keys at positions below a sequence's length are its real tokens.
All inputs are finite; a program needn't handle non-finite values.
Results may differ from a plain program's by a relative error of at most 0.015.
Values may be sent and summed in bfloat16 or wider, within the bound.
No kernel may reach another device: no remote copies, remote signals or barrier semaphores. Data moves between devices by JAX's collectives and lax.ppermute only.
A program may use at most 64 MiB of HBM per device.

v0:
```python
import functools

import jax
import jax.numpy as jnp
from jax import lax
from jax.experimental import pallas as pl
from jax.experimental.pallas import tpu as pltpu
from jax.sharding import PartitionSpec as P

HEAD = 64
SECTIONS = 4
CHUNKS = 1

epsilon = 1e-06
score_scale = 0.125


VMEM = pl.BlockSpec(memory_space=pltpu.VMEM)
ANY = pl.BlockSpec(memory_space=pl.ANY)
SMEM = pl.BlockSpec(memory_space=pltpu.SMEM)
f32 = jnp.float32
bf16 = jnp.bfloat16


def dot(a, b):
    return jnp.dot(a, b, preferred_element_type=f32)


def column_tile(width):
    return 512 if width % 512 == 0 else width


def params(vmem):
    return pltpu.CompilerParams(vmem_limit_bytes=vmem)


def scaled(x_refs, gain_ref, part, group, share, sections):
    squares = 0.0
    lhs = []
    per = sections // len(x_refs)
    for z in range(sections):
        ref = x_refs[z // per]
        at = (z % per) * share
        x = ref[:, at : at + share].astype(f32)
        squares = squares + jnp.sum(x * x, axis=-1, keepdims=True)
        column = pl.multiple_of((z * group + part) * share, share)
        lhs.append((x * gain_ref[:, pl.ds(column, share)]).astype(bf16))
    return lhs, squares


def rows_of(z, part, group, share):
    return pl.ds(pl.multiple_of((z * group + part) * share, share), share)


def project(lhs_q, lhs_kv, w_ref, parts, group, share, head_cols, emit):
    tile = column_tile(head_cols)
    for start in range(0, 3 * head_cols, tile):
        total = None
        for (part, lq), (_, lk) in zip(zip(parts, lhs_q), zip(parts, lhs_kv)):
            source = lq if start < head_cols else lk
            for z, block in enumerate(source):
                rows = rows_of(z, part, group, share)
                term = dot(block, w_ref[rows, start : start + tile])
                total = term if total is None else total + term
        emit(start, tile, total)


def own_kernel(group, same, t, table, after, *refs):
    scal = [table[t, i] for i in range(4)]
    n = CHUNKS
    xk = refs[:n]
    refs = refs[n:]
    if same:
        xq = xk
    else:
        xq = refs[:n]
        refs = refs[n:]
    gq, gk, w, acc, sums = refs
    head_cols = w.shape[1] // 3
    share = w.shape[0] // (group * SECTIONS)

    @pl.when(scal[1] == 1)
    def _():
        part = scal[0]
        lk, sk = scaled(xk, gk, part, group, share, SECTIONS)
        lq, sq = scaled(xq, gq, part, group, share, SECTIONS)

        def emit(start, tile, total):
            acc[:, start : start + tile] = total

        project([lq], [lk], w, [part], group, share, head_cols, emit)
        sums[:, 0:128] = jnp.broadcast_to(sq, (sq.shape[0], 128))
        sums[:, 128:256] = jnp.broadcast_to(sk, (sk.shape[0], 128))


def rest_kernel(group, same, t, table, after, *refs):
    scal = [table[t, i] for i in range(4)]
    n = CHUNKS * (group - 1)
    xk = refs[:n]
    refs = refs[n:]
    if same:
        xq = xk
    else:
        xq = refs[:n]
        refs = refs[n:]
    gq, gk, w, wo, acc, sums = refs[:6]
    sends = refs[6 : 6 + n]
    mix, qkv = refs[6 + n :]
    head_cols = w.shape[1] // 3
    width = w.shape[0]
    share = width // (group * SECTIONS)
    rows = mix.shape[0]

    @pl.when(scal[1] == 1)
    def _():
        me = scal[0]
        parts, lqs, lks = [], [], []
        sq = sums[:, 0:1]
        sk = sums[:, 128:129]
        for k in range(1, group):
            part = lax.rem(me + group - k, group)
            at = CHUNKS * (k - 1)
            lk, s = scaled(xk[at : at + CHUNKS], gk, part, group, share, SECTIONS)
            sk = sk + s
            lq, s = scaled(xq[at : at + CHUNKS], gq, part, group, share, SECTIONS)
            sq = sq + s
            parts.append(part)
            lqs.append(lq)
            lks.append(lk)
        rq = lax.rsqrt(sq / width + epsilon)
        rk = lax.rsqrt(sk / width + epsilon)

        def emit(start, tile, total):
            scale = rq if start < head_cols else rk
            total = (acc[:, start : start + tile] + total) * scale
            qkv[:, start : start + tile] = total.astype(bf16)

        project(lqs, lks, w, parts, group, share, head_cols, emit)

        query = lax.broadcasted_iota(jnp.int32, (rows, rows), 0)
        key = lax.broadcasted_iota(jnp.int32, (rows, rows), 1)
        allowed = (key < scal[2]) & ((key <= query) | (scal[3] == 0))
        allowed = jnp.concatenate([allowed.astype(f32)] * 2, 0) > 0.5
        lane = lax.broadcasted_iota(jnp.int32, (rows, 2 * HEAD), 1)
        low = lane < HEAD
        zero = jnp.zeros((), bf16)
        for at in range(0, head_cols, 2 * HEAD):
            q = qkv[:, at : at + 2 * HEAD]
            k = qkv[:, head_cols + at : head_cols + at + 2 * HEAD]
            v = qkv[:, 2 * head_cols + at : 2 * head_cols + at + 2 * HEAD]
            both = jnp.concatenate([jnp.where(low, q, zero), jnp.where(low, zero, q)], 0)
            scores = lax.dot_general(
                both, k, (((1,), (1,)), ((), ())), preferred_element_type=f32
            )
            scores = jnp.where(allowed, scores * score_scale, -1000000000.0)
            top = jnp.max(scores, axis=-1, keepdims=True)
            e = jnp.exp(scores - top)
            weights = (e * (1.0 / jnp.sum(e, axis=-1, keepdims=True))).astype(bf16)
            out = dot(weights, v)
            mix[:, at : at + 2 * HEAD] = jnp.where(low, out[:rows], out[rows:]).astype(bf16)

        mixture = mix[...]
        per = SECTIONS // CHUNKS
        for k in range(1, group):
            part = lax.rem(me + k, group)
            for z in range(SECTIONS):
                ref = sends[(k - 1) * CHUNKS + z // per]
                column = rows_of(z, part, group, share)
                at = (z % per) * share
                ref[:, at : at + share] = dot(mixture, wo[:, column]).astype(bf16)


def tail_kernel(group, t, table, mix, *refs):
    scal = [table[t, i] for i in range(4)]
    xq = refs[:CHUNKS]
    wo = refs[CHUNKS]
    bases = refs[CHUNKS + 1 :]
    share = wo.shape[1] // (group * SECTIONS)

    @pl.when(scal[1] == 1)
    def _():
        mixture = mix[...]
        per = SECTIONS // CHUNKS
        for z in range(SECTIONS):
            column = rows_of(z, scal[0], group, share)
            at = (z % per) * share
            res = xq[z // per][:, at : at + share].astype(f32)
            bases[z // per][:, at : at + share] = dot(mixture, wo[:, column]) + res


def hold_weights(w_in, w_out):
    w_in = pltpu.with_memory_space_constraint(w_in, pltpu.VMEM)
    w_out = pltpu.with_memory_space_constraint(w_out, pltpu.VMEM)

    def touch(a_ref, b_ref, out):
        out[...] = jnp.zeros_like(out)

    token = pl.pallas_call(
        touch,
        out_shape=jax.ShapeDtypeStruct((8, 128), f32),
        in_specs=[VMEM, VMEM],
        out_specs=VMEM,
        compiler_params=params(1 << 20),
        name="touch",
    )(w_in, w_out)
    return w_in, w_out, token


def relay(
    src_embed, tgt_embed, src_lengths, tgt_lengths, attn_in, attn_out, norm_gain, final_gain
):
    axis = "segment"
    segments = lax.axis_size(axis)
    group = segments // SECTIONS
    index = lax.axis_index(axis)
    section = index // group
    member = index % group
    batches, rows, share = src_embed.shape
    part_width = SECTIONS * share
    chunk_width = part_width // CHUNKS
    w_in = attn_in[0]
    w_out = attn_out[0]
    head_cols = w_out.shape[0]
    gain_q = lax.dynamic_index_in_dim(norm_gain, section, 0, keepdims=True)
    gain_kv = jnp.where(section == 2, final_gain[None], gain_q)

    def permute(value, pairs):
        return lax.ppermute(value, axis, pairs)

    def partners(k):
        return [
            (p * group + q, p * group + (q + k) % group)
            for p in range(SECTIONS)
            for q in range(group)
        ]

    def onward(k):
        return [
            (p * group + q, (p + 1) * group + (q + k) % group)
            for p in range(SECTIONS - 1)
            for q in range(group)
        ]

    def shift_pairs(by):
        return [
            (((0 if first else 2) + by) % SECTIONS * group + q, (0 if first else 2) * group + q)
            for first in (True, False)
            for q in range(group)
        ]

    def collect(low, high):
        source = src_embed[low:high]
        target = tgt_embed[low:high]
        payloads = [jnp.where(section == by, source, target) for by in range(SECTIONS)]
        payloads = lax.optimization_barrier(payloads)
        pieces = {0: payloads[0]}
        for by in range(1, SECTIONS):
            pieces[by] = permute(payloads[by], shift_pairs(by))
        return pieces

    def part_of(pieces, at):
        rotated = [pieces[by][at] for by in range(SECTIONS)]
        ordered = []
        for z in range(SECTIONS):
            value = rotated[z]
            other = rotated[(z - 2) % SECTIONS]
            ordered.append(jnp.where(section == 0, value, other))
        width = chunk_width // share
        return [
            jnp.concatenate(ordered[c * width : (c + 1) * width], -1) for c in range(CHUNKS)
        ]

    periods = batches + SECTIONS - 1
    step = jnp.arange(periods, dtype=jnp.int32)
    slot = step - section
    lengths = jnp.where(section == SECTIONS - 1, tgt_lengths, src_lengths)
    here = slot[:, None] == jnp.arange(batches, dtype=jnp.int32)[None]
    table = jnp.stack(
        [
            jnp.broadcast_to(member, step.shape),
            jnp.any(here, axis=1).astype(jnp.int32),
            jnp.sum(jnp.where(here, lengths[None], 0), axis=1),
            jnp.broadcast_to((section == SECTIONS - 1).astype(jnp.int32), step.shape),
        ],
        axis=1,
    ).astype(jnp.int32)

    early = collect(0, 1)
    late = collect(1, batches)
    w_in, w_out, token = hold_weights(w_in, w_out)
    entry = {}

    def enter(b):
        mine = part_of(early, 0) if b == 0 else part_of(late, b - 1)
        parts = [mine]
        for k in range(1, group):
            parts.append([permute(v, partners(k)) for v in mine])
        entry[b] = parts


    def flat(lists):
        return [v for inner in lists for v in inner]

    def feed(t, came):
        def merge(at, ours, theirs):
            return [
                [jnp.where(section == at, a, c) for a, c in zip(ra, rc)]
                for ra, rc in zip(ours, theirs)
            ]

        xk = came
        if t < batches:
            xk = entry[t] if came is None else merge(0, entry[t], came)
        xq = xk
        if 0 <= t - 2 < batches:
            xq = merge(2, entry[t - 2], xk)
        return t, xk, xq

    def own(fed, after):
        t, xk, xq = fed
        same = xq is xk
        inputs = list(xk[0]) + ([] if same else list(xq[0]))
        return pl.pallas_call(
            functools.partial(own_kernel, group, same, t),
            out_shape=(
                jax.ShapeDtypeStruct((rows, 3 * head_cols), f32),
                jax.ShapeDtypeStruct((rows, 256), f32),
            ),
            in_specs=[SMEM, ANY] + [VMEM] * (len(inputs) + 3),
            out_specs=(VMEM, VMEM),
            compiler_params=params(2 << 20),
            cost_estimate=pl.CostEstimate(
                flops=2 * rows * part_width * 3 * head_cols,
                bytes_accessed=1 << 20,
                transcendentals=0,
            ),
            name="own",
        )(table, after, *inputs, gain_q, gain_kv, w_in)

    n_send = CHUNKS * (group - 1)

    def rest(fed, partial, after):
        t, xk, xq = fed
        same = xq is xk
        inputs = flat(xk[1:]) + ([] if same else flat(xq[1:]))
        outs = pl.pallas_call(
            functools.partial(rest_kernel, group, same, t),
            out_shape=tuple(
                [jax.ShapeDtypeStruct((rows, chunk_width), bf16)] * n_send
                + [jax.ShapeDtypeStruct((rows, head_cols), bf16)]
            ),
            in_specs=[SMEM, ANY] + [VMEM] * (len(inputs) + 6),
            out_specs=tuple([VMEM] * (n_send + 1)),
            scratch_shapes=[pltpu.VMEM((rows, 3 * head_cols), bf16)],
            compiler_params=params(4 << 20),
            cost_estimate=pl.CostEstimate(
                flops=4 * rows * part_width * 3 * head_cols,
                bytes_accessed=1 << 20,
                transcendentals=rows * rows * (head_cols // HEAD),
            ),
            name="rest",
        )(table, after, *inputs, gain_q, gain_kv, w_in, w_out, *partial)
        return outs[:n_send], outs[n_send]

    def tail(fed, mix):
        t, _, xq = fed
        return pl.pallas_call(
            functools.partial(tail_kernel, group, t),
            out_shape=tuple([jax.ShapeDtypeStruct((rows, chunk_width), f32)] * CHUNKS),
            in_specs=[SMEM] + [VMEM] * (2 + CHUNKS),
            out_specs=tuple([VMEM] * CHUNKS),
            compiler_params=params(1 << 20),
            cost_estimate=pl.CostEstimate(
                flops=2 * rows * part_width * head_cols, bytes_accessed=1 << 20, transcendentals=0
            ),
            name="tail",
        )(table, mix, *xq[0], w_out)

    enter(0)
    fed = feed(0, None)
    finals = {}
    exits = {}

    def leave(b):
        value = finals[b]
        pieces = []
        for z in range(SECTIONS):
            at, offset = divmod(z * share, chunk_width)
            piece = value[at][:, offset : offset + share]
            if z < SECTIONS - 1:
                pairs = [((SECTIONS - 1) * group + q, z * group + q) for q in range(group)]
                piece = permute(piece, pairs)
            pieces.append(piece)
        result = pieces[-1]
        for z in range(SECTIONS - 1):
            result = jnp.where(section == z, pieces[z], result)
        exits[b] = result

    for t in range(periods):
        partial = own(fed, token)
        sends, mix = rest(fed, partial, token)
        bases = tail(fed, mix)
        taken = [
            [permute(sends[(k - 1) * CHUNKS + c], partners(k)) for k in range(1, group)]
            for c in range(CHUNKS)
        ]
        if t + 1 < batches:
            enter(t + 1)
        if t - SECTIONS in finals:
            leave(t - SECTIONS)
        came = [[None] * CHUNKS for _ in range(group)]
        done = []
        for c in range(CHUNKS):
            total = bases[c]
            for v in taken[c]:
                total = total + v.astype(f32)
            total = total.astype(bf16)
            done.append(total)
            if t + 1 < periods:
                for k in range(group):
                    came[k][c] = permute(total, onward(k))
        if t >= SECTIONS - 1:
            finals[t - SECTIONS + 1] = done
        if t + 1 < periods:
            fed = feed(t + 1, came)
    leave(batches - 1)
    return jnp.stack([exits[b] for b in range(batches)])


def solution(mesh):
    in_specs = (
        P("dp", None, "segment"),
        P("dp", None, "segment"),
        P("dp"),
        P("dp"),
        P("segment", None, None),
        P("segment", None, None),
        P(),
        P(),
    )
    out_specs = P("dp", None, "segment")
    return jax.shard_map(relay, mesh=mesh, in_specs=in_specs, out_specs=out_specs, check_vma=False)
```

profile of v0, /device:TPU:12, one launch (start us, length us, event | category | flops | bytes accessed | tf_op | source)
XLA Modules:
  0.0 202.5 jit_solution(7848829393578171936)
XLA Ops:
  1.6 6.2 %collective-permute-start.7 = (bf16[1,128,256]{2,1,0:T(8,128)(2,1)S(1)}, bf16[1,128,256]{2,1,0:T(8,128)(2,1)S(1)}, u32[]{:S(2)}, u32[]{:S(2)}) collective-permute-start(bf16[1,128,256]{2,1,0:T(8,128)(2,1)S(1)} %get-tuple-element.47), channel_id=1, source_target_pairs={{8,0},{12,4},{24,16},{28,20},{9,1},{13,5},{25,17},{29,21},{10,2},{... | collective-permute-start | bytes 196616 | tf_op jit(solution)/shard_map/ppermute | solution.py:228
  10.9 4.6 %copy-done = bf16[1,2048,3072]{2,1,0:T(8,128)(2,1)S(1)} copy-done((bf16[1,2048,3072]{2,1,0:T(8,128)(2,1)S(1)}, bf16[1,2048,3072]{2,1,0:T(8,128)(2,1)}, u32[]{:S(2)}) %copy-start) | copy-done | bytes 12582936
  28.3 5.1 %collective-permute-start.1 = (bf16[3,128,256]{2,1,0:T(8,128)(2,1)S(1)}, bf16[3,128,256]{2,1,0:T(8,128)(2,1)S(1)}, u32[]{:S(2)}, u32[]{:S(2)}) collective-permute-start(bf16[3,128,256]{2,1,0:T(8,128)(2,1)S(1)} %get-tuple-element.43), channel_id=1, source_target_pairs={{8,0},{12,4},{24,16},{28,20},{9,1},{13,5},{25,17},{29,21},{10,2},{... | collective-permute-start | bytes 589832 | tf_op jit(solution)/shard_map/ppermute | solution.py:228
  38.8 4.7 %collective-permute-done.1 = bf16[3,128,256]{2,1,0:T(8,128)(2,1)S(1)} collective-permute-done((bf16[3,128,256]{2,1,0:T(8,128)(2,1)S(1)}, bf16[3,128,256]{2,1,0:T(8,128)(2,1)S(1)}, u32[]{:S(2)}, u32[]{:S(2)}) %collective-permute-start.1) | collective-permute-done | bytes 196640 | tf_op jit(solution)/shard_map/ppermute | solution.py:228
  49.1 5.1 %collective-permute-done.11 = bf16[128,1024]{1,0:T(8,128)(2,1)S(1)} collective-permute-done((bf16[128,1024]{1,0:T(8,128)(2,1)S(1)}, bf16[128,1024]{1,0:T(8,128)(2,1)S(1)}, u32[]{:S(2)}, u32[]{:S(2)}) %collective-permute-start.11) | collective-permute-done | bytes 262176 | tf_op jit(solution)/shard_map/ppermute | solution.py:228
  54.1 4.8 %collective-permute-done.5 = bf16[128,1024]{1,0:T(8,128)(2,1)S(1)} collective-permute-done((bf16[128,1024]{1,0:T(8,128)(2,1)S(1)}, bf16[128,1024]{1,0:T(8,128)(2,1)S(1)}, u32[]{:S(2)}, u32[]{:S(2)}) %collective-permute-start.5) | collective-permute-done | bytes 262176 | tf_op jit(solution)/shard_map/ppermute | solution.py:228
  63.5 5.9 %collective-permute-done.13 = bf16[128,1024]{1,0:T(8,128)(2,1)S(1)} collective-permute-done((bf16[128,1024]{1,0:T(8,128)(2,1)S(1)}, bf16[128,1024]{1,0:T(8,128)(2,1)S(1)}, u32[]{:S(2)}, u32[]{:S(2)}) %collective-permute-start.13) | collective-permute-done | bytes 262176 | tf_op jit(solution)/shard_map/ppermute | solution.py:228
  73.4 7.2 %collective-permute-done.15 = bf16[128,1024]{1,0:T(8,128)(2,1)S(1)} collective-permute-done((bf16[128,1024]{1,0:T(8,128)(2,1)S(1)}, bf16[128,1024]{1,0:T(8,128)(2,1)S(1)}, u32[]{:S(2)}, u32[]{:S(2)}) %collective-permute-start.15) | collective-permute-done | bytes 262176 | tf_op jit(solution)/shard_map/ppermute | solution.py:228
  83.3 4.8 %collective-permute-done.4 = bf16[128,1024]{1,0:T(8,128)(2,1)S(1)} collective-permute-done((bf16[128,1024]{1,0:T(8,128)(2,1)S(1)}, bf16[128,1024]{1,0:T(8,128)(2,1)S(1)}, u32[]{:S(2)}, u32[]{:S(2)}) %collective-permute-start.4) | collective-permute-done | bytes 262176 | tf_op jit(solution)/shard_map/ppermute | solution.py:228
  88.2 2.9 %rest.9 = (bf16[128,1024]{1,0:T(8,128)(2,1)S(1)}, bf16[128,1024]{1,0:T(8,128)(2,1)S(1)}) custom-call(s32[7,4]{1,0:T(8,128)S(1)} %add_add_fusion.table, f32[8,128]{1,0:T(8,128)S(1)} %touch.1.after, bf16[128,1024]{1,0:T(8,128)(2,1)S(1)} %get-tuple-element.84.refs_0_, bf16[128,1024]{1,0:T(8,128)(2,1)S(1)} %get-tuple-element.83.refs_1_, ...), custom_call_target="tpu_custom_call" | custom-call | flops 1610612736 | bytes 1048576 | tf_op jit(solution)/shard_map/rest/pallas_call | solution.py:346
  93.4 4.2 %collective-permute-done.16 = bf16[128,1024]{1,0:T(8,128)(2,1)S(1)} collective-permute-done((bf16[128,1024]{1,0:T(8,128)(2,1)S(1)}, bf16[128,1024]{1,0:T(8,128)(2,1)S(1)}, u32[]{:S(2)}, u32[]{:S(2)}) %collective-permute-start.16) | collective-permute-done | bytes 262176 | tf_op jit(solution)/shard_map/ppermute | solution.py:228
  102.9 5.7 %collective-permute-done.18 = bf16[128,1024]{1,0:T(8,128)(2,1)S(1)} collective-permute-done((bf16[128,1024]{1,0:T(8,128)(2,1)S(1)}, bf16[128,1024]{1,0:T(8,128)(2,1)S(1)}, u32[]{:S(2)}, u32[]{:S(2)}) %collective-permute-start.18) | collective-permute-done | bytes 262176 | tf_op jit(solution)/shard_map/ppermute | solution.py:228
  111.6 3.5 %collective-permute-done.3 = bf16[128,1024]{1,0:T(8,128)(2,1)S(1)} collective-permute-done((bf16[128,1024]{1,0:T(8,128)(2,1)S(1)}, bf16[128,1024]{1,0:T(8,128)(2,1)S(1)}, u32[]{:S(2)}, u32[]{:S(2)}) %collective-permute-start.3) | collective-permute-done | bytes 262176 | tf_op jit(solution)/shard_map/ppermute | solution.py:228
  115.2 2.9 %rest.10 = (bf16[128,1024]{1,0:T(8,128)(2,1)S(1)}, bf16[128,1024]{1,0:T(8,128)(2,1)S(1)}) custom-call(s32[7,4]{1,0:T(8,128)S(1)} %add_add_fusion.table, f32[8,128]{1,0:T(8,128)S(1)} %touch.1.after, bf16[128,1024]{1,0:T(8,128)(2,1)S(1)} %get-tuple-element.80.refs_0_, bf16[128,1024]{1,0:T(8,128)(2,1)S(1)} %get-tuple-element.79.refs_1_, ...), custom_call_target="tpu_custom_call" | custom-call | flops 1610612736 | bytes 1048576 | tf_op jit(solution)/shard_map/rest/pallas_call | solution.py:346
  120.6 4.0 %collective-permute-done.19 = bf16[128,1024]{1,0:T(8,128)(2,1)S(1)} collective-permute-done((bf16[128,1024]{1,0:T(8,128)(2,1)S(1)}, bf16[128,1024]{1,0:T(8,128)(2,1)S(1)}, u32[]{:S(2)}, u32[]{:S(2)}) %collective-permute-start.19) | collective-permute-done | bytes 262176 | tf_op jit(solution)/shard_map/ppermute | solution.py:228
  130.3 3.9 %collective-permute-done.24.refs_0_ = bf16[128,1024]{1,0:T(8,128)(2,1)S(1)} collective-permute-done((bf16[128,1024]{1,0:T(8,128)(2,1)S(1)}, bf16[128,1024]{1,0:T(8,128)(2,1)S(1)}, u32[]{:S(2)}, u32[]{:S(2)}) %collective-permute-start.24) | collective-permute-done | bytes 262176 | tf_op jit(solution)/shard_map/ppermute | solution.py:228
  134.3 3.6 %collective-permute-done.23.refs_0_ = bf16[128,1024]{1,0:T(8,128)(2,1)S(1)} collective-permute-done((bf16[128,1024]{1,0:T(8,128)(2,1)S(1)}, bf16[128,1024]{1,0:T(8,128)(2,1)S(1)}, u32[]{:S(2)}, u32[]{:S(2)}) %collective-permute-start.23) | collective-permute-done | bytes 262176 | tf_op jit(solution)/shard_map/ppermute | solution.py:228
  139.6 2.9 %rest.11 = (bf16[128,1024]{1,0:T(8,128)(2,1)S(1)}, bf16[128,1024]{1,0:T(8,128)(2,1)S(1)}) custom-call(s32[7,4]{1,0:T(8,128)S(1)} %add_add_fusion.table, f32[8,128]{1,0:T(8,128)S(1)} %touch.1.after, bf16[128,1024]{1,0:T(8,128)(2,1)S(1)} %collective-permute-done.23.refs_0_, bf16[128,1024]{1,0:T(8,128)(2,1)S(1)} %broadcast_select_fusion.3.refs_1_, ...), custom_call_target="tpu_custom_call" | custom-call | flops 1610612736 | bytes 1048576 | tf_op jit(solution)/shard_map/rest/pallas_call | solution.py:346
  144.2 4.7 %collective-permute-done.25 = bf16[128,1024]{1,0:T(8,128)(2,1)S(1)} collective-permute-done((bf16[128,1024]{1,0:T(8,128)(2,1)S(1)}, bf16[128,1024]{1,0:T(8,128)(2,1)S(1)}, u32[]{:S(2)}, u32[]{:S(2)}) %collective-permute-start.25) | collective-permute-done | bytes 262176 | tf_op jit(solution)/shard_map/ppermute | solution.py:228
  151.4 3.1 %collective-permute-start.29 = (bf16[128,1024]{1,0:T(8,128)(2,1)S(1)}, bf16[128,1024]{1,0:T(8,128)(2,1)S(1)}, u32[]{:S(2)}, u32[]{:S(2)}) collective-permute-start(bf16[128,1024]{1,0:T(8,128)(2,1)S(1)} %add_convert_fusion.2), channel_id=1, source_target_pairs={{0,12},{4,8},{8,20},{12,16},{16,28},{20,24},{1,13},{5,9},{9,21},{1... | collective-permute-start | bytes 786440 | tf_op jit(solution)/shard_map/ppermute | solution.py:228
  157.3 3.3 %collective-permute-done.29.refs_0_ = bf16[128,1024]{1,0:T(8,128)(2,1)S(1)} collective-permute-done((bf16[128,1024]{1,0:T(8,128)(2,1)S(1)}, bf16[128,1024]{1,0:T(8,128)(2,1)S(1)}, u32[]{:S(2)}, u32[]{:S(2)}) %collective-permute-start.29) | collective-permute-done | bytes 262176 | tf_op jit(solution)/shard_map/ppermute | solution.py:228
  168.4 5.9 %collective-permute-start.36 = (bf16[128,1024]{1,0:T(8,128)(2,1)S(1)}, bf16[128,1024]{1,0:T(8,128)(2,1)S(1)}, u32[]{:S(2)}, u32[]{:S(2)}) collective-permute-start(bf16[128,1024]{1,0:T(8,128)(2,1)S(1)} %add_convert_fusion.1), channel_id=1, source_target_pairs={{0,8},{4,12},{8,16},{12,20},{16,24},{20,28},{1,9},{5,13},{9,17},{1... | collective-permute-start | bytes 786440 | tf_op jit(solution)/shard_map/ppermute | solution.py:228
  174.4 3.4 %collective-permute-start.35 = (bf16[128,1024]{1,0:T(8,128)(2,1)S(1)}, bf16[128,1024]{1,0:T(8,128)(2,1)S(1)}, u32[]{:S(2)}, u32[]{:S(2)}) collective-permute-start(bf16[128,1024]{1,0:T(8,128)(2,1)S(1)} %add_convert_fusion.1), channel_id=1, source_target_pairs={{0,12},{4,8},{8,20},{12,16},{16,28},{20,24},{1,13},{5,9},{9,21},{1... | collective-permute-start | bytes 786440 | tf_op jit(solution)/shard_map/ppermute | solution.py:228
  196.2 5.5 %collective-permute-done.39 = bf16[128,256]{1,0:T(8,128)(2,1)S(1)} collective-permute-done((bf16[128,256]{1,0:T(8,128)(2,1)S(1)}, bf16[128,256]{1,0:T(8,128)(2,1)S(1)}, u32[]{:S(2)}, u32[]{:S(2)}) %collective-permute-start.39) | collective-permute-done | bytes 65568 | tf_op jit(solution)/shard_map/ppermute | solution.py:228
  (136 shorter events, 93.8 us)
Async XLA Ops:
  0.9 16.8 %collective-permute-start.6 = (bf16[1,128,256]{2,1,0:T(8,128)(2,1)S(1)}, bf16[1,128,256]{2,1,0:T(8,128)(2,1)S(1)}, u32[]{:S(2)}, u32[]{:S(2)}) collective-permute-start(bf16[1,128,256]{2,1,0:T(8,128)(2,1)S(1)} %get-tuple-element.46), channel_id=1, source_target_pairs={{16,0},{20,4},{0,16},{4,20},{17,1},{21,5},{1,17},{5,21},{18,2},{22... | collective-permute-start | bytes 196616 | tf_op jit(solution)/shard_map/ppermute | solution.py:228
  1.6 16.2 %collective-permute-start.7 = (bf16[1,128,256]{2,1,0:T(8,128)(2,1)S(1)}, bf16[1,128,256]{2,1,0:T(8,128)(2,1)S(1)}, u32[]{:S(2)}, u32[]{:S(2)}) collective-permute-start(bf16[1,128,256]{2,1,0:T(8,128)(2,1)S(1)} %get-tuple-element.47), channel_id=1, source_target_pairs={{8,0},{12,4},{24,16},{28,20},{9,1},{13,5},{25,17},{29,21},{10,2},{... | collective-permute-start | bytes 196616 | tf_op jit(solution)/shard_map/ppermute | solution.py:228
  7.8 10.0 %collective-permute-start.8 = (bf16[1,128,256]{2,1,0:T(8,128)(2,1)S(1)}, bf16[1,128,256]{2,1,0:T(8,128)(2,1)S(1)}, u32[]{:S(2)}, u32[]{:S(2)}) collective-permute-start(bf16[1,128,256]{2,1,0:T(8,128)(2,1)S(1)} %get-tuple-element.48), channel_id=1, source_target_pairs={{24,0},{28,4},{8,16},{12,20},{25,1},{29,5},{9,17},{13,21},{26,2},{... | collective-permute-start | bytes 196616 | tf_op jit(solution)/shard_map/ppermute | solution.py:228
  26.0 10.8 %collective-permute-start.10 = (bf16[128,1024]{1,0:T(8,128)(2,1)S(1)}, bf16[128,1024]{1,0:T(8,128)(2,1)S(1)}, u32[]{:S(2)}, u32[]{:S(2)}) collective-permute-start(bf16[128,1024]{1,0:T(8,128)(2,1)S(1)} %get-tuple-element.52), channel_id=1, source_target_pairs={{0,4},{4,0},{8,12},{12,8},{16,20},{20,16},{24,28},{28,24},{1,5},{5... | collective-permute-start | bytes 786440 | tf_op jit(solution)/shard_map/ppermute | solution.py:228
  27.6 11.2 %collective-permute-start = (bf16[3,128,256]{2,1,0:T(8,128)(2,1)S(1)}, bf16[3,128,256]{2,1,0:T(8,128)(2,1)S(1)}, u32[]{:S(2)}, u32[]{:S(2)}) collective-permute-start(bf16[3,128,256]{2,1,0:T(8,128)(2,1)S(1)} %get-tuple-element.42), channel_id=1, source_target_pairs={{16,0},{20,4},{0,16},{4,20},{17,1},{21,5},{1,17},{5,21},{18,2},{22... | collective-permute-start | bytes 589832 | tf_op jit(solution)/shard_map/ppermute | solution.py:228
  28.3 15.2 %collective-permute-start.1 = (bf16[3,128,256]{2,1,0:T(8,128)(2,1)S(1)}, bf16[3,128,256]{2,1,0:T(8,128)(2,1)S(1)}, u32[]{:S(2)}, u32[]{:S(2)}) collective-permute-start(bf16[3,128,256]{2,1,0:T(8,128)(2,1)S(1)} %get-tuple-element.43), channel_id=1, source_target_pairs={{8,0},{12,4},{24,16},{28,20},{9,1},{13,5},{25,17},{29,21},{10,2},{... | collective-permute-start | bytes 589832 | tf_op jit(solution)/shard_map/ppermute | solution.py:228
  33.4 10.1 %collective-permute-start.2 = (bf16[3,128,256]{2,1,0:T(8,128)(2,1)S(1)}, bf16[3,128,256]{2,1,0:T(8,128)(2,1)S(1)}, u32[]{:S(2)}, u32[]{:S(2)}) collective-permute-start(bf16[3,128,256]{2,1,0:T(8,128)(2,1)S(1)} %get-tuple-element.44), channel_id=1, source_target_pairs={{24,0},{28,4},{8,16},{12,20},{25,1},{29,5},{9,17},{13,21},{26,2},{... | collective-permute-start | bytes 589832 | tf_op jit(solution)/shard_map/ppermute | solution.py:228
  36.8 9.0 %collective-permute-start.12 = (bf16[128,1024]{1,0:T(8,128)(2,1)S(1)}, bf16[128,1024]{1,0:T(8,128)(2,1)S(1)}, u32[]{:S(2)}, u32[]{:S(2)}) collective-permute-start(bf16[128,1024]{1,0:T(8,128)(2,1)S(1)} %add_convert_fusion.6), channel_id=1, source_target_pairs={{0,8},{4,12},{8,16},{12,20},{16,24},{20,28},{1,9},{5,13},{9,17},{1... | collective-permute-start | bytes 786440 | tf_op jit(solution)/shard_map/ppermute | solution.py:228
  43.5 10.6 %collective-permute-start.11 = (bf16[128,1024]{1,0:T(8,128)(2,1)S(1)}, bf16[128,1024]{1,0:T(8,128)(2,1)S(1)}, u32[]{:S(2)}, u32[]{:S(2)}) collective-permute-start(bf16[128,1024]{1,0:T(8,128)(2,1)S(1)} %add_convert_fusion.6), channel_id=1, source_target_pairs={{0,12},{4,8},{8,20},{12,16},{16,28},{20,24},{1,13},{5,9},{9,21},{1... | collective-permute-start | bytes 786440 | tf_op jit(solution)/shard_map/ppermute | solution.py:228
  45.9 13.1 %collective-permute-start.5 = (bf16[128,1024]{1,0:T(8,128)(2,1)S(1)}, bf16[128,1024]{1,0:T(8,128)(2,1)S(1)}, u32[]{:S(2)}, u32[]{:S(2)}) collective-permute-start(bf16[128,1024]{1,0:T(8,128)(2,1)S(1)} %get-tuple-element.122), channel_id=1, source_target_pairs={{0,4},{4,0},{8,12},{12,8},{16,20},{20,16},{24,28},{28,24},{1,5},{5... | collective-permute-start | bytes 786440 | tf_op jit(solution)/shard_map/ppermute | solution.py:228
  69.5 11.1 %collective-permute-start.15 = (bf16[128,1024]{1,0:T(8,128)(2,1)S(1)}, bf16[128,1024]{1,0:T(8,128)(2,1)S(1)}, u32[]{:S(2)}, u32[]{:S(2)}) collective-permute-start(bf16[128,1024]{1,0:T(8,128)(2,1)S(1)} %add_convert_fusion.5), channel_id=1, source_target_pairs={{0,8},{4,12},{8,16},{12,20},{16,24},{20,28},{1,9},{5,13},{9,17},{1... | collective-permute-start | bytes 786440 | tf_op jit(solution)/shard_map/ppermute | solution.py:228
  71.4 11.8 %collective-permute-start.14 = (bf16[128,1024]{1,0:T(8,128)(2,1)S(1)}, bf16[128,1024]{1,0:T(8,128)(2,1)S(1)}, u32[]{:S(2)}, u32[]{:S(2)}) collective-permute-start(bf16[128,1024]{1,0:T(8,128)(2,1)S(1)} %add_convert_fusion.5), channel_id=1, source_target_pairs={{0,12},{4,8},{8,20},{12,16},{16,28},{20,24},{1,13},{5,9},{9,21},{1... | collective-permute-start | bytes 786440 | tf_op jit(solution)/shard_map/ppermute | solution.py:228
  97.7 10.9 %collective-permute-start.18 = (bf16[128,1024]{1,0:T(8,128)(2,1)S(1)}, bf16[128,1024]{1,0:T(8,128)(2,1)S(1)}, u32[]{:S(2)}, u32[]{:S(2)}) collective-permute-start(bf16[128,1024]{1,0:T(8,128)(2,1)S(1)} %add_convert_fusion.4), channel_id=1, source_target_pairs={{0,8},{4,12},{8,16},{12,20},{16,24},{20,28},{1,9},{5,13},{9,17},{1... | collective-permute-start | bytes 786440 | tf_op jit(solution)/shard_map/ppermute | solution.py:228
  100.3 11.4 %collective-permute-start.17 = (bf16[128,1024]{1,0:T(8,128)(2,1)S(1)}, bf16[128,1024]{1,0:T(8,128)(2,1)S(1)}, u32[]{:S(2)}, u32[]{:S(2)}) collective-permute-start(bf16[128,1024]{1,0:T(8,128)(2,1)S(1)} %add_convert_fusion.4), channel_id=1, source_target_pairs={{0,12},{4,8},{8,20},{12,16},{16,28},{20,24},{1,13},{5,9},{9,21},{1... | collective-permute-start | bytes 786440 | tf_op jit(solution)/shard_map/ppermute | solution.py:228
  124.7 9.5 %collective-permute-start.24 = (bf16[128,1024]{1,0:T(8,128)(2,1)S(1)}, bf16[128,1024]{1,0:T(8,128)(2,1)S(1)}, u32[]{:S(2)}, u32[]{:S(2)}) collective-permute-start(bf16[128,1024]{1,0:T(8,128)(2,1)S(1)} %add_convert_fusion.3), channel_id=1, source_target_pairs={{0,8},{4,12},{8,16},{12,20},{16,24},{20,28},{1,9},{5,13},{9,17},{1... | collective-permute-start | bytes 786440 | tf_op jit(solution)/shard_map/ppermute | solution.py:228
  127.5 10.4 %collective-permute-start.23 = (bf16[128,1024]{1,0:T(8,128)(2,1)S(1)}, bf16[128,1024]{1,0:T(8,128)(2,1)S(1)}, u32[]{:S(2)}, u32[]{:S(2)}) collective-permute-start(bf16[128,1024]{1,0:T(8,128)(2,1)S(1)} %add_convert_fusion.3), channel_id=1, source_target_pairs={{0,12},{4,8},{8,20},{12,16},{16,28},{20,24},{1,13},{5,9},{9,21},{1... | collective-permute-start | bytes 786440 | tf_op jit(solution)/shard_map/ppermute | solution.py:228
  151.4 9.3 %collective-permute-start.29 = (bf16[128,1024]{1,0:T(8,128)(2,1)S(1)}, bf16[128,1024]{1,0:T(8,128)(2,1)S(1)}, u32[]{:S(2)}, u32[]{:S(2)}) collective-permute-start(bf16[128,1024]{1,0:T(8,128)(2,1)S(1)} %add_convert_fusion.2), channel_id=1, source_target_pairs={{0,12},{4,8},{8,20},{12,16},{16,28},{20,24},{1,13},{5,9},{9,21},{1... | collective-permute-start | bytes 786440 | tf_op jit(solution)/shard_map/ppermute | solution.py:228
  163.2 11.2 %collective-permute-start.22 = (bf16[128,256]{1,0:T(8,128)(2,1)S(1)}, bf16[128,256]{1,0:T(8,128)(2,1)S(1)}, u32[]{:S(2)}, u32[]{:S(2)}) collective-permute-start(bf16[128,256]{1,0:T(8,128)(2,1)S(1)} %get-tuple-element.107), channel_id=1, source_target_pairs={{24,0},{28,4},{25,1},{29,5},{26,2},{30,6},{27,3},{31,7}} | collective-permute-start | bytes 196616 | tf_op jit(solution)/shard_map/ppermute | solution.py:228
  163.8 10.5 %collective-permute-start.21 = (bf16[128,256]{1,0:T(8,128)(2,1)S(1)}, bf16[128,256]{1,0:T(8,128)(2,1)S(1)}, u32[]{:S(2)}, u32[]{:S(2)}) collective-permute-start(bf16[128,256]{1,0:T(8,128)(2,1)S(1)} %get-tuple-element.108), channel_id=1, source_target_pairs={{24,8},{28,12},{25,9},{29,13},{26,10},{30,14},{27,11},{31,15}} | collective-permute-start | bytes 196616 | tf_op jit(solution)/shard_map/ppermute | solution.py:228
  165.1 9.3 %collective-permute-start.20 = (bf16[128,256]{1,0:T(8,128)(2,1)S(1)}, bf16[128,256]{1,0:T(8,128)(2,1)S(1)}, u32[]{:S(2)}, u32[]{:S(2)}) collective-permute-start(bf16[128,256]{1,0:T(8,128)(2,1)S(1)} %get-tuple-element.109), channel_id=1, source_target_pairs={{24,16},{28,20},{25,17},{29,21},{26,18},{30,22},{27,19},{31,23}} | collective-permute-start | bytes 196616 | tf_op jit(solution)/shard_map/ppermute | solution.py:228
  168.4 12.1 %collective-permute-start.36 = (bf16[128,1024]{1,0:T(8,128)(2,1)S(1)}, bf16[128,1024]{1,0:T(8,128)(2,1)S(1)}, u32[]{:S(2)}, u32[]{:S(2)}) collective-permute-start(bf16[128,1024]{1,0:T(8,128)(2,1)S(1)} %add_convert_fusion.1), channel_id=1, source_target_pairs={{0,8},{4,12},{8,16},{12,20},{16,24},{20,28},{1,9},{5,13},{9,17},{1... | collective-permute-start | bytes 786440 | tf_op jit(solution)/shard_map/ppermute | solution.py:228
  174.4 9.2 %collective-permute-start.35 = (bf16[128,1024]{1,0:T(8,128)(2,1)S(1)}, bf16[128,1024]{1,0:T(8,128)(2,1)S(1)}, u32[]{:S(2)}, u32[]{:S(2)}) collective-permute-start(bf16[128,1024]{1,0:T(8,128)(2,1)S(1)} %add_convert_fusion.1), channel_id=1, source_target_pairs={{0,12},{4,8},{8,20},{12,16},{16,28},{20,24},{1,13},{5,9},{9,21},{1... | collective-permute-start | bytes 786440 | tf_op jit(solution)/shard_map/ppermute | solution.py:228
  178.5 8.9 %collective-permute-start.27 = (bf16[128,256]{1,0:T(8,128)(2,1)S(1)}, bf16[128,256]{1,0:T(8,128)(2,1)S(1)}, u32[]{:S(2)}, u32[]{:S(2)}) collective-permute-start(bf16[128,256]{1,0:T(8,128)(2,1)S(1)} %get-tuple-element.111), channel_id=1, source_target_pairs={{24,8},{28,12},{25,9},{29,13},{26,10},{30,14},{27,11},{31,15}} | collective-permute-start | bytes 196616 | tf_op jit(solution)/shard_map/ppermute | solution.py:228
  191.5 10.2 %collective-permute-start.39 = (bf16[128,256]{1,0:T(8,128)(2,1)S(1)}, bf16[128,256]{1,0:T(8,128)(2,1)S(1)}, u32[]{:S(2)}, u32[]{:S(2)}) collective-permute-start(bf16[128,256]{1,0:T(8,128)(2,1)S(1)} %get-tuple-element.117), channel_id=1, source_target_pairs={{24,8},{28,12},{25,9},{29,13},{26,10},{30,14},{27,11},{31,15}} | collective-permute-start | bytes 196616 | tf_op jit(solution)/shard_map/ppermute | solution.py:228
  (23 other events, 137.9 us)
where the time goes:
time: 204 us; the launch traced here: 202 us
  waiting for transfers between devices  86.7 us (42%)
  starting transfers between devices  72.3 us (35%)
  Pallas kernels  28.1 us (14%)
  local copies, waits for them, and re-layouts  9.95 us (5%)
  other arithmetic  4.64 us (2%)
    ppermute x41, waiting for transfers between devices, permute(): return lax.ppermute(value, axis, pairs)  86.7 us
    ppermute x41, starting transfers between devices, permute(): return lax.ppermute(value, axis, pairs)  72.3 us
    pallas_call x7, Pallas kernels, rest(): pl.pallas_call(functools.partial(rest_kernel, group, same, t), out_shape=...  13.4 us
    unnamed x12, local copies, waits for them, and re-layouts  9.62 us
    pallas_call x7, Pallas kernels, own(): pl.pallas_call(functools.partial(own_kernel, group, same, t), out_shape=(...  8.42 us
    pallas_call x7, Pallas kernels, tail(): pl.pallas_call(functools.partial(tail_kernel, group, t), out_shape=tuple(...  6.31 us
  transfers between devices with their start and end apart: 41, of which 23 were waited for; matrix products, arithmetic and copies ran while one was open for 1% of the time, Pallas kernels for 6%

commit v1 on v0

--- a/solution.py
+++ b/solution.py
@@ -212,17 +212,21 @@
     axis = "segment"
     segments = lax.axis_size(axis)
     group = segments // SECTIONS
-    index = lax.axis_index(axis)
-    section = index // group
-    member = index % group
+    index = lax.axis_index(axis).astype(jnp.uint32)
+    section = lax.div(index, jnp.uint32(group)).astype(jnp.int32)
+    member = lax.rem(index, jnp.uint32(group)).astype(jnp.int32)
+    at_section = [section == p for p in range(SECTIONS)]
+    section, member, at_section = lax.optimization_barrier((section, member, at_section))
     batches, rows, share = src_embed.shape
     part_width = SECTIONS * share
     chunk_width = part_width // CHUNKS
     w_in = attn_in[0]
     w_out = attn_out[0]
     head_cols = w_out.shape[0]
-    gain_q = lax.dynamic_index_in_dim(norm_gain, section, 0, keepdims=True)
-    gain_kv = jnp.where(section == 2, final_gain[None], gain_q)
+    gain_q = norm_gain[:1]
+    for p in range(1, SECTIONS):
+        gain_q = jnp.where(at_section[p], norm_gain[p : p + 1], gain_q)
+    gain_kv = jnp.where(at_section[2], final_gain[None], gain_q)
 
     def permute(value, pairs):
         return lax.ppermute(value, axis, pairs)
@@ -251,7 +255,7 @@
     def collect(low, high):
         source = src_embed[low:high]
         target = tgt_embed[low:high]
-        payloads = [jnp.where(section == by, source, target) for by in range(SECTIONS)]
+        payloads = [jnp.where(at_section[by], source, target) for by in range(SECTIONS)]
         payloads = lax.optimization_barrier(payloads)
         pieces = {0: payloads[0]}
         for by in range(1, SECTIONS):
@@ -264,7 +268,7 @@
         for z in range(SECTIONS):
             value = rotated[z]
             other = rotated[(z - 2) % SECTIONS]
-            ordered.append(jnp.where(section == 0, value, other))
+            ordered.append(jnp.where(at_section[0], value, other))
         width = chunk_width // share
         return [
             jnp.concatenate(ordered[c * width : (c + 1) * width], -1) for c in range(CHUNKS)
@@ -273,25 +277,27 @@
     periods = batches + SECTIONS - 1
     step = jnp.arange(periods, dtype=jnp.int32)
     slot = step - section
-    lengths = jnp.where(section == SECTIONS - 1, tgt_lengths, src_lengths)
+    lengths = jnp.where(at_section[SECTIONS - 1], tgt_lengths, src_lengths)
     here = slot[:, None] == jnp.arange(batches, dtype=jnp.int32)[None]
     table = jnp.stack(
         [
             jnp.broadcast_to(member, step.shape),
             jnp.any(here, axis=1).astype(jnp.int32),
             jnp.sum(jnp.where(here, lengths[None], 0), axis=1),
-            jnp.broadcast_to((section == SECTIONS - 1).astype(jnp.int32), step.shape),
+            jnp.where(at_section[SECTIONS - 1], jnp.ones_like(step), 0),
         ],
         axis=1,
     ).astype(jnp.int32)
+    table = pltpu.with_memory_space_constraint(table, pltpu.SMEM)
 
     early = collect(0, 1)
-    late = collect(1, batches)
+    late = [collect(1, batches)]
     w_in, w_out, token = hold_weights(w_in, w_out)
     entry = {}
 
     def enter(b):
-        mine = part_of(early, 0) if b == 0 else part_of(late, b - 1)
+        mine = part_of(early, 0) if b == 0 else part_of(late[0], b - 1)
+        mine = lax.optimization_barrier(mine)
         parts = [mine]
         for k in range(1, group):
             parts.append([permute(v, partners(k)) for v in mine])
@@ -301,20 +307,34 @@
     def flat(lists):
         return [v for inner in lists for v in inner]
 
+    def gated(values, gate):
+        return lax.optimization_barrier((values, gate))[0]
+
+    def merge(at, ours, theirs):
+        return [
+            [jnp.where(at_section[at], a, c) for a, c in zip(ra, rc)]
+            for ra, rc in zip(ours, theirs)
+        ]
+
     def feed(t, came):
-        def merge(at, ours, theirs):
-            return [
-                [jnp.where(section == at, a, c) for a, c in zip(ra, rc)]
-                for ra, rc in zip(ours, theirs)
-            ]
-
-        xk = came
-        if t < batches:
-            xk = entry[t] if came is None else merge(0, entry[t], came)
-        xq = xk
-        if 0 <= t - 2 < batches:
-            xq = merge(2, entry[t - 2], xk)
-        return t, xk, xq
+        def select(rows):
+            xk = None if came is None else came[rows]
+            if t < batches:
+                mine = entry[t][rows]
+                xk = mine if xk is None else merge(0, mine, xk)
+            xq = xk
+            if 0 <= t - 2 < batches:
+                xq = merge(2, entry[t - 2][rows], xk)
+            return xk, xq
+
+        xk, xq = select(slice(0, 1))
+        partial = own((t, xk, xq), token)
+        if came is not None:
+            came = came[:1] + gated(came[1:], partial[1])
+        more_k, more_q = select(slice(1, None))
+        same = xq is xk
+        xk = xk + more_k
+        return (t, xk, xk if same else xq + more_q), partial
 
     def own(fed, after):
         t, xk, xq = fed
@@ -377,7 +397,7 @@
         )(table, mix, *xq[0], w_out)
 
     enter(0)
-    fed = feed(0, None)
+    fed, partial = feed(0, None)
     finals = {}
     exits = {}
 
@@ -393,18 +413,17 @@
             pieces.append(piece)
         result = pieces[-1]
         for z in range(SECTIONS - 1):
-            result = jnp.where(section == z, pieces[z], result)
+            result = jnp.where(at_section[z], pieces[z], result)
         exits[b] = result
 
     for t in range(periods):
-        partial = own(fed, token)
         sends, mix = rest(fed, partial, token)
         bases = tail(fed, mix)
         taken = [
             [permute(sends[(k - 1) * CHUNKS + c], partners(k)) for k in range(1, group)]
             for c in range(CHUNKS)
         ]
-        if t + 1 < batches:
+        if 0 < t < batches - 1:
             enter(t + 1)
         if t - SECTIONS in finals:
             leave(t - SECTIONS)
@@ -419,10 +438,13 @@
             if t + 1 < periods:
                 for k in range(group):
                     came[k][c] = permute(total, onward(k))
+        if t == 0:
+            late[0] = gated(late[0], done)
+            enter(1)
         if t >= SECTIONS - 1:
             finals[t - SECTIONS + 1] = done
         if t + 1 < periods:
-            fed = feed(t + 1, came)
+            fed, partial = feed(t + 1, came)
     leave(batches - 1)
     return jnp.stack([exits[b] for b in range(batches)])
 

time: 204 us -> 186 us (0.912)
  the two profiles are of different devices: /device:TPU:12 before, /device:TPU:0 now
where the time goes in v1:
time: 186 us
  starting transfers between devices  84 us (45%)
  waiting for transfers between devices  58.2 us (31%)
  Pallas kernels  28.1 us (15%)
  local copies, waits for them, and re-layouts  9.94 us (5%)
  other arithmetic  4.57 us (2%)
    ppermute x41, starting transfers between devices, permute(): return lax.ppermute(value, axis, pairs)  84 us
    ppermute x41, waiting for transfers between devices, permute(): return lax.ppermute(value, axis, pairs)  58.2 us
    pallas_call x7, Pallas kernels, rest(): pl.pallas_call(functools.partial(rest_kernel, group, same, t), out_shape=...  13.3 us
    unnamed x12, local copies, waits for them, and re-layouts  9.62 us
    pallas_call x7, Pallas kernels, own(): pl.pallas_call(functools.partial(own_kernel, group, same, t), out_shape=(...  8.42 us
    pallas_call x7, Pallas kernels, tail(): pl.pallas_call(functools.partial(tail_kernel, group, t), out_shape=tuple(...  6.31 us
  transfers between devices with their start and end apart: 41, of which 23 were waited for; matrix products, arithmetic and copies ran while one was open for 1% of the time, Pallas kernels for 8%

profile of v1, /device:TPU:0, one launch (start us, length us, event | category | flops | bytes accessed | tf_op | source)
XLA Modules:
  0.0 185.5 jit_solution(15095252034091304330)
XLA Ops:
  0.9 6.0 %collective-permute-start.3 = (bf16[1,128,256]{2,1,0:T(8,128)(2,1)S(1)}, bf16[1,128,256]{2,1,0:T(8,128)(2,1)S(1)}, u32[]{:S(2)}, u32[]{:S(2)}) collective-permute-start(bf16[1,128,256]{2,1,0:T(8,128)(2,1)S(1)} %get-tuple-element.68), channel_id=1, source_target_pairs={{16,0},{20,4},{0,16},{4,20},{17,1},{21,5},{1,17},{5,21},{18,2},{22... | collective-permute-start | bytes 196616 | tf_op jit(solution)/shard_map/ppermute | solution.py:232
  11.5 4.6 %copy-done = bf16[1,2048,3072]{2,1,0:T(8,128)(2,1)S(1)} copy-done((bf16[1,2048,3072]{2,1,0:T(8,128)(2,1)S(1)}, bf16[1,2048,3072]{2,1,0:T(8,128)(2,1)}, u32[]{:S(2)}) %copy-start) | copy-done | bytes 12582936
  20.0 2.8 %copy-done.1 = bf16[1,2048,3072]{2,1,0:T(8,128)(2,1)S(1)} copy-done((bf16[1,2048,3072]{2,1,0:T(8,128)(2,1)S(1)}, bf16[1,2048,3072]{2,1,0:T(8,128)(2,1)}, u32[]{:S(2)}) %copy-start.1) | copy-done | bytes 12582936
  26.2 2.9 %rest.7 = (bf16[128,1024]{1,0:T(8,128)(2,1)S(1)}, bf16[128,1024]{1,0:T(8,128)(2,1)S(1)}) custom-call(s32[7,4]{1,0:T(8,128)S(1)} %add_add_fusion.table, f32[8,128]{1,0:T(8,128)S(1)} %touch.1.after, bf16[128,1024]{1,0:T(8,128)(2,1)S(1)} %collective-permute-done.6.refs_0_, f32[1,2048]{1,0:T(1,128)S(1)} %get-tuple-element.118.refs_1_.refs_2_, ...), custom_call_target="tpu_custom_call" | custom-call | flops 1610612736 | bytes 1048576 | tf_op jit(solution)/shard_map/rest/pallas_call | solution.py:366
  36.4 5.6 %collective-permute-start.12 = (bf16[128,1024]{1,0:T(8,128)(2,1)S(1)}, bf16[128,1024]{1,0:T(8,128)(2,1)S(1)}, u32[]{:S(2)}, u32[]{:S(2)}) collective-permute-start(bf16[128,1024]{1,0:T(8,128)(2,1)S(1)} %add_convert_fusion.6), channel_id=1, source_target_pairs={{0,8},{4,12},{8,16},{12,20},{16,24},{20,28},{1,9},{5,13},{9,17},{1... | collective-permute-start | bytes 786440 | tf_op jit(solution)/shard_map/ppermute | solution.py:232
  52.9 2.9 %rest.8 = (bf16[128,1024]{1,0:T(8,128)(2,1)S(1)}, bf16[128,1024]{1,0:T(8,128)(2,1)S(1)}) custom-call(s32[7,4]{1,0:T(8,128)S(1)} %add_add_fusion.table, f32[8,128]{1,0:T(8,128)S(1)} %touch.1.after, bf16[128,1024]{1,0:T(8,128)(2,1)S(1)} %broadcast_select_fusion.12.refs_0_, f32[1,2048]{1,0:T(1,128)S(1)} %get-tuple-element.118.refs_1_.refs_2_, ...), custom_call_target="tpu_custom_call" | custom-call | flops 1610612736 | bytes 1048576 | tf_op jit(solution)/shard_map/rest/pallas_call | solution.py:366
  57.4 4.8 %collective-permute-done.13 = bf16[128,1024]{1,0:T(8,128)(2,1)S(1)} collective-permute-done((bf16[128,1024]{1,0:T(8,128)(2,1)S(1)}, bf16[128,1024]{1,0:T(8,128)(2,1)S(1)}, u32[]{:S(2)}, u32[]{:S(2)}) %collective-permute-start.13) | collective-permute-done | bytes 262176 | tf_op jit(solution)/shard_map/ppermute | solution.py:232
  62.3 5.6 %collective-permute-start.15 = (bf16[128,1024]{1,0:T(8,128)(2,1)S(1)}, bf16[128,1024]{1,0:T(8,128)(2,1)S(1)}, u32[]{:S(2)}, u32[]{:S(2)}) collective-permute-start(bf16[128,1024]{1,0:T(8,128)(2,1)S(1)} %add_convert_fusion.5), channel_id=1, source_target_pairs={{0,8},{4,12},{8,16},{12,20},{16,24},{20,28},{1,9},{5,13},{9,17},{1... | collective-permute-start | bytes 786440 | tf_op jit(solution)/shard_map/ppermute | solution.py:232
  71.4 3.0 %collective-permute-done.15 = bf16[128,1024]{1,0:T(8,128)(2,1)S(1)} collective-permute-done((bf16[128,1024]{1,0:T(8,128)(2,1)S(1)}, bf16[128,1024]{1,0:T(8,128)(2,1)S(1)}, u32[]{:S(2)}, u32[]{:S(2)}) %collective-permute-start.15) | collective-permute-done | bytes 262176 | tf_op jit(solution)/shard_map/ppermute | solution.py:232
  77.2 2.9 %rest.9 = (bf16[128,1024]{1,0:T(8,128)(2,1)S(1)}, bf16[128,1024]{1,0:T(8,128)(2,1)S(1)}) custom-call(s32[7,4]{1,0:T(8,128)S(1)} %add_add_fusion.table, f32[8,128]{1,0:T(8,128)S(1)} %touch.1.after, bf16[128,1024]{1,0:T(8,128)(2,1)S(1)} %get-tuple-element.114.refs_0_, bf16[128,1024]{1,0:T(8,128)(2,1)S(1)} %get-tuple-element.113.refs_1_, ...), custom_call_target="tpu_custom_call" | custom-call | flops 1610612736 | bytes 1048576 | tf_op jit(solution)/shard_map/rest/pallas_call | solution.py:366
  83.1 3.4 %collective-permute-done.16 = bf16[128,1024]{1,0:T(8,128)(2,1)S(1)} collective-permute-done((bf16[128,1024]{1,0:T(8,128)(2,1)S(1)}, bf16[128,1024]{1,0:T(8,128)(2,1)S(1)}, u32[]{:S(2)}, u32[]{:S(2)}) %collective-permute-start.16) | collective-permute-done | bytes 262176 | tf_op jit(solution)/shard_map/ppermute | solution.py:232
  86.6 5.5 %collective-permute-start.18 = (bf16[128,1024]{1,0:T(8,128)(2,1)S(1)}, bf16[128,1024]{1,0:T(8,128)(2,1)S(1)}, u32[]{:S(2)}, u32[]{:S(2)}) collective-permute-start(bf16[128,1024]{1,0:T(8,128)(2,1)S(1)} %add_convert_fusion.4), channel_id=1, source_target_pairs={{0,8},{4,12},{8,16},{12,20},{16,24},{20,28},{1,9},{5,13},{9,17},{1... | collective-permute-start | bytes 786440 | tf_op jit(solution)/shard_map/ppermute | solution.py:232
  92.7 2.9 %collective-permute-start.17 = (bf16[128,1024]{1,0:T(8,128)(2,1)S(1)}, bf16[128,1024]{1,0:T(8,128)(2,1)S(1)}, u32[]{:S(2)}, u32[]{:S(2)}) collective-permute-start(bf16[128,1024]{1,0:T(8,128)(2,1)S(1)} %add_convert_fusion.4), channel_id=1, source_target_pairs={{0,12},{4,8},{8,20},{12,16},{16,28},{20,24},{1,13},{5,9},{9,21},{1... | collective-permute-start | bytes 786440 | tf_op jit(solution)/shard_map/ppermute | solution.py:232
  99.6 2.9 %rest.10 = (bf16[128,1024]{1,0:T(8,128)(2,1)S(1)}, bf16[128,1024]{1,0:T(8,128)(2,1)S(1)}) custom-call(s32[7,4]{1,0:T(8,128)S(1)} %add_add_fusion.table, f32[8,128]{1,0:T(8,128)S(1)} %touch.1.after, bf16[128,1024]{1,0:T(8,128)(2,1)S(1)} %get-tuple-element.110.refs_0_, bf16[128,1024]{1,0:T(8,128)(2,1)S(1)} %get-tuple-element.109.refs_1_, ...), custom_call_target="tpu_custom_call" | custom-call | flops 1610612736 | bytes 1048576 | tf_op jit(solution)/shard_map/rest/pallas_call | solution.py:366
  104.7 4.2 %collective-permute-done.19 = bf16[128,1024]{1,0:T(8,128)(2,1)S(1)} collective-permute-done((bf16[128,1024]{1,0:T(8,128)(2,1)S(1)}, bf16[128,1024]{1,0:T(8,128)(2,1)S(1)}, u32[]{:S(2)}, u32[]{:S(2)}) %collective-permute-start.19) | collective-permute-done | bytes 262176 | tf_op jit(solution)/shard_map/ppermute | solution.py:232
  109.0 5.0 %collective-permute-start.24 = (bf16[128,1024]{1,0:T(8,128)(2,1)S(1)}, bf16[128,1024]{1,0:T(8,128)(2,1)S(1)}, u32[]{:S(2)}, u32[]{:S(2)}) collective-permute-start(bf16[128,1024]{1,0:T(8,128)(2,1)S(1)} %add_convert_fusion.3), channel_id=1, source_target_pairs={{0,8},{4,12},{8,16},{12,20},{16,24},{20,28},{1,9},{5,13},{9,17},{1... | collective-permute-start | bytes 786440 | tf_op jit(solution)/shard_map/ppermute | solution.py:232
  122.8 4.9 %collective-permute-done.25 = bf16[128,1024]{1,0:T(8,128)(2,1)S(1)} collective-permute-done((bf16[128,1024]{1,0:T(8,128)(2,1)S(1)}, bf16[128,1024]{1,0:T(8,128)(2,1)S(1)}, u32[]{:S(2)}, u32[]{:S(2)}) %collective-permute-start.25) | collective-permute-done | bytes 262176 | tf_op jit(solution)/shard_map/ppermute | solution.py:232
  127.8 7.1 %collective-permute-start.30 = (bf16[128,1024]{1,0:T(8,128)(2,1)S(1)}, bf16[128,1024]{1,0:T(8,128)(2,1)S(1)}, u32[]{:S(2)}, u32[]{:S(2)}) collective-permute-start(bf16[128,1024]{1,0:T(8,128)(2,1)S(1)} %add_convert_fusion.2), channel_id=1, source_target_pairs={{0,8},{4,12},{8,16},{12,20},{16,24},{20,28},{1,9},{5,13},{9,17},{1... | collective-permute-start | bytes 786440 | tf_op jit(solution)/shard_map/ppermute | solution.py:232
  134.9 2.7 %collective-permute-start.29 = (bf16[128,1024]{1,0:T(8,128)(2,1)S(1)}, bf16[128,1024]{1,0:T(8,128)(2,1)S(1)}, u32[]{:S(2)}, u32[]{:S(2)}) collective-permute-start(bf16[128,1024]{1,0:T(8,128)(2,1)S(1)} %add_convert_fusion.2), channel_id=1, source_target_pairs={{0,12},{4,8},{8,20},{12,16},{16,28},{20,24},{1,13},{5,9},{9,21},{1... | collective-permute-start | bytes 786440 | tf_op jit(solution)/shard_map/ppermute | solution.py:232
  148.8 5.3 %collective-permute-start.36 = (bf16[128,1024]{1,0:T(8,128)(2,1)S(1)}, bf16[128,1024]{1,0:T(8,128)(2,1)S(1)}, u32[]{:S(2)}, u32[]{:S(2)}) collective-permute-start(bf16[128,1024]{1,0:T(8,128)(2,1)S(1)} %add_convert_fusion.1), channel_id=1, source_target_pairs={{0,8},{4,12},{8,16},{12,20},{16,24},{20,28},{1,9},{5,13},{9,17},{1... | collective-permute-start | bytes 786440 | tf_op jit(solution)/shard_map/ppermute | solution.py:232
  154.1 2.5 %collective-permute-done.22 = bf16[128,256]{1,0:T(8,128)(2,1)S(1)} collective-permute-done((bf16[128,256]{1,0:T(8,128)(2,1)S(1)}, bf16[128,256]{1,0:T(8,128)(2,1)S(1)}, u32[]{:S(2)}, u32[]{:S(2)}) %collective-permute-start.22) | collective-permute-done | bytes 65568 | tf_op jit(solution)/shard_map/ppermute | solution.py:232
  164.6 5.4 %collective-permute-done.28 = bf16[128,256]{1,0:T(8,128)(2,1)S(1)} collective-permute-done((bf16[128,256]{1,0:T(8,128)(2,1)S(1)}, bf16[128,256]{1,0:T(8,128)(2,1)S(1)}, u32[]{:S(2)}, u32[]{:S(2)}) %collective-permute-start.28) | collective-permute-done | bytes 65568 | tf_op jit(solution)/shard_map/ppermute | solution.py:232
  176.1 3.3 %collective-permute-done.34 = bf16[128,256]{1,0:T(8,128)(2,1)S(1)} collective-permute-done((bf16[128,256]{1,0:T(8,128)(2,1)S(1)}, bf16[128,256]{1,0:T(8,128)(2,1)S(1)}, u32[]{:S(2)}, u32[]{:S(2)}) %collective-permute-start.34) | collective-permute-done | bytes 65568 | tf_op jit(solution)/shard_map/ppermute | solution.py:232
  179.4 5.3 %collective-permute-done.40 = bf16[128,256]{1,0:T(8,128)(2,1)S(1)} collective-permute-done((bf16[128,256]{1,0:T(8,128)(2,1)S(1)}, bf16[128,256]{1,0:T(8,128)(2,1)S(1)}, u32[]{:S(2)}, u32[]{:S(2)}) %collective-permute-start.40) | collective-permute-done | bytes 65568 | tf_op jit(solution)/shard_map/ppermute | solution.py:232
  (139 shorter events, 83.5 us)
Async XLA Ops:
  0.9 17.4 %collective-permute-start.3 = (bf16[1,128,256]{2,1,0:T(8,128)(2,1)S(1)}, bf16[1,128,256]{2,1,0:T(8,128)(2,1)S(1)}, u32[]{:S(2)}, u32[]{:S(2)}) collective-permute-start(bf16[1,128,256]{2,1,0:T(8,128)(2,1)S(1)} %get-tuple-element.68), channel_id=1, source_target_pairs={{16,0},{20,4},{0,16},{4,20},{17,1},{21,5},{1,17},{5,21},{18,2},{22... | collective-permute-start | bytes 196616 | tf_op jit(solution)/shard_map/ppermute | solution.py:232
  6.9 11.4 %collective-permute-start.4 = (bf16[1,128,256]{2,1,0:T(8,128)(2,1)S(1)}, bf16[1,128,256]{2,1,0:T(8,128)(2,1)S(1)}, u32[]{:S(2)}, u32[]{:S(2)}) collective-permute-start(bf16[1,128,256]{2,1,0:T(8,128)(2,1)S(1)} %get-tuple-element.69), channel_id=1, source_target_pairs={{8,0},{12,4},{24,16},{28,20},{9,1},{13,5},{25,17},{29,21},{10,2},{... | collective-permute-start | bytes 196616 | tf_op jit(solution)/shard_map/ppermute | solution.py:232
  8.2 10.1 %collective-permute-start.5 = (bf16[1,128,256]{2,1,0:T(8,128)(2,1)S(1)}, bf16[1,128,256]{2,1,0:T(8,128)(2,1)S(1)}, u32[]{:S(2)}, u32[]{:S(2)}) collective-permute-start(bf16[1,128,256]{2,1,0:T(8,128)(2,1)S(1)} %get-tuple-element.70), channel_id=1, source_target_pairs={{24,0},{28,4},{8,16},{12,20},{25,1},{29,5},{9,17},{13,21},{26,2},{... | collective-permute-start | bytes 196616 | tf_op jit(solution)/shard_map/ppermute | solution.py:232
  18.4 7.8 %collective-permute-start.6 = (bf16[128,1024]{1,0:T(8,128)(2,1)S(1)}, bf16[128,1024]{1,0:T(8,128)(2,1)S(1)}, u32[]{:S(2)}, u32[]{:S(2)}) collective-permute-start(bf16[128,1024]{1,0:T(8,128)(2,1)S(1)} %pad_maximum_fusion.refs_0_), channel_id=1, source_target_pairs={{0,4},{4,0},{8,12},{12,8},{16,20},{20,16},{24,28},{28,24},{1,5},{5... | collective-permute-start | bytes 786440 | tf_op jit(solution)/shard_map/ppermute | solution.py:232
  30.7 15.6 %collective-permute-start = (bf16[3,128,256]{2,1,0:T(8,128)(2,1)S(1)}, bf16[3,128,256]{2,1,0:T(8,128)(2,1)S(1)}, u32[]{:S(2)}, u32[]{:S(2)}) collective-permute-start(bf16[3,128,256]{2,1,0:T(8,128)(2,1)S(1)} %get-tuple-element.64), channel_id=1, source_target_pairs={{8,0},{12,4},{24,16},{28,20},{9,1},{13,5},{25,17},{29,21},{10,2},{... | collective-permute-start | bytes 589832 | tf_op jit(solution)/shard_map/ppermute | solution.py:232
  32.0 14.3 %collective-permute-start.1 = (bf16[3,128,256]{2,1,0:T(8,128)(2,1)S(1)}, bf16[3,128,256]{2,1,0:T(8,128)(2,1)S(1)}, u32[]{:S(2)}, u32[]{:S(2)}) collective-permute-start(bf16[3,128,256]{2,1,0:T(8,128)(2,1)S(1)} %get-tuple-element.65), channel_id=1, source_target_pairs={{16,0},{20,4},{0,16},{4,20},{17,1},{21,5},{1,17},{5,21},{18,2},{22... | collective-permute-start | bytes 589832 | tf_op jit(solution)/shard_map/ppermute | solution.py:232
  33.9 12.4 %collective-permute-start.2 = (bf16[3,128,256]{2,1,0:T(8,128)(2,1)S(1)}, bf16[3,128,256]{2,1,0:T(8,128)(2,1)S(1)}, u32[]{:S(2)}, u32[]{:S(2)}) collective-permute-start(bf16[3,128,256]{2,1,0:T(8,128)(2,1)S(1)} %get-tuple-element.66), channel_id=1, source_target_pairs={{24,0},{28,4},{8,16},{12,20},{25,1},{29,5},{9,17},{13,21},{26,2},{... | collective-permute-start | bytes 589832 | tf_op jit(solution)/shard_map/ppermute | solution.py:232
  36.4 11.9 %collective-permute-start.12 = (bf16[128,1024]{1,0:T(8,128)(2,1)S(1)}, bf16[128,1024]{1,0:T(8,128)(2,1)S(1)}, u32[]{:S(2)}, u32[]{:S(2)}) collective-permute-start(bf16[128,1024]{1,0:T(8,128)(2,1)S(1)} %add_convert_fusion.6), channel_id=1, source_target_pairs={{0,8},{4,12},{8,16},{12,20},{16,24},{20,28},{1,9},{5,13},{9,17},{1... | collective-permute-start | bytes 786440 | tf_op jit(solution)/shard_map/ppermute | solution.py:232
  42.0 9.2 %collective-permute-start.11 = (bf16[128,1024]{1,0:T(8,128)(2,1)S(1)}, bf16[128,1024]{1,0:T(8,128)(2,1)S(1)}, u32[]{:S(2)}, u32[]{:S(2)}) collective-permute-start(bf16[128,1024]{1,0:T(8,128)(2,1)S(1)} %add_convert_fusion.6), channel_id=1, source_target_pairs={{0,12},{4,8},{8,20},{12,16},{16,28},{20,24},{1,13},{5,9},{9,21},{1... | collective-permute-start | bytes 786440 | tf_op jit(solution)/shard_map/ppermute | solution.py:232
  62.3 12.0 %collective-permute-start.15 = (bf16[128,1024]{1,0:T(8,128)(2,1)S(1)}, bf16[128,1024]{1,0:T(8,128)(2,1)S(1)}, u32[]{:S(2)}, u32[]{:S(2)}) collective-permute-start(bf16[128,1024]{1,0:T(8,128)(2,1)S(1)} %add_convert_fusion.5), channel_id=1, source_target_pairs={{0,8},{4,12},{8,16},{12,20},{16,24},{20,28},{1,9},{5,13},{9,17},{1... | collective-permute-start | bytes 786440 | tf_op jit(solution)/shard_map/ppermute | solution.py:232
  67.9 9.3 %collective-permute-start.9 = (bf16[128,1024]{1,0:T(8,128)(2,1)S(1)}, bf16[128,1024]{1,0:T(8,128)(2,1)S(1)}, u32[]{:S(2)}, u32[]{:S(2)}) collective-permute-start(bf16[128,1024]{1,0:T(8,128)(2,1)S(1)} %pad_maximum_fusion.2), channel_id=1, source_target_pairs={{0,4},{4,0},{8,12},{12,8},{16,20},{20,16},{24,28},{28,24},{1,5},{5... | collective-permute-start | bytes 786440 | tf_op jit(solution)/shard_map/ppermute | solution.py:232
  69.7 7.5 %collective-permute-start.14 = (bf16[128,1024]{1,0:T(8,128)(2,1)S(1)}, bf16[128,1024]{1,0:T(8,128)(2,1)S(1)}, u32[]{:S(2)}, u32[]{:S(2)}) collective-permute-start(bf16[128,1024]{1,0:T(8,128)(2,1)S(1)} %add_convert_fusion.5), channel_id=1, source_target_pairs={{0,12},{4,8},{8,20},{12,16},{16,28},{20,24},{1,13},{5,9},{9,21},{1... | collective-permute-start | bytes 786440 | tf_op jit(solution)/shard_map/ppermute | solution.py:232
  86.6 10.1 %collective-permute-start.18 = (bf16[128,1024]{1,0:T(8,128)(2,1)S(1)}, bf16[128,1024]{1,0:T(8,128)(2,1)S(1)}, u32[]{:S(2)}, u32[]{:S(2)}) collective-permute-start(bf16[128,1024]{1,0:T(8,128)(2,1)S(1)} %add_convert_fusion.4), channel_id=1, source_target_pairs={{0,8},{4,12},{8,16},{12,20},{16,24},{20,28},{1,9},{5,13},{9,17},{1... | collective-permute-start | bytes 786440 | tf_op jit(solution)/shard_map/ppermute | solution.py:232
  92.2 7.3 %collective-permute-start.8 = (bf16[128,1024]{1,0:T(8,128)(2,1)S(1)}, bf16[128,1024]{1,0:T(8,128)(2,1)S(1)}, u32[]{:S(2)}, u32[]{:S(2)}) collective-permute-start(bf16[128,1024]{1,0:T(8,128)(2,1)S(1)} %pad_maximum_fusion.1), channel_id=1, source_target_pairs={{0,4},{4,0},{8,12},{12,8},{16,20},{20,16},{24,28},{28,24},{1,5},{5... | collective-permute-start | bytes 786440 | tf_op jit(solution)/shard_map/ppermute | solution.py:232
  109.0 8.9 %collective-permute-start.24 = (bf16[128,1024]{1,0:T(8,128)(2,1)S(1)}, bf16[128,1024]{1,0:T(8,128)(2,1)S(1)}, u32[]{:S(2)}, u32[]{:S(2)}) collective-permute-start(bf16[128,1024]{1,0:T(8,128)(2,1)S(1)} %add_convert_fusion.3), channel_id=1, source_target_pairs={{0,8},{4,12},{8,16},{12,20},{16,24},{20,28},{1,9},{5,13},{9,17},{1... | collective-permute-start | bytes 786440 | tf_op jit(solution)/shard_map/ppermute | solution.py:232
  127.8 10.9 %collective-permute-start.30 = (bf16[128,1024]{1,0:T(8,128)(2,1)S(1)}, bf16[128,1024]{1,0:T(8,128)(2,1)S(1)}, u32[]{:S(2)}, u32[]{:S(2)}) collective-permute-start(bf16[128,1024]{1,0:T(8,128)(2,1)S(1)} %add_convert_fusion.2), channel_id=1, source_target_pairs={{0,8},{4,12},{8,16},{12,20},{16,24},{20,28},{1,9},{5,13},{9,17},{1... | collective-permute-start | bytes 786440 | tf_op jit(solution)/shard_map/ppermute | solution.py:232
  143.5 10.6 %collective-permute-start.20 = (bf16[128,256]{1,0:T(8,128)(2,1)S(1)}, bf16[128,256]{1,0:T(8,128)(2,1)S(1)}, u32[]{:S(2)}, u32[]{:S(2)}) collective-permute-start(bf16[128,256]{1,0:T(8,128)(2,1)S(1)} %get-tuple-element.141), channel_id=1, source_target_pairs={{24,16},{28,20},{25,17},{29,21},{26,18},{30,22},{27,19},{31,23}} | collective-permute-start | bytes 196616 | tf_op jit(solution)/shard_map/ppermute | solution.py:232
  144.2 9.9 %collective-permute-start.21 = (bf16[128,256]{1,0:T(8,128)(2,1)S(1)}, bf16[128,256]{1,0:T(8,128)(2,1)S(1)}, u32[]{:S(2)}, u32[]{:S(2)}) collective-permute-start(bf16[128,256]{1,0:T(8,128)(2,1)S(1)} %get-tuple-element.140), channel_id=1, source_target_pairs={{24,8},{28,12},{25,9},{29,13},{26,10},{30,14},{27,11},{31,15}} | collective-permute-start | bytes 196616 | tf_op jit(solution)/shard_map/ppermute | solution.py:232
  144.8 11.8 %collective-permute-start.22 = (bf16[128,256]{1,0:T(8,128)(2,1)S(1)}, bf16[128,256]{1,0:T(8,128)(2,1)S(1)}, u32[]{:S(2)}, u32[]{:S(2)}) collective-permute-start(bf16[128,256]{1,0:T(8,128)(2,1)S(1)} %get-tuple-element.139), channel_id=1, source_target_pairs={{24,0},{28,4},{25,1},{29,5},{26,2},{30,6},{27,3},{31,7}} | collective-permute-start | bytes 196616 | tf_op jit(solution)/shard_map/ppermute | solution.py:232
  148.8 12.5 %collective-permute-start.36 = (bf16[128,1024]{1,0:T(8,128)(2,1)S(1)}, bf16[128,1024]{1,0:T(8,128)(2,1)S(1)}, u32[]{:S(2)}, u32[]{:S(2)}) collective-permute-start(bf16[128,1024]{1,0:T(8,128)(2,1)S(1)} %add_convert_fusion.1), channel_id=1, source_target_pairs={{0,8},{4,12},{8,16},{12,20},{16,24},{20,28},{1,9},{5,13},{9,17},{1... | collective-permute-start | bytes 786440 | tf_op jit(solution)/shard_map/ppermute | solution.py:232
  160.0 10.0 %collective-permute-start.28 = (bf16[128,256]{1,0:T(8,128)(2,1)S(1)}, bf16[128,256]{1,0:T(8,128)(2,1)S(1)}, u32[]{:S(2)}, u32[]{:S(2)}) collective-permute-start(bf16[128,256]{1,0:T(8,128)(2,1)S(1)} %get-tuple-element.142), channel_id=1, source_target_pairs={{24,0},{28,4},{25,1},{29,5},{26,2},{30,6},{27,3},{31,7}} | collective-permute-start | bytes 196616 | tf_op jit(solution)/shard_map/ppermute | solution.py:232
  163.1 10.2 %collective-permute-start.37 = (bf16[128,1024]{1,0:T(8,128)(2,1)S(1)}, bf16[128,1024]{1,0:T(8,128)(2,1)S(1)}, u32[]{:S(2)}, u32[]{:S(2)}) collective-permute-start(bf16[128,1024]{1,0:T(8,128)(2,1)S(1)} %get-tuple-element.108), channel_id=1, source_target_pairs={{0,4},{4,0},{8,12},{12,8},{16,20},{20,16},{24,28},{28,24},{1,5},{5... | collective-permute-start | bytes 786440 | tf_op jit(solution)/shard_map/ppermute | solution.py:232
  171.4 8.0 %collective-permute-start.34 = (bf16[128,256]{1,0:T(8,128)(2,1)S(1)}, bf16[128,256]{1,0:T(8,128)(2,1)S(1)}, u32[]{:S(2)}, u32[]{:S(2)}) collective-permute-start(bf16[128,256]{1,0:T(8,128)(2,1)S(1)} %get-tuple-element.145), channel_id=1, source_target_pairs={{24,0},{28,4},{25,1},{29,5},{26,2},{30,6},{27,3},{31,7}} | collective-permute-start | bytes 196616 | tf_op jit(solution)/shard_map/ppermute | solution.py:232
  174.8 10.0 %collective-permute-start.40 = (bf16[128,256]{1,0:T(8,128)(2,1)S(1)}, bf16[128,256]{1,0:T(8,128)(2,1)S(1)}, u32[]{:S(2)}, u32[]{:S(2)}) collective-permute-start(bf16[128,256]{1,0:T(8,128)(2,1)S(1)} %get-tuple-element.148), channel_id=1, source_target_pairs={{24,0},{28,4},{25,1},{29,5},{26,2},{30,6},{27,3},{31,7}} | collective-permute-start | bytes 196616 | tf_op jit(solution)/shard_map/ppermute | solution.py:232
  (23 other events, 128.0 us)

commit v2 on v1

--- a/solution.py
+++ b/solution.py
@@ -17,7 +17,6 @@
 
 VMEM = pl.BlockSpec(memory_space=pltpu.VMEM)
 ANY = pl.BlockSpec(memory_space=pl.ANY)
-SMEM = pl.BlockSpec(memory_space=pltpu.SMEM)
 f32 = jnp.float32
 bf16 = jnp.bfloat16
 
@@ -65,8 +64,14 @@
         emit(start, tile, total)
 
 
-def own_kernel(group, same, t, table, after, *refs):
-    scal = [table[t, i] for i in range(4)]
+def position(group, t, batches):
+    index = lax.axis_index("segment")
+    section = lax.div(index, group)
+    return section, lax.rem(index, group), (t >= section) & (t < section + batches)
+
+
+def own_kernel(group, same, t, batches, lens, after, *refs):
+    _, me, active = position(group, t, batches)
     n = CHUNKS
     xk = refs[:n]
     refs = refs[n:]
@@ -79,9 +84,9 @@
     head_cols = w.shape[1] // 3
     share = w.shape[0] // (group * SECTIONS)
 
-    @pl.when(scal[1] == 1)
+    @pl.when(active)
     def _():
-        part = scal[0]
+        part = me
         lk, sk = scaled(xk, gk, part, group, share, SECTIONS)
         lq, sq = scaled(xq, gq, part, group, share, SECTIONS)
 
@@ -93,8 +98,8 @@
         sums[:, 128:256] = jnp.broadcast_to(sk, (sk.shape[0], 128))
 
 
-def rest_kernel(group, same, t, table, after, *refs):
-    scal = [table[t, i] for i in range(4)]
+def rest_kernel(group, same, t, batches, lens, after, *refs):
+    section, me, active = position(group, t, batches)
     n = CHUNKS * (group - 1)
     xk = refs[:n]
     refs = refs[n:]
@@ -111,9 +116,8 @@
     share = width // (group * SECTIONS)
     rows = mix.shape[0]
 
-    @pl.when(scal[1] == 1)
+    @pl.when(active)
     def _():
-        me = scal[0]
         parts, lqs, lks = [], [], []
         sq = sums[:, 0:1]
         sk = sums[:, 128:129]
@@ -139,7 +143,9 @@
 
         query = lax.broadcasted_iota(jnp.int32, (rows, rows), 0)
         key = lax.broadcasted_iota(jnp.int32, (rows, rows), 1)
-        allowed = (key < scal[2]) & ((key <= query) | (scal[3] == 0))
+        last = section == SECTIONS - 1
+        slot = jnp.clip(t - section, 0, batches - 1) + jnp.where(last, batches, 0)
+        allowed = (key < lens[pl.ds(slot, 1), :]) & ((key <= query) | jnp.logical_not(last))
         allowed = jnp.concatenate([allowed.astype(f32)] * 2, 0) > 0.5
         lane = lax.broadcasted_iota(jnp.int32, (rows, 2 * HEAD), 1)
         low = lane < HEAD
@@ -170,19 +176,19 @@
                 ref[:, at : at + share] = dot(mixture, wo[:, column]).astype(bf16)
 
 
-def tail_kernel(group, t, table, mix, *refs):
-    scal = [table[t, i] for i in range(4)]
+def tail_kernel(group, t, batches, mix, *refs):
+    _, me, active = position(group, t, batches)
     xq = refs[:CHUNKS]
     wo = refs[CHUNKS]
     bases = refs[CHUNKS + 1 :]
     share = wo.shape[1] // (group * SECTIONS)
 
-    @pl.when(scal[1] == 1)
+    @pl.when(active)
     def _():
         mixture = mix[...]
         per = SECTIONS // CHUNKS
         for z in range(SECTIONS):
-            column = rows_of(z, scal[0], group, share)
+            column = rows_of(z, me, group, share)
             at = (z % per) * share
             res = xq[z // per][:, at : at + share].astype(f32)
             bases[z // per][:, at : at + share] = dot(mixture, wo[:, column]) + res
@@ -275,20 +281,8 @@
         ]
 
     periods = batches + SECTIONS - 1
-    step = jnp.arange(periods, dtype=jnp.int32)
-    slot = step - section
-    lengths = jnp.where(at_section[SECTIONS - 1], tgt_lengths, src_lengths)
-    here = slot[:, None] == jnp.arange(batches, dtype=jnp.int32)[None]
-    table = jnp.stack(
-        [
-            jnp.broadcast_to(member, step.shape),
-            jnp.any(here, axis=1).astype(jnp.int32),
-            jnp.sum(jnp.where(here, lengths[None], 0), axis=1),
-            jnp.where(at_section[SECTIONS - 1], jnp.ones_like(step), 0),
-        ],
-        axis=1,
-    ).astype(jnp.int32)
-    table = pltpu.with_memory_space_constraint(table, pltpu.SMEM)
+    lens = jnp.concatenate([src_lengths, tgt_lengths]).astype(jnp.int32)
+    lens = jnp.broadcast_to(lens[:, None], (2 * batches, rows))
 
     early = collect(0, 1)
     late = [collect(1, batches)]
@@ -341,12 +335,12 @@
         same = xq is xk
         inputs = list(xk[0]) + ([] if same else list(xq[0]))
         return pl.pallas_call(
-            functools.partial(own_kernel, group, same, t),
+            functools.partial(own_kernel, group, same, t, batches),
             out_shape=(
                 jax.ShapeDtypeStruct((rows, 3 * head_cols), f32),
                 jax.ShapeDtypeStruct((rows, 256), f32),
             ),
-            in_specs=[SMEM, ANY] + [VMEM] * (len(inputs) + 3),
+            in_specs=[VMEM, ANY] + [VMEM] * (len(inputs) + 3),
             out_specs=(VMEM, VMEM),
             compiler_params=params(2 << 20),
             cost_estimate=pl.CostEstimate(
@@ -355,7 +349,7 @@
                 transcendentals=0,
             ),
             name="own",
-        )(table, after, *inputs, gain_q, gain_kv, w_in)
+        )(lens, after, *inputs, gain_q, gain_kv, w_in)
 
     n_send = CHUNKS * (group - 1)
 
@@ -364,12 +358,12 @@
         same = xq is xk
         inputs = flat(xk[1:]) + ([] if same else flat(xq[1:]))
         outs = pl.pallas_call(
-            functools.partial(rest_kernel, group, same, t),
+            functools.partial(rest_kernel, group, same, t, batches),
             out_shape=tuple(
                 [jax.ShapeDtypeStruct((rows, chunk_width), bf16)] * n_send
                 + [jax.ShapeDtypeStruct((rows, head_cols), bf16)]
             ),
-            in_specs=[SMEM, ANY] + [VMEM] * (len(inputs) + 6),
+            in_specs=[VMEM, ANY] + [VMEM] * (len(inputs) + 6),
             out_specs=tuple([VMEM] * (n_send + 1)),
             scratch_shapes=[pltpu.VMEM((rows, 3 * head_cols), bf16)],
             compiler_params=params(4 << 20),
@@ -379,22 +373,22 @@
                 transcendentals=rows * rows * (head_cols // HEAD),
             ),
             name="rest",
-        )(table, after, *inputs, gain_q, gain_kv, w_in, w_out, *partial)
+        )(lens, after, *inputs, gain_q, gain_kv, w_in, w_out, *partial)
         return outs[:n_send], outs[n_send]
 
     def tail(fed, mix):
         t, _, xq = fed
         return pl.pallas_call(
-            functools.partial(tail_kernel, group, t),
+            functools.partial(tail_kernel, group, t, batches),
             out_shape=tuple([jax.ShapeDtypeStruct((rows, chunk_width), f32)] * CHUNKS),
-            in_specs=[SMEM] + [VMEM] * (2 + CHUNKS),
+            in_specs=[VMEM] * (2 + CHUNKS),
             out_specs=tuple([VMEM] * CHUNKS),
             compiler_params=params(1 << 20),
             cost_estimate=pl.CostEstimate(
                 flops=2 * rows * part_width * head_cols, bytes_accessed=1 << 20, transcendentals=0
             ),
             name="tail",
-        )(table, mix, *xq[0], w_out)
+        )(mix, *xq[0], w_out)
 
     enter(0)
     fed, partial = feed(0, None)

time: 186 us -> 186 us (level)
  Pallas kernels: 28.1 us -> 15.3 us
  waiting for transfers between devices: 58.2 us -> 70.2 us
  local copies, waits for them, and re-layouts: 9.94 us -> 12.5 us
    pallas_call x21, Pallas kernels: 28.1 us -> 15.3 us  [the longest x7 9.15 us: rest(): pl.pallas_call(functools.partial(rest_kernel, group, same, t, batches), o...]
    ppermute x41, waiting for transfers between devices: 58.2 us -> 70.2 us  [permute(): return lax.ppermute(value, axis, pairs)]
    unnamed x12 -> x16, local copies, waits for them, and re-layouts: 9.62 us -> 12.4 us
  transfers between devices with their start and end apart: 41 -> 41, of which waited for: 23 -> 23; matrix products, arithmetic and copies ran while one was open for 1% -> 1% of each run, Pallas kernels for 8% -> 3%
where the time goes in v2:
time: 186 us; the launch traced here: 185 us
  starting transfers between devices  82.6 us (44%)
  waiting for transfers between devices  70.2 us (38%)
  Pallas kernels  15.3 us (8%)
  local copies, waits for them, and re-layouts  12.5 us (7%)
  other arithmetic  3.81 us (2%)
    ppermute x41, starting transfers between devices, permute(): return lax.ppermute(value, axis, pairs)  82.6 us
    ppermute x41, waiting for transfers between devices, permute(): return lax.ppermute(value, axis, pairs)  70.2 us
    unnamed x16, local copies, waits for them, and re-layouts  12.4 us
    pallas_call x7, Pallas kernels, rest(): pl.pallas_call(functools.partial(rest_kernel, group, same, t, batches), o...  9.15 us
    pallas_call x7, Pallas kernels, own(): pl.pallas_call(functools.partial(own_kernel, group, same, t, batches), ou...  4.24 us
  transfers between devices with their start and end apart: 41, of which 23 were waited for; matrix products, arithmetic and copies ran while one was open for 1% of the time, Pallas kernels for 3%

profile of v2, /device:TPU:0, one launch (start us, length us, event | category | flops | bytes accessed | tf_op | source)
XLA Modules:
  0.0 185.1 jit_solution(9068739115532222248)
XLA Ops:
  0.9 6.0 %collective-permute-start.3 = (bf16[1,128,256]{2,1,0:T(8,128)(2,1)S(1)}, bf16[1,128,256]{2,1,0:T(8,128)(2,1)S(1)}, u32[]{:S(2)}, u32[]{:S(2)}) collective-permute-start(bf16[1,128,256]{2,1,0:T(8,128)(2,1)S(1)} %get-tuple-element.64), channel_id=1, source_target_pairs={{16,0},{20,4},{0,16},{4,20},{17,1},{21,5},{1,17},{5,21},{18,2},{22... | collective-permute-start | bytes 196616 | tf_op jit(solution)/shard_map/ppermute | solution.py:238
  9.5 3.5 %collective-permute-done.4 = bf16[1,128,256]{2,1,0:T(8,128)(2,1)S(1)} collective-permute-done((bf16[1,128,256]{2,1,0:T(8,128)(2,1)S(1)}, bf16[1,128,256]{2,1,0:T(8,128)(2,1)S(1)}, u32[]{:S(2)}, u32[]{:S(2)}) %collective-permute-start.4) | collective-permute-done | bytes 65568 | tf_op jit(solution)/shard_map/ppermute | solution.py:238
  13.0 3.1 %collective-permute-done.5 = bf16[1,128,256]{2,1,0:T(8,128)(2,1)S(1)} collective-permute-done((bf16[1,128,256]{2,1,0:T(8,128)(2,1)S(1)}, bf16[1,128,256]{2,1,0:T(8,128)(2,1)S(1)}, u32[]{:S(2)}, u32[]{:S(2)}) %collective-permute-start.5) | collective-permute-done | bytes 65568 | tf_op jit(solution)/shard_map/ppermute | solution.py:238
  18.7 4.6 %copy-done = bf16[1,2048,3072]{2,1,0:T(8,128)(2,1)S(1)} copy-done((bf16[1,2048,3072]{2,1,0:T(8,128)(2,1)S(1)}, bf16[1,2048,3072]{2,1,0:T(8,128)(2,1)}, u32[]{:S(2)}) %copy-start) | copy-done | bytes 12582936
  26.3 3.8 %copy-done.1 = bf16[1,2048,3072]{2,1,0:T(8,128)(2,1)S(1)} copy-done((bf16[1,2048,3072]{2,1,0:T(8,128)(2,1)S(1)}, bf16[1,2048,3072]{2,1,0:T(8,128)(2,1)}, u32[]{:S(2)}) %copy-start.1) | copy-done | bytes 12582936
  41.0 4.8 %collective-permute-start.12 = (bf16[128,1024]{1,0:T(8,128)(2,1)S(1)}, bf16[128,1024]{1,0:T(8,128)(2,1)S(1)}, u32[]{:S(2)}, u32[]{:S(2)}) collective-permute-start(bf16[128,1024]{1,0:T(8,128)(2,1)S(1)} %add_convert_fusion.6), channel_id=1, source_target_pairs={{0,8},{4,12},{8,16},{12,20},{16,24},{20,28},{1,9},{5,13},{9,17},{1... | collective-permute-start | bytes 786440 | tf_op jit(solution)/shard_map/ppermute | solution.py:238
  45.8 2.9 %collective-permute-start.11 = (bf16[128,1024]{1,0:T(8,128)(2,1)S(1)}, bf16[128,1024]{1,0:T(8,128)(2,1)S(1)}, u32[]{:S(2)}, u32[]{:S(2)}) collective-permute-start(bf16[128,1024]{1,0:T(8,128)(2,1)S(1)} %add_convert_fusion.6), channel_id=1, source_target_pairs={{0,12},{4,8},{8,20},{12,16},{16,28},{20,24},{1,13},{5,9},{9,21},{1... | collective-permute-start | bytes 786440 | tf_op jit(solution)/shard_map/ppermute | solution.py:238
  54.5 3.0 %collective-permute-done.10 = bf16[128,1024]{1,0:T(8,128)(2,1)S(1)} collective-permute-done((bf16[128,1024]{1,0:T(8,128)(2,1)S(1)}, bf16[128,1024]{1,0:T(8,128)(2,1)S(1)}, u32[]{:S(2)}, u32[]{:S(2)}) %collective-permute-start.10) | collective-permute-done | bytes 262176 | tf_op jit(solution)/shard_map/ppermute | solution.py:238
  62.1 4.1 %collective-permute-done.13 = bf16[128,1024]{1,0:T(8,128)(2,1)S(1)} collective-permute-done((bf16[128,1024]{1,0:T(8,128)(2,1)S(1)}, bf16[128,1024]{1,0:T(8,128)(2,1)S(1)}, u32[]{:S(2)}, u32[]{:S(2)}) %collective-permute-start.13) | collective-permute-done | bytes 262176 | tf_op jit(solution)/shard_map/ppermute | solution.py:238
  66.3 5.2 %collective-permute-start.15 = (bf16[128,1024]{1,0:T(8,128)(2,1)S(1)}, bf16[128,1024]{1,0:T(8,128)(2,1)S(1)}, u32[]{:S(2)}, u32[]{:S(2)}) collective-permute-start(bf16[128,1024]{1,0:T(8,128)(2,1)S(1)} %add_convert_fusion.5), channel_id=1, source_target_pairs={{0,8},{4,12},{8,16},{12,20},{16,24},{20,28},{1,9},{5,13},{9,17},{1... | collective-permute-start | bytes 786440 | tf_op jit(solution)/shard_map/ppermute | solution.py:238
  72.1 3.5 %collective-permute-start.14 = (bf16[128,1024]{1,0:T(8,128)(2,1)S(1)}, bf16[128,1024]{1,0:T(8,128)(2,1)S(1)}, u32[]{:S(2)}, u32[]{:S(2)}) collective-permute-start(bf16[128,1024]{1,0:T(8,128)(2,1)S(1)} %add_convert_fusion.5), channel_id=1, source_target_pairs={{0,12},{4,8},{8,20},{12,16},{16,28},{20,24},{1,13},{5,9},{9,21},{1... | collective-permute-start | bytes 786440 | tf_op jit(solution)/shard_map/ppermute | solution.py:238
  83.9 5.6 %collective-permute-done.16 = bf16[128,1024]{1,0:T(8,128)(2,1)S(1)} collective-permute-done((bf16[128,1024]{1,0:T(8,128)(2,1)S(1)}, bf16[128,1024]{1,0:T(8,128)(2,1)S(1)}, u32[]{:S(2)}, u32[]{:S(2)}) %collective-permute-start.16) | collective-permute-done | bytes 262176 | tf_op jit(solution)/shard_map/ppermute | solution.py:238
  89.6 4.7 %collective-permute-start.18 = (bf16[128,1024]{1,0:T(8,128)(2,1)S(1)}, bf16[128,1024]{1,0:T(8,128)(2,1)S(1)}, u32[]{:S(2)}, u32[]{:S(2)}) collective-permute-start(bf16[128,1024]{1,0:T(8,128)(2,1)S(1)} %add_convert_fusion.4), channel_id=1, source_target_pairs={{0,8},{4,12},{8,16},{12,20},{16,24},{20,28},{1,9},{5,13},{9,17},{1... | collective-permute-start | bytes 786440 | tf_op jit(solution)/shard_map/ppermute | solution.py:238
  106.2 5.3 %collective-permute-done.19 = bf16[128,1024]{1,0:T(8,128)(2,1)S(1)} collective-permute-done((bf16[128,1024]{1,0:T(8,128)(2,1)S(1)}, bf16[128,1024]{1,0:T(8,128)(2,1)S(1)}, u32[]{:S(2)}, u32[]{:S(2)}) %collective-permute-start.19) | collective-permute-done | bytes 262176 | tf_op jit(solution)/shard_map/ppermute | solution.py:238
  111.5 4.6 %collective-permute-start.24 = (bf16[128,1024]{1,0:T(8,128)(2,1)S(1)}, bf16[128,1024]{1,0:T(8,128)(2,1)S(1)}, u32[]{:S(2)}, u32[]{:S(2)}) collective-permute-start(bf16[128,1024]{1,0:T(8,128)(2,1)S(1)} %add_convert_fusion.3), channel_id=1, source_target_pairs={{0,8},{4,12},{8,16},{12,20},{16,24},{20,28},{1,9},{5,13},{9,17},{1... | collective-permute-start | bytes 786440 | tf_op jit(solution)/shard_map/ppermute | solution.py:238
  120.0 2.8 %collective-permute-done.23.refs_0_ = bf16[128,1024]{1,0:T(8,128)(2,1)S(1)} collective-permute-done((bf16[128,1024]{1,0:T(8,128)(2,1)S(1)}, bf16[128,1024]{1,0:T(8,128)(2,1)S(1)}, u32[]{:S(2)}, u32[]{:S(2)}) %collective-permute-start.23) | collective-permute-done | bytes 262176 | tf_op jit(solution)/shard_map/ppermute | solution.py:238
  124.3 5.0 %collective-permute-done.25 = bf16[128,1024]{1,0:T(8,128)(2,1)S(1)} collective-permute-done((bf16[128,1024]{1,0:T(8,128)(2,1)S(1)}, bf16[128,1024]{1,0:T(8,128)(2,1)S(1)}, u32[]{:S(2)}, u32[]{:S(2)}) %collective-permute-start.25) | collective-permute-done | bytes 262176 | tf_op jit(solution)/shard_map/ppermute | solution.py:238
  129.4 7.5 %collective-permute-start.30 = (bf16[128,1024]{1,0:T(8,128)(2,1)S(1)}, bf16[128,1024]{1,0:T(8,128)(2,1)S(1)}, u32[]{:S(2)}, u32[]{:S(2)}) collective-permute-start(bf16[128,1024]{1,0:T(8,128)(2,1)S(1)} %add_convert_fusion.2), channel_id=1, source_target_pairs={{0,8},{4,12},{8,16},{12,20},{16,24},{20,28},{1,9},{5,13},{9,17},{1... | collective-permute-start | bytes 786440 | tf_op jit(solution)/shard_map/ppermute | solution.py:238
  147.1 3.0 %collective-permute-done.31 = bf16[128,1024]{1,0:T(8,128)(2,1)S(1)} collective-permute-done((bf16[128,1024]{1,0:T(8,128)(2,1)S(1)}, bf16[128,1024]{1,0:T(8,128)(2,1)S(1)}, u32[]{:S(2)}, u32[]{:S(2)}) %collective-permute-start.31) | collective-permute-done | bytes 262176 | tf_op jit(solution)/shard_map/ppermute | solution.py:238
  150.2 4.8 %collective-permute-start.36 = (bf16[128,1024]{1,0:T(8,128)(2,1)S(1)}, bf16[128,1024]{1,0:T(8,128)(2,1)S(1)}, u32[]{:S(2)}, u32[]{:S(2)}) collective-permute-start(bf16[128,1024]{1,0:T(8,128)(2,1)S(1)} %add_convert_fusion.1), channel_id=1, source_target_pairs={{0,8},{4,12},{8,16},{12,20},{16,24},{20,28},{1,9},{5,13},{9,17},{1... | collective-permute-start | bytes 786440 | tf_op jit(solution)/shard_map/ppermute | solution.py:238
  155.0 3.0 %collective-permute-done.22 = bf16[128,256]{1,0:T(8,128)(2,1)S(1)} collective-permute-done((bf16[128,256]{1,0:T(8,128)(2,1)S(1)}, bf16[128,256]{1,0:T(8,128)(2,1)S(1)}, u32[]{:S(2)}, u32[]{:S(2)}) %collective-permute-start.22) | collective-permute-done | bytes 65568 | tf_op jit(solution)/shard_map/ppermute | solution.py:238
  164.6 5.9 %collective-permute-done.28 = bf16[128,256]{1,0:T(8,128)(2,1)S(1)} collective-permute-done((bf16[128,256]{1,0:T(8,128)(2,1)S(1)}, bf16[128,256]{1,0:T(8,128)(2,1)S(1)}, u32[]{:S(2)}, u32[]{:S(2)}) %collective-permute-start.28) | collective-permute-done | bytes 65568 | tf_op jit(solution)/shard_map/ppermute | solution.py:238
  176.0 3.9 %collective-permute-done.34 = bf16[128,256]{1,0:T(8,128)(2,1)S(1)} collective-permute-done((bf16[128,256]{1,0:T(8,128)(2,1)S(1)}, bf16[128,256]{1,0:T(8,128)(2,1)S(1)}, u32[]{:S(2)}, u32[]{:S(2)}) %collective-permute-start.34) | collective-permute-done | bytes 65568 | tf_op jit(solution)/shard_map/ppermute | solution.py:238
  179.9 4.5 %collective-permute-done.40 = bf16[128,256]{1,0:T(8,128)(2,1)S(1)} collective-permute-done((bf16[128,256]{1,0:T(8,128)(2,1)S(1)}, bf16[128,256]{1,0:T(8,128)(2,1)S(1)}, u32[]{:S(2)}, u32[]{:S(2)}) %collective-permute-start.40) | collective-permute-done | bytes 65568 | tf_op jit(solution)/shard_map/ppermute | solution.py:238
  (135 shorter events, 79.5 us)
Async XLA Ops:
  0.9 8.6 %collective-permute-start.3 = (bf16[1,128,256]{2,1,0:T(8,128)(2,1)S(1)}, bf16[1,128,256]{2,1,0:T(8,128)(2,1)S(1)}, u32[]{:S(2)}, u32[]{:S(2)}) collective-permute-start(bf16[1,128,256]{2,1,0:T(8,128)(2,1)S(1)} %get-tuple-element.64), channel_id=1, source_target_pairs={{16,0},{20,4},{0,16},{4,20},{17,1},{21,5},{1,17},{5,21},{18,2},{22... | collective-permute-start | bytes 196616 | tf_op jit(solution)/shard_map/ppermute | solution.py:238
  8.2 8.0 %collective-permute-start.5 = (bf16[1,128,256]{2,1,0:T(8,128)(2,1)S(1)}, bf16[1,128,256]{2,1,0:T(8,128)(2,1)S(1)}, u32[]{:S(2)}, u32[]{:S(2)}) collective-permute-start(bf16[1,128,256]{2,1,0:T(8,128)(2,1)S(1)} %get-tuple-element.66), channel_id=1, source_target_pairs={{24,0},{28,4},{8,16},{12,20},{25,1},{29,5},{9,17},{13,21},{26,2},{... | collective-permute-start | bytes 196616 | tf_op jit(solution)/shard_map/ppermute | solution.py:238
  16.2 14.9 %collective-permute-start.6 = (bf16[128,1024]{1,0:T(8,128)(2,1)S(1)}, bf16[128,1024]{1,0:T(8,128)(2,1)S(1)}, u32[]{:S(2)}, u32[]{:S(2)}) collective-permute-start(bf16[128,1024]{1,0:T(8,128)(2,1)S(1)} %pad_maximum_fusion.refs_0_), channel_id=1, source_target_pairs={{0,4},{4,0},{8,12},{12,8},{16,20},{20,16},{24,28},{28,24},{1,5},{5... | collective-permute-start | bytes 786440 | tf_op jit(solution)/shard_map/ppermute | solution.py:238
  35.2 15.1 %collective-permute-start = (bf16[3,128,256]{2,1,0:T(8,128)(2,1)S(1)}, bf16[3,128,256]{2,1,0:T(8,128)(2,1)S(1)}, u32[]{:S(2)}, u32[]{:S(2)}) collective-permute-start(bf16[3,128,256]{2,1,0:T(8,128)(2,1)S(1)} %get-tuple-element.60), channel_id=1, source_target_pairs={{8,0},{12,4},{24,16},{28,20},{9,1},{13,5},{25,17},{29,21},{10,2},{... | collective-permute-start | bytes 589832 | tf_op jit(solution)/shard_map/ppermute | solution.py:238
  36.5 13.8 %collective-permute-start.1 = (bf16[3,128,256]{2,1,0:T(8,128)(2,1)S(1)}, bf16[3,128,256]{2,1,0:T(8,128)(2,1)S(1)}, u32[]{:S(2)}, u32[]{:S(2)}) collective-permute-start(bf16[3,128,256]{2,1,0:T(8,128)(2,1)S(1)} %get-tuple-element.61), channel_id=1, source_target_pairs={{16,0},{20,4},{0,16},{4,20},{17,1},{21,5},{1,17},{5,21},{18,2},{22... | collective-permute-start | bytes 589832 | tf_op jit(solution)/shard_map/ppermute | solution.py:238
  38.4 11.8 %collective-permute-start.2 = (bf16[3,128,256]{2,1,0:T(8,128)(2,1)S(1)}, bf16[3,128,256]{2,1,0:T(8,128)(2,1)S(1)}, u32[]{:S(2)}, u32[]{:S(2)}) collective-permute-start(bf16[3,128,256]{2,1,0:T(8,128)(2,1)S(1)} %get-tuple-element.62), channel_id=1, source_target_pairs={{24,0},{28,4},{8,16},{12,20},{25,1},{29,5},{9,17},{13,21},{26,2},{... | collective-permute-start | bytes 589832 | tf_op jit(solution)/shard_map/ppermute | solution.py:238
  41.0 10.9 %collective-permute-start.12 = (bf16[128,1024]{1,0:T(8,128)(2,1)S(1)}, bf16[128,1024]{1,0:T(8,128)(2,1)S(1)}, u32[]{:S(2)}, u32[]{:S(2)}) collective-permute-start(bf16[128,1024]{1,0:T(8,128)(2,1)S(1)} %add_convert_fusion.6), channel_id=1, source_target_pairs={{0,8},{4,12},{8,16},{12,20},{16,24},{20,28},{1,9},{5,13},{9,17},{1... | collective-permute-start | bytes 786440 | tf_op jit(solution)/shard_map/ppermute | solution.py:238
  45.8 8.7 %collective-permute-start.11 = (bf16[128,1024]{1,0:T(8,128)(2,1)S(1)}, bf16[128,1024]{1,0:T(8,128)(2,1)S(1)}, u32[]{:S(2)}, u32[]{:S(2)}) collective-permute-start(bf16[128,1024]{1,0:T(8,128)(2,1)S(1)} %add_convert_fusion.6), channel_id=1, source_target_pairs={{0,12},{4,8},{8,20},{12,16},{16,28},{20,24},{1,13},{5,9},{9,21},{1... | collective-permute-start | bytes 786440 | tf_op jit(solution)/shard_map/ppermute | solution.py:238
  50.3 7.1 %collective-permute-start.10 = (bf16[128,1024]{1,0:T(8,128)(2,1)S(1)}, bf16[128,1024]{1,0:T(8,128)(2,1)S(1)}, u32[]{:S(2)}, u32[]{:S(2)}) collective-permute-start(bf16[128,1024]{1,0:T(8,128)(2,1)S(1)} %pad_maximum_fusion.3), channel_id=1, source_target_pairs={{0,4},{4,0},{8,12},{12,8},{16,20},{20,16},{24,28},{28,24},{1,5},{5... | collective-permute-start | bytes 786440 | tf_op jit(solution)/shard_map/ppermute | solution.py:238
  66.3 11.6 %collective-permute-start.15 = (bf16[128,1024]{1,0:T(8,128)(2,1)S(1)}, bf16[128,1024]{1,0:T(8,128)(2,1)S(1)}, u32[]{:S(2)}, u32[]{:S(2)}) collective-permute-start(bf16[128,1024]{1,0:T(8,128)(2,1)S(1)} %add_convert_fusion.5), channel_id=1, source_target_pairs={{0,8},{4,12},{8,16},{12,20},{16,24},{20,28},{1,9},{5,13},{9,17},{1... | collective-permute-start | bytes 786440 | tf_op jit(solution)/shard_map/ppermute | solution.py:238
  71.6 9.2 %collective-permute-start.9 = (bf16[128,1024]{1,0:T(8,128)(2,1)S(1)}, bf16[128,1024]{1,0:T(8,128)(2,1)S(1)}, u32[]{:S(2)}, u32[]{:S(2)}) collective-permute-start(bf16[128,1024]{1,0:T(8,128)(2,1)S(1)} %pad_maximum_fusion.2), channel_id=1, source_target_pairs={{0,4},{4,0},{8,12},{12,8},{16,20},{20,16},{24,28},{28,24},{1,5},{5... | collective-permute-start | bytes 786440 | tf_op jit(solution)/shard_map/ppermute | solution.py:238
  72.1 8.7 %collective-permute-start.14 = (bf16[128,1024]{1,0:T(8,128)(2,1)S(1)}, bf16[128,1024]{1,0:T(8,128)(2,1)S(1)}, u32[]{:S(2)}, u32[]{:S(2)}) collective-permute-start(bf16[128,1024]{1,0:T(8,128)(2,1)S(1)} %add_convert_fusion.5), channel_id=1, source_target_pairs={{0,12},{4,8},{8,20},{12,16},{16,28},{20,24},{1,13},{5,9},{9,21},{1... | collective-permute-start | bytes 786440 | tf_op jit(solution)/shard_map/ppermute | solution.py:238
  89.6 9.2 %collective-permute-start.18 = (bf16[128,1024]{1,0:T(8,128)(2,1)S(1)}, bf16[128,1024]{1,0:T(8,128)(2,1)S(1)}, u32[]{:S(2)}, u32[]{:S(2)}) collective-permute-start(bf16[128,1024]{1,0:T(8,128)(2,1)S(1)} %add_convert_fusion.4), channel_id=1, source_target_pairs={{0,8},{4,12},{8,16},{12,20},{16,24},{20,28},{1,9},{5,13},{9,17},{1... | collective-permute-start | bytes 786440 | tf_op jit(solution)/shard_map/ppermute | solution.py:238
  94.4 8.3 %collective-permute-start.8 = (bf16[128,1024]{1,0:T(8,128)(2,1)S(1)}, bf16[128,1024]{1,0:T(8,128)(2,1)S(1)}, u32[]{:S(2)}, u32[]{:S(2)}) collective-permute-start(bf16[128,1024]{1,0:T(8,128)(2,1)S(1)} %pad_maximum_fusion.1), channel_id=1, source_target_pairs={{0,4},{4,0},{8,12},{12,8},{16,20},{20,16},{24,28},{28,24},{1,5},{5... | collective-permute-start | bytes 786440 | tf_op jit(solution)/shard_map/ppermute | solution.py:238
  111.5 8.4 %collective-permute-start.24 = (bf16[128,1024]{1,0:T(8,128)(2,1)S(1)}, bf16[128,1024]{1,0:T(8,128)(2,1)S(1)}, u32[]{:S(2)}, u32[]{:S(2)}) collective-permute-start(bf16[128,1024]{1,0:T(8,128)(2,1)S(1)} %add_convert_fusion.3), channel_id=1, source_target_pairs={{0,8},{4,12},{8,16},{12,20},{16,24},{20,28},{1,9},{5,13},{9,17},{1... | collective-permute-start | bytes 786440 | tf_op jit(solution)/shard_map/ppermute | solution.py:238
  129.4 11.4 %collective-permute-start.30 = (bf16[128,1024]{1,0:T(8,128)(2,1)S(1)}, bf16[128,1024]{1,0:T(8,128)(2,1)S(1)}, u32[]{:S(2)}, u32[]{:S(2)}) collective-permute-start(bf16[128,1024]{1,0:T(8,128)(2,1)S(1)} %add_convert_fusion.2), channel_id=1, source_target_pairs={{0,8},{4,12},{8,16},{12,20},{16,24},{20,28},{1,9},{5,13},{9,17},{1... | collective-permute-start | bytes 786440 | tf_op jit(solution)/shard_map/ppermute | solution.py:238
  144.5 10.5 %collective-permute-start.20 = (bf16[128,256]{1,0:T(8,128)(2,1)S(1)}, bf16[128,256]{1,0:T(8,128)(2,1)S(1)}, u32[]{:S(2)}, u32[]{:S(2)}) collective-permute-start(bf16[128,256]{1,0:T(8,128)(2,1)S(1)} %get-tuple-element.137), channel_id=1, source_target_pairs={{24,16},{28,20},{25,17},{29,21},{26,18},{30,22},{27,19},{31,23}} | collective-permute-start | bytes 196616 | tf_op jit(solution)/shard_map/ppermute | solution.py:238
  145.1 9.9 %collective-permute-start.21 = (bf16[128,256]{1,0:T(8,128)(2,1)S(1)}, bf16[128,256]{1,0:T(8,128)(2,1)S(1)}, u32[]{:S(2)}, u32[]{:S(2)}) collective-permute-start(bf16[128,256]{1,0:T(8,128)(2,1)S(1)} %get-tuple-element.136), channel_id=1, source_target_pairs={{24,8},{28,12},{25,9},{29,13},{26,10},{30,14},{27,11},{31,15}} | collective-permute-start | bytes 196616 | tf_op jit(solution)/shard_map/ppermute | solution.py:238
  145.8 12.2 %collective-permute-start.22 = (bf16[128,256]{1,0:T(8,128)(2,1)S(1)}, bf16[128,256]{1,0:T(8,128)(2,1)S(1)}, u32[]{:S(2)}, u32[]{:S(2)}) collective-permute-start(bf16[128,256]{1,0:T(8,128)(2,1)S(1)} %get-tuple-element.135), channel_id=1, source_target_pairs={{24,0},{28,4},{25,1},{29,5},{26,2},{30,6},{27,3},{31,7}} | collective-permute-start | bytes 196616 | tf_op jit(solution)/shard_map/ppermute | solution.py:238
  150.2 12.5 %collective-permute-start.36 = (bf16[128,1024]{1,0:T(8,128)(2,1)S(1)}, bf16[128,1024]{1,0:T(8,128)(2,1)S(1)}, u32[]{:S(2)}, u32[]{:S(2)}) collective-permute-start(bf16[128,1024]{1,0:T(8,128)(2,1)S(1)} %add_convert_fusion.1), channel_id=1, source_target_pairs={{0,8},{4,12},{8,16},{12,20},{16,24},{20,28},{1,9},{5,13},{9,17},{1... | collective-permute-start | bytes 786440 | tf_op jit(solution)/shard_map/ppermute | solution.py:238
  161.4 9.1 %collective-permute-start.28 = (bf16[128,256]{1,0:T(8,128)(2,1)S(1)}, bf16[128,256]{1,0:T(8,128)(2,1)S(1)}, u32[]{:S(2)}, u32[]{:S(2)}) collective-permute-start(bf16[128,256]{1,0:T(8,128)(2,1)S(1)} %get-tuple-element.138), channel_id=1, source_target_pairs={{24,0},{28,4},{25,1},{29,5},{26,2},{30,6},{27,3},{31,7}} | collective-permute-start | bytes 196616 | tf_op jit(solution)/shard_map/ppermute | solution.py:238
  163.9 9.3 %collective-permute-start.37 = (bf16[128,1024]{1,0:T(8,128)(2,1)S(1)}, bf16[128,1024]{1,0:T(8,128)(2,1)S(1)}, u32[]{:S(2)}, u32[]{:S(2)}) collective-permute-start(bf16[128,1024]{1,0:T(8,128)(2,1)S(1)} %get-tuple-element.104), channel_id=1, source_target_pairs={{0,4},{4,0},{8,12},{12,8},{16,20},{20,16},{24,28},{28,24},{1,5},{5... | collective-permute-start | bytes 786440 | tf_op jit(solution)/shard_map/ppermute | solution.py:238
  171.9 8.0 %collective-permute-start.34 = (bf16[128,256]{1,0:T(8,128)(2,1)S(1)}, bf16[128,256]{1,0:T(8,128)(2,1)S(1)}, u32[]{:S(2)}, u32[]{:S(2)}) collective-permute-start(bf16[128,256]{1,0:T(8,128)(2,1)S(1)} %get-tuple-element.141), channel_id=1, source_target_pairs={{24,0},{28,4},{25,1},{29,5},{26,2},{30,6},{27,3},{31,7}} | collective-permute-start | bytes 196616 | tf_op jit(solution)/shard_map/ppermute | solution.py:238
  174.6 9.7 %collective-permute-start.40 = (bf16[128,256]{1,0:T(8,128)(2,1)S(1)}, bf16[128,256]{1,0:T(8,128)(2,1)S(1)}, u32[]{:S(2)}, u32[]{:S(2)}) collective-permute-start(bf16[128,256]{1,0:T(8,128)(2,1)S(1)} %get-tuple-element.144), channel_id=1, source_target_pairs={{24,0},{28,4},{25,1},{29,5},{26,2},{30,6},{27,3},{31,7}} | collective-permute-start | bytes 196616 | tf_op jit(solution)/shard_map/ppermute | solution.py:238
  (25 other events, 121.1 us)

commit v3 on v2

--- a/solution.py
+++ b/solution.py
@@ -393,14 +393,13 @@
     enter(0)
     fed, partial = feed(0, None)
     finals = {}
-    exits = {}
-
-    def leave(b):
-        value = finals[b]
+    exits = []
+
+    def leave(slots):
         pieces = []
         for z in range(SECTIONS):
             at, offset = divmod(z * share, chunk_width)
-            piece = value[at][:, offset : offset + share]
+            piece = jnp.stack([finals[b][at][:, offset : offset + share] for b in slots])
             if z < SECTIONS - 1:
                 pairs = [((SECTIONS - 1) * group + q, z * group + q) for q in range(group)]
                 piece = permute(piece, pairs)
@@ -408,7 +407,7 @@
         result = pieces[-1]
         for z in range(SECTIONS - 1):
             result = jnp.where(at_section[z], pieces[z], result)
-        exits[b] = result
+        exits.append(result)
 
     for t in range(periods):
         sends, mix = rest(fed, partial, token)
@@ -419,8 +418,8 @@
         ]
         if 0 < t < batches - 1:
             enter(t + 1)
-        if t - SECTIONS in finals:
-            leave(t - SECTIONS)
+        if t + 1 == periods and batches > 1:
+            leave(range(batches - 1))
         came = [[None] * CHUNKS for _ in range(group)]
         done = []
         for c in range(CHUNKS):
@@ -439,8 +438,8 @@
             finals[t - SECTIONS + 1] = done
         if t + 1 < periods:
             fed, partial = feed(t + 1, came)
-    leave(batches - 1)
-    return jnp.stack([exits[b] for b in range(batches)])
+    leave(range(batches - 1, batches))
+    return jnp.concatenate(exits)
 
 
 def solution(mesh):

time: 186 us -> 185 us (level)
  starting transfers between devices: 82.6 us -> 80.4 us
    ppermute x41 -> x35, starting transfers between devices: 82.6 us -> 80.4 us  [permute(): return lax.ppermute(value, axis, pairs)]
    ppermute x41 -> x35, waiting for transfers between devices: 70.2 us -> 71.3 us  [permute(): return lax.ppermute(value, axis, pairs)]
  transfers between devices with their start and end apart: 41 -> 35, of which waited for: 23 -> 22; matrix products, arithmetic and copies ran while one was open for 1% -> 1% of each run, Pallas kernels for 3% -> 3%
where the time goes in v3:
time: 185 us; the launch traced here: 184 us
  starting transfers between devices  80.4 us (43%)
  waiting for transfers between devices  71.3 us (39%)
  Pallas kernels  15.3 us (8%)
  local copies, waits for them, and re-layouts  12.5 us (7%)
  other arithmetic  3.91 us (2%)
    ppermute x35, starting transfers between devices, permute(): return lax.ppermute(value, axis, pairs)  80.4 us
    ppermute x35, waiting for transfers between devices, permute(): return lax.ppermute(value, axis, pairs)  71.3 us
    unnamed x16, local copies, waits for them, and re-layouts  12.4 us
    pallas_call x7, Pallas kernels, rest(): pl.pallas_call(functools.partial(rest_kernel, group, same, t, batches), o...  9.16 us
    pallas_call x7, Pallas kernels, own(): pl.pallas_call(functools.partial(own_kernel, group, same, t, batches), ou...  4.24 us
  transfers between devices with their start and end apart: 35, of which 22 were waited for; matrix products, arithmetic and copies ran while one was open for 1% of the time, Pallas kernels for 3%

profile of v3, /device:TPU:0, one launch (start us, length us, event | category | flops | bytes accessed | tf_op | source)
XLA Modules:
  0.0 184.0 jit_solution(2841171044406146854)
XLA Ops:
  0.9 6.0 %collective-permute-start.3 = (bf16[1,128,256]{2,1,0:T(8,128)(2,1)S(1)}, bf16[1,128,256]{2,1,0:T(8,128)(2,1)S(1)}, u32[]{:S(2)}, u32[]{:S(2)}) collective-permute-start(bf16[1,128,256]{2,1,0:T(8,128)(2,1)S(1)} %get-tuple-element.64), channel_id=1, source_target_pairs={{16,0},{20,4},{0,16},{4,20},{17,1},{21,5},{1,17},{5,21},{18,2},{22... | collective-permute-start | bytes 196616 | tf_op jit(solution)/shard_map/ppermute | solution.py:238
  9.5 3.5 %collective-permute-done.4 = bf16[1,128,256]{2,1,0:T(8,128)(2,1)S(1)} collective-permute-done((bf16[1,128,256]{2,1,0:T(8,128)(2,1)S(1)}, bf16[1,128,256]{2,1,0:T(8,128)(2,1)S(1)}, u32[]{:S(2)}, u32[]{:S(2)}) %collective-permute-start.4) | collective-permute-done | bytes 65568 | tf_op jit(solution)/shard_map/ppermute | solution.py:238
  13.0 3.1 %collective-permute-done.5 = bf16[1,128,256]{2,1,0:T(8,128)(2,1)S(1)} collective-permute-done((bf16[1,128,256]{2,1,0:T(8,128)(2,1)S(1)}, bf16[1,128,256]{2,1,0:T(8,128)(2,1)S(1)}, u32[]{:S(2)}, u32[]{:S(2)}) %collective-permute-start.5) | collective-permute-done | bytes 65568 | tf_op jit(solution)/shard_map/ppermute | solution.py:238
  18.7 4.6 %copy-done = bf16[1,2048,3072]{2,1,0:T(8,128)(2,1)S(1)} copy-done((bf16[1,2048,3072]{2,1,0:T(8,128)(2,1)S(1)}, bf16[1,2048,3072]{2,1,0:T(8,128)(2,1)}, u32[]{:S(2)}) %copy-start) | copy-done | bytes 12582936
  26.3 3.8 %copy-done.1 = bf16[1,2048,3072]{2,1,0:T(8,128)(2,1)S(1)} copy-done((bf16[1,2048,3072]{2,1,0:T(8,128)(2,1)S(1)}, bf16[1,2048,3072]{2,1,0:T(8,128)(2,1)}, u32[]{:S(2)}) %copy-start.1) | copy-done | bytes 12582936
  41.0 4.8 %collective-permute-start.12 = (bf16[128,1024]{1,0:T(8,128)(2,1)S(1)}, bf16[128,1024]{1,0:T(8,128)(2,1)S(1)}, u32[]{:S(2)}, u32[]{:S(2)}) collective-permute-start(bf16[128,1024]{1,0:T(8,128)(2,1)S(1)} %add_convert_fusion.6), channel_id=1, source_target_pairs={{0,8},{4,12},{8,16},{12,20},{16,24},{20,28},{1,9},{5,13},{9,17},{1... | collective-permute-start | bytes 786440 | tf_op jit(solution)/shard_map/ppermute | solution.py:238
  45.8 2.9 %collective-permute-start.11 = (bf16[128,1024]{1,0:T(8,128)(2,1)S(1)}, bf16[128,1024]{1,0:T(8,128)(2,1)S(1)}, u32[]{:S(2)}, u32[]{:S(2)}) collective-permute-start(bf16[128,1024]{1,0:T(8,128)(2,1)S(1)} %add_convert_fusion.6), channel_id=1, source_target_pairs={{0,12},{4,8},{8,20},{12,16},{16,28},{20,24},{1,13},{5,9},{9,21},{1... | collective-permute-start | bytes 786440 | tf_op jit(solution)/shard_map/ppermute | solution.py:238
  54.5 3.0 %collective-permute-done.10 = bf16[128,1024]{1,0:T(8,128)(2,1)S(1)} collective-permute-done((bf16[128,1024]{1,0:T(8,128)(2,1)S(1)}, bf16[128,1024]{1,0:T(8,128)(2,1)S(1)}, u32[]{:S(2)}, u32[]{:S(2)}) %collective-permute-start.10) | collective-permute-done | bytes 262176 | tf_op jit(solution)/shard_map/ppermute | solution.py:238
  62.1 4.1 %collective-permute-done.13 = bf16[128,1024]{1,0:T(8,128)(2,1)S(1)} collective-permute-done((bf16[128,1024]{1,0:T(8,128)(2,1)S(1)}, bf16[128,1024]{1,0:T(8,128)(2,1)S(1)}, u32[]{:S(2)}, u32[]{:S(2)}) %collective-permute-start.13) | collective-permute-done | bytes 262176 | tf_op jit(solution)/shard_map/ppermute | solution.py:238
  66.3 5.2 %collective-permute-start.15 = (bf16[128,1024]{1,0:T(8,128)(2,1)S(1)}, bf16[128,1024]{1,0:T(8,128)(2,1)S(1)}, u32[]{:S(2)}, u32[]{:S(2)}) collective-permute-start(bf16[128,1024]{1,0:T(8,128)(2,1)S(1)} %add_convert_fusion.5), channel_id=1, source_target_pairs={{0,8},{4,12},{8,16},{12,20},{16,24},{20,28},{1,9},{5,13},{9,17},{1... | collective-permute-start | bytes 786440 | tf_op jit(solution)/shard_map/ppermute | solution.py:238
  72.1 3.5 %collective-permute-start.14 = (bf16[128,1024]{1,0:T(8,128)(2,1)S(1)}, bf16[128,1024]{1,0:T(8,128)(2,1)S(1)}, u32[]{:S(2)}, u32[]{:S(2)}) collective-permute-start(bf16[128,1024]{1,0:T(8,128)(2,1)S(1)} %add_convert_fusion.5), channel_id=1, source_target_pairs={{0,12},{4,8},{8,20},{12,16},{16,28},{20,24},{1,13},{5,9},{9,21},{1... | collective-permute-start | bytes 786440 | tf_op jit(solution)/shard_map/ppermute | solution.py:238
  83.9 5.6 %collective-permute-done.16 = bf16[128,1024]{1,0:T(8,128)(2,1)S(1)} collective-permute-done((bf16[128,1024]{1,0:T(8,128)(2,1)S(1)}, bf16[128,1024]{1,0:T(8,128)(2,1)S(1)}, u32[]{:S(2)}, u32[]{:S(2)}) %collective-permute-start.16) | collective-permute-done | bytes 262176 | tf_op jit(solution)/shard_map/ppermute | solution.py:238
  89.6 4.8 %collective-permute-start.18 = (bf16[128,1024]{1,0:T(8,128)(2,1)S(1)}, bf16[128,1024]{1,0:T(8,128)(2,1)S(1)}, u32[]{:S(2)}, u32[]{:S(2)}) collective-permute-start(bf16[128,1024]{1,0:T(8,128)(2,1)S(1)} %add_convert_fusion.4), channel_id=1, source_target_pairs={{0,8},{4,12},{8,16},{12,20},{16,24},{20,28},{1,9},{5,13},{9,17},{1... | collective-permute-start | bytes 786440 | tf_op jit(solution)/shard_map/ppermute | solution.py:238
  106.2 5.2 %collective-permute-done.19 = bf16[128,1024]{1,0:T(8,128)(2,1)S(1)} collective-permute-done((bf16[128,1024]{1,0:T(8,128)(2,1)S(1)}, bf16[128,1024]{1,0:T(8,128)(2,1)S(1)}, u32[]{:S(2)}, u32[]{:S(2)}) %collective-permute-start.19) | collective-permute-done | bytes 262176 | tf_op jit(solution)/shard_map/ppermute | solution.py:238
  111.5 4.6 %collective-permute-start.21 = (bf16[128,1024]{1,0:T(8,128)(2,1)S(1)}, bf16[128,1024]{1,0:T(8,128)(2,1)S(1)}, u32[]{:S(2)}, u32[]{:S(2)}) collective-permute-start(bf16[128,1024]{1,0:T(8,128)(2,1)S(1)} %add_convert_fusion.3), channel_id=1, source_target_pairs={{0,8},{4,12},{8,16},{12,20},{16,24},{20,28},{1,9},{5,13},{9,17},{1... | collective-permute-start | bytes 786440 | tf_op jit(solution)/shard_map/ppermute | solution.py:238
  124.3 5.0 %collective-permute-done.22 = bf16[128,1024]{1,0:T(8,128)(2,1)S(1)} collective-permute-done((bf16[128,1024]{1,0:T(8,128)(2,1)S(1)}, bf16[128,1024]{1,0:T(8,128)(2,1)S(1)}, u32[]{:S(2)}, u32[]{:S(2)}) %collective-permute-start.22) | collective-permute-done | bytes 262176 | tf_op jit(solution)/shard_map/ppermute | solution.py:238
  129.4 7.5 %collective-permute-start.24 = (bf16[128,1024]{1,0:T(8,128)(2,1)S(1)}, bf16[128,1024]{1,0:T(8,128)(2,1)S(1)}, u32[]{:S(2)}, u32[]{:S(2)}) collective-permute-start(bf16[128,1024]{1,0:T(8,128)(2,1)S(1)} %add_convert_fusion.2), channel_id=1, source_target_pairs={{0,8},{4,12},{8,16},{12,20},{16,24},{20,28},{1,9},{5,13},{9,17},{1... | collective-permute-start | bytes 786440 | tf_op jit(solution)/shard_map/ppermute | solution.py:238
  144.5 5.6 %collective-permute-done.25 = bf16[128,1024]{1,0:T(8,128)(2,1)S(1)} collective-permute-done((bf16[128,1024]{1,0:T(8,128)(2,1)S(1)}, bf16[128,1024]{1,0:T(8,128)(2,1)S(1)}, u32[]{:S(2)}, u32[]{:S(2)}) %collective-permute-start.25) | collective-permute-done | bytes 262176 | tf_op jit(solution)/shard_map/ppermute | solution.py:238
  150.2 4.6 %collective-permute-start.30 = (bf16[128,1024]{1,0:T(8,128)(2,1)S(1)}, bf16[128,1024]{1,0:T(8,128)(2,1)S(1)}, u32[]{:S(2)}, u32[]{:S(2)}) collective-permute-start(bf16[128,1024]{1,0:T(8,128)(2,1)S(1)} %add_convert_fusion.1), channel_id=1, source_target_pairs={{0,8},{4,12},{8,16},{12,20},{16,24},{20,28},{1,9},{5,13},{9,17},{1... | collective-permute-start | bytes 786440 | tf_op jit(solution)/shard_map/ppermute | solution.py:238
  154.8 5.2 %collective-permute-start.29 = (bf16[128,1024]{1,0:T(8,128)(2,1)S(1)}, bf16[128,1024]{1,0:T(8,128)(2,1)S(1)}, u32[]{:S(2)}, u32[]{:S(2)}) collective-permute-start(bf16[128,1024]{1,0:T(8,128)(2,1)S(1)} %add_convert_fusion.1), channel_id=1, source_target_pairs={{0,12},{4,8},{8,20},{12,16},{16,28},{20,24},{1,13},{5,9},{9,21},{1... | collective-permute-start | bytes 786440 | tf_op jit(solution)/shard_map/ppermute | solution.py:238
  160.1 3.6 %collective-permute-done.29.refs_0_ = bf16[128,1024]{1,0:T(8,128)(2,1)S(1)} collective-permute-done((bf16[128,1024]{1,0:T(8,128)(2,1)S(1)}, bf16[128,1024]{1,0:T(8,128)(2,1)S(1)}, u32[]{:S(2)}, u32[]{:S(2)}) %collective-permute-start.29) | collective-permute-done | bytes 262176 | tf_op jit(solution)/shard_map/ppermute | solution.py:238
  167.2 2.9 %collective-permute-done.31 = bf16[128,1024]{1,0:T(8,128)(2,1)S(1)} collective-permute-done((bf16[128,1024]{1,0:T(8,128)(2,1)S(1)}, bf16[128,1024]{1,0:T(8,128)(2,1)S(1)}, u32[]{:S(2)}, u32[]{:S(2)}) %collective-permute-start.31) | collective-permute-done | bytes 262176 | tf_op jit(solution)/shard_map/ppermute | solution.py:238
  171.5 3.8 %collective-permute-done.28 = bf16[3,128,256]{2,1,0:T(8,128)(2,1)S(1)} collective-permute-done((bf16[3,128,256]{2,1,0:T(8,128)(2,1)S(1)}, bf16[3,128,256]{2,1,0:T(8,128)(2,1)S(1)}, u32[]{:S(2)}, u32[]{:S(2)}) %collective-permute-start.28) | collective-permute-done | bytes 196640 | tf_op jit(solution)/shard_map/ppermute | solution.py:238
  176.7 6.6 %collective-permute-done.34 = bf16[1,128,256]{2,1,0:T(8,128)(2,1)S(1)} collective-permute-done((bf16[1,128,256]{2,1,0:T(8,128)(2,1)S(1)}, bf16[1,128,256]{2,1,0:T(8,128)(2,1)S(1)}, u32[]{:S(2)}, u32[]{:S(2)}) %collective-permute-start.34) | collective-permute-done | bytes 65568 | tf_op jit(solution)/shard_map/ppermute | solution.py:238
  (124 shorter events, 74.0 us)
Async XLA Ops:
  0.9 8.6 %collective-permute-start.3 = (bf16[1,128,256]{2,1,0:T(8,128)(2,1)S(1)}, bf16[1,128,256]{2,1,0:T(8,128)(2,1)S(1)}, u32[]{:S(2)}, u32[]{:S(2)}) collective-permute-start(bf16[1,128,256]{2,1,0:T(8,128)(2,1)S(1)} %get-tuple-element.64), channel_id=1, source_target_pairs={{16,0},{20,4},{0,16},{4,20},{17,1},{21,5},{1,17},{5,21},{18,2},{22... | collective-permute-start | bytes 196616 | tf_op jit(solution)/shard_map/ppermute | solution.py:238
  8.2 8.0 %collective-permute-start.5 = (bf16[1,128,256]{2,1,0:T(8,128)(2,1)S(1)}, bf16[1,128,256]{2,1,0:T(8,128)(2,1)S(1)}, u32[]{:S(2)}, u32[]{:S(2)}) collective-permute-start(bf16[1,128,256]{2,1,0:T(8,128)(2,1)S(1)} %get-tuple-element.66), channel_id=1, source_target_pairs={{24,0},{28,4},{8,16},{12,20},{25,1},{29,5},{9,17},{13,21},{26,2},{... | collective-permute-start | bytes 196616 | tf_op jit(solution)/shard_map/ppermute | solution.py:238
  16.2 14.9 %collective-permute-start.6 = (bf16[128,1024]{1,0:T(8,128)(2,1)S(1)}, bf16[128,1024]{1,0:T(8,128)(2,1)S(1)}, u32[]{:S(2)}, u32[]{:S(2)}) collective-permute-start(bf16[128,1024]{1,0:T(8,128)(2,1)S(1)} %pad_maximum_fusion.refs_0_), channel_id=1, source_target_pairs={{0,4},{4,0},{8,12},{12,8},{16,20},{20,16},{24,28},{28,24},{1,5},{5... | collective-permute-start | bytes 786440 | tf_op jit(solution)/shard_map/ppermute | solution.py:238
  35.2 15.1 %collective-permute-start = (bf16[3,128,256]{2,1,0:T(8,128)(2,1)S(1)}, bf16[3,128,256]{2,1,0:T(8,128)(2,1)S(1)}, u32[]{:S(2)}, u32[]{:S(2)}) collective-permute-start(bf16[3,128,256]{2,1,0:T(8,128)(2,1)S(1)} %get-tuple-element.60), channel_id=1, source_target_pairs={{8,0},{12,4},{24,16},{28,20},{9,1},{13,5},{25,17},{29,21},{10,2},{... | collective-permute-start | bytes 589832 | tf_op jit(solution)/shard_map/ppermute | solution.py:238
  36.5 13.8 %collective-permute-start.1 = (bf16[3,128,256]{2,1,0:T(8,128)(2,1)S(1)}, bf16[3,128,256]{2,1,0:T(8,128)(2,1)S(1)}, u32[]{:S(2)}, u32[]{:S(2)}) collective-permute-start(bf16[3,128,256]{2,1,0:T(8,128)(2,1)S(1)} %get-tuple-element.61), channel_id=1, source_target_pairs={{16,0},{20,4},{0,16},{4,20},{17,1},{21,5},{1,17},{5,21},{18,2},{22... | collective-permute-start | bytes 589832 | tf_op jit(solution)/shard_map/ppermute | solution.py:238
  38.4 11.8 %collective-permute-start.2 = (bf16[3,128,256]{2,1,0:T(8,128)(2,1)S(1)}, bf16[3,128,256]{2,1,0:T(8,128)(2,1)S(1)}, u32[]{:S(2)}, u32[]{:S(2)}) collective-permute-start(bf16[3,128,256]{2,1,0:T(8,128)(2,1)S(1)} %get-tuple-element.62), channel_id=1, source_target_pairs={{24,0},{28,4},{8,16},{12,20},{25,1},{29,5},{9,17},{13,21},{26,2},{... | collective-permute-start | bytes 589832 | tf_op jit(solution)/shard_map/ppermute | solution.py:238
  41.0 10.9 %collective-permute-start.12 = (bf16[128,1024]{1,0:T(8,128)(2,1)S(1)}, bf16[128,1024]{1,0:T(8,128)(2,1)S(1)}, u32[]{:S(2)}, u32[]{:S(2)}) collective-permute-start(bf16[128,1024]{1,0:T(8,128)(2,1)S(1)} %add_convert_fusion.6), channel_id=1, source_target_pairs={{0,8},{4,12},{8,16},{12,20},{16,24},{20,28},{1,9},{5,13},{9,17},{1... | collective-permute-start | bytes 786440 | tf_op jit(solution)/shard_map/ppermute | solution.py:238
  45.8 8.7 %collective-permute-start.11 = (bf16[128,1024]{1,0:T(8,128)(2,1)S(1)}, bf16[128,1024]{1,0:T(8,128)(2,1)S(1)}, u32[]{:S(2)}, u32[]{:S(2)}) collective-permute-start(bf16[128,1024]{1,0:T(8,128)(2,1)S(1)} %add_convert_fusion.6), channel_id=1, source_target_pairs={{0,12},{4,8},{8,20},{12,16},{16,28},{20,24},{1,13},{5,9},{9,21},{1... | collective-permute-start | bytes 786440 | tf_op jit(solution)/shard_map/ppermute | solution.py:238
  50.3 7.1 %collective-permute-start.10 = (bf16[128,1024]{1,0:T(8,128)(2,1)S(1)}, bf16[128,1024]{1,0:T(8,128)(2,1)S(1)}, u32[]{:S(2)}, u32[]{:S(2)}) collective-permute-start(bf16[128,1024]{1,0:T(8,128)(2,1)S(1)} %pad_maximum_fusion.3), channel_id=1, source_target_pairs={{0,4},{4,0},{8,12},{12,8},{16,20},{20,16},{24,28},{28,24},{1,5},{5... | collective-permute-start | bytes 786440 | tf_op jit(solution)/shard_map/ppermute | solution.py:238
  66.3 11.6 %collective-permute-start.15 = (bf16[128,1024]{1,0:T(8,128)(2,1)S(1)}, bf16[128,1024]{1,0:T(8,128)(2,1)S(1)}, u32[]{:S(2)}, u32[]{:S(2)}) collective-permute-start(bf16[128,1024]{1,0:T(8,128)(2,1)S(1)} %add_convert_fusion.5), channel_id=1, source_target_pairs={{0,8},{4,12},{8,16},{12,20},{16,24},{20,28},{1,9},{5,13},{9,17},{1... | collective-permute-start | bytes 786440 | tf_op jit(solution)/shard_map/ppermute | solution.py:238
  71.6 9.2 %collective-permute-start.9 = (bf16[128,1024]{1,0:T(8,128)(2,1)S(1)}, bf16[128,1024]{1,0:T(8,128)(2,1)S(1)}, u32[]{:S(2)}, u32[]{:S(2)}) collective-permute-start(bf16[128,1024]{1,0:T(8,128)(2,1)S(1)} %pad_maximum_fusion.2), channel_id=1, source_target_pairs={{0,4},{4,0},{8,12},{12,8},{16,20},{20,16},{24,28},{28,24},{1,5},{5... | collective-permute-start | bytes 786440 | tf_op jit(solution)/shard_map/ppermute | solution.py:238
  72.1 8.7 %collective-permute-start.14 = (bf16[128,1024]{1,0:T(8,128)(2,1)S(1)}, bf16[128,1024]{1,0:T(8,128)(2,1)S(1)}, u32[]{:S(2)}, u32[]{:S(2)}) collective-permute-start(bf16[128,1024]{1,0:T(8,128)(2,1)S(1)} %add_convert_fusion.5), channel_id=1, source_target_pairs={{0,12},{4,8},{8,20},{12,16},{16,28},{20,24},{1,13},{5,9},{9,21},{1... | collective-permute-start | bytes 786440 | tf_op jit(solution)/shard_map/ppermute | solution.py:238
  89.6 9.2 %collective-permute-start.18 = (bf16[128,1024]{1,0:T(8,128)(2,1)S(1)}, bf16[128,1024]{1,0:T(8,128)(2,1)S(1)}, u32[]{:S(2)}, u32[]{:S(2)}) collective-permute-start(bf16[128,1024]{1,0:T(8,128)(2,1)S(1)} %add_convert_fusion.4), channel_id=1, source_target_pairs={{0,8},{4,12},{8,16},{12,20},{16,24},{20,28},{1,9},{5,13},{9,17},{1... | collective-permute-start | bytes 786440 | tf_op jit(solution)/shard_map/ppermute | solution.py:238
  94.4 8.3 %collective-permute-start.8 = (bf16[128,1024]{1,0:T(8,128)(2,1)S(1)}, bf16[128,1024]{1,0:T(8,128)(2,1)S(1)}, u32[]{:S(2)}, u32[]{:S(2)}) collective-permute-start(bf16[128,1024]{1,0:T(8,128)(2,1)S(1)} %pad_maximum_fusion.1), channel_id=1, source_target_pairs={{0,4},{4,0},{8,12},{12,8},{16,20},{20,16},{24,28},{28,24},{1,5},{5... | collective-permute-start | bytes 786440 | tf_op jit(solution)/shard_map/ppermute | solution.py:238
  111.5 8.4 %collective-permute-start.21 = (bf16[128,1024]{1,0:T(8,128)(2,1)S(1)}, bf16[128,1024]{1,0:T(8,128)(2,1)S(1)}, u32[]{:S(2)}, u32[]{:S(2)}) collective-permute-start(bf16[128,1024]{1,0:T(8,128)(2,1)S(1)} %add_convert_fusion.3), channel_id=1, source_target_pairs={{0,8},{4,12},{8,16},{12,20},{16,24},{20,28},{1,9},{5,13},{9,17},{1... | collective-permute-start | bytes 786440 | tf_op jit(solution)/shard_map/ppermute | solution.py:238
  116.1 6.7 %collective-permute-start.20 = (bf16[128,1024]{1,0:T(8,128)(2,1)S(1)}, bf16[128,1024]{1,0:T(8,128)(2,1)S(1)}, u32[]{:S(2)}, u32[]{:S(2)}) collective-permute-start(bf16[128,1024]{1,0:T(8,128)(2,1)S(1)} %add_convert_fusion.3), channel_id=1, source_target_pairs={{0,12},{4,8},{8,20},{12,16},{16,28},{20,24},{1,13},{5,9},{9,21},{1... | collective-permute-start | bytes 786440 | tf_op jit(solution)/shard_map/ppermute | solution.py:238
  129.4 11.4 %collective-permute-start.24 = (bf16[128,1024]{1,0:T(8,128)(2,1)S(1)}, bf16[128,1024]{1,0:T(8,128)(2,1)S(1)}, u32[]{:S(2)}, u32[]{:S(2)}) collective-permute-start(bf16[128,1024]{1,0:T(8,128)(2,1)S(1)} %add_convert_fusion.2), channel_id=1, source_target_pairs={{0,8},{4,12},{8,16},{12,20},{16,24},{20,28},{1,9},{5,13},{9,17},{1... | collective-permute-start | bytes 786440 | tf_op jit(solution)/shard_map/ppermute | solution.py:238
  136.9 6.7 %collective-permute-start.23 = (bf16[128,1024]{1,0:T(8,128)(2,1)S(1)}, bf16[128,1024]{1,0:T(8,128)(2,1)S(1)}, u32[]{:S(2)}, u32[]{:S(2)}) collective-permute-start(bf16[128,1024]{1,0:T(8,128)(2,1)S(1)} %add_convert_fusion.2), channel_id=1, source_target_pairs={{0,12},{4,8},{8,20},{12,16},{16,28},{20,24},{1,13},{5,9},{9,21},{1... | collective-permute-start | bytes 786440 | tf_op jit(solution)/shard_map/ppermute | solution.py:238
  150.2 9.8 %collective-permute-start.30 = (bf16[128,1024]{1,0:T(8,128)(2,1)S(1)}, bf16[128,1024]{1,0:T(8,128)(2,1)S(1)}, u32[]{:S(2)}, u32[]{:S(2)}) collective-permute-start(bf16[128,1024]{1,0:T(8,128)(2,1)S(1)} %add_convert_fusion.1), channel_id=1, source_target_pairs={{0,8},{4,12},{8,16},{12,20},{16,24},{20,28},{1,9},{5,13},{9,17},{1... | collective-permute-start | bytes 786440 | tf_op jit(solution)/shard_map/ppermute | solution.py:238
  154.8 8.9 %collective-permute-start.29 = (bf16[128,1024]{1,0:T(8,128)(2,1)S(1)}, bf16[128,1024]{1,0:T(8,128)(2,1)S(1)}, u32[]{:S(2)}, u32[]{:S(2)}) collective-permute-start(bf16[128,1024]{1,0:T(8,128)(2,1)S(1)} %add_convert_fusion.1), channel_id=1, source_target_pairs={{0,12},{4,8},{8,20},{12,16},{16,28},{20,24},{1,13},{5,9},{9,21},{1... | collective-permute-start | bytes 786440 | tf_op jit(solution)/shard_map/ppermute | solution.py:238
  164.4 10.9 %collective-permute-start.28 = (bf16[3,128,256]{2,1,0:T(8,128)(2,1)S(1)}, bf16[3,128,256]{2,1,0:T(8,128)(2,1)S(1)}, u32[]{:S(2)}, u32[]{:S(2)}) collective-permute-start(bf16[3,128,256]{2,1,0:T(8,128)(2,1)S(1)} %pad_maximum_fusion.7), channel_id=1, source_target_pairs={{24,0},{28,4},{25,1},{29,5},{26,2},{30,6},{27,3},{31,7}} | collective-permute-start | bytes 589832 | tf_op jit(solution)/shard_map/ppermute | solution.py:238
  165.8 10.9 %collective-permute-start.27 = (bf16[3,128,256]{2,1,0:T(8,128)(2,1)S(1)}, bf16[3,128,256]{2,1,0:T(8,128)(2,1)S(1)}, u32[]{:S(2)}, u32[]{:S(2)}) collective-permute-start(bf16[3,128,256]{2,1,0:T(8,128)(2,1)S(1)} %pad_maximum_fusion.6), channel_id=1, source_target_pairs={{24,8},{28,12},{25,9},{29,13},{26,10},{30,14},{27,11},{31,15}} | collective-permute-start | bytes 589832 | tf_op jit(solution)/shard_map/ppermute | solution.py:238
  166.5 10.2 %collective-permute-start.26 = (bf16[3,128,256]{2,1,0:T(8,128)(2,1)S(1)}, bf16[3,128,256]{2,1,0:T(8,128)(2,1)S(1)}, u32[]{:S(2)}, u32[]{:S(2)}) collective-permute-start(bf16[3,128,256]{2,1,0:T(8,128)(2,1)S(1)} %pad_maximum_fusion.5), channel_id=1, source_target_pairs={{24,16},{28,20},{25,17},{29,21},{26,18},{30,22},{27,19},{31,23}} | collective-permute-start | bytes 589832 | tf_op jit(solution)/shard_map/ppermute | solution.py:238
  175.4 7.9 %collective-permute-start.34 = (bf16[1,128,256]{2,1,0:T(8,128)(2,1)S(1)}, bf16[1,128,256]{2,1,0:T(8,128)(2,1)S(1)}, u32[]{:S(2)}, u32[]{:S(2)}) collective-permute-start(bf16[1,128,256]{2,1,0:T(8,128)(2,1)S(1)} %get-tuple-element.147), channel_id=1, source_target_pairs={{24,0},{28,4},{25,1},{29,5},{26,2},{30,6},{27,3},{31,7}} | collective-permute-start | bytes 196616 | tf_op jit(solution)/shard_map/ppermute | solution.py:238
  (19 other events, 90.8 us)

commit v4 on v3

--- a/solution.py
+++ b/solution.py
@@ -198,17 +198,17 @@
     w_in = pltpu.with_memory_space_constraint(w_in, pltpu.VMEM)
     w_out = pltpu.with_memory_space_constraint(w_out, pltpu.VMEM)
 
-    def touch(a_ref, b_ref, out):
+    def touch(a_ref, out):
         out[...] = jnp.zeros_like(out)
 
     token = pl.pallas_call(
         touch,
         out_shape=jax.ShapeDtypeStruct((8, 128), f32),
-        in_specs=[VMEM, VMEM],
+        in_specs=[VMEM],
         out_specs=VMEM,
         compiler_params=params(1 << 20),
         name="touch",
-    )(w_in, w_out)
+    )(w_in)
     return w_in, w_out, token
 
 

time: 185 us -> 183 us (0.989)
  local copies, waits for them, and re-layouts: 12.5 us -> 10.3 us
    unnamed x16 -> x14, local copies, waits for them, and re-layouts: 12.4 us -> 10.2 us
where the time goes in v4:
time: 183 us; the launch traced here: 182 us
  starting transfers between devices  80.4 us (44%)
  waiting for transfers between devices  71.2 us (39%)
  Pallas kernels  15.4 us (8%)
  local copies, waits for them, and re-layouts  10.3 us (6%)
  other arithmetic  3.92 us (2%)
    ppermute x35, starting transfers between devices, permute(): return lax.ppermute(value, axis, pairs)  80.4 us
    ppermute x35, waiting for transfers between devices, permute(): return lax.ppermute(value, axis, pairs)  71.2 us
    unnamed x14, local copies, waits for them, and re-layouts  10.2 us
    pallas_call x7, Pallas kernels, rest(): pl.pallas_call(functools.partial(rest_kernel, group, same, t, batches), o...  9.17 us
    pallas_call x7, Pallas kernels, own(): pl.pallas_call(functools.partial(own_kernel, group, same, t, batches), ou...  4.25 us
  transfers between devices with their start and end apart: 35, of which 22 were waited for; matrix products, arithmetic and copies ran while one was open for 1% of the time, Pallas kernels for 3%

profile of v4, /device:TPU:0, one launch (start us, length us, event | category | flops | bytes accessed | tf_op | source)
XLA Modules:
  0.0 181.9 jit_solution(9772800470065855254)
XLA Ops:
  0.9 6.0 %collective-permute-start.3 = (bf16[1,128,256]{2,1,0:T(8,128)(2,1)S(1)}, bf16[1,128,256]{2,1,0:T(8,128)(2,1)S(1)}, u32[]{:S(2)}, u32[]{:S(2)}) collective-permute-start(bf16[1,128,256]{2,1,0:T(8,128)(2,1)S(1)} %get-tuple-element.64), channel_id=1, source_target_pairs={{16,0},{20,4},{0,16},{4,20},{17,1},{21,5},{1,17},{5,21},{18,2},{22... | collective-permute-start | bytes 196616 | tf_op jit(solution)/shard_map/ppermute | solution.py:238
  9.5 3.5 %collective-permute-done.4 = bf16[1,128,256]{2,1,0:T(8,128)(2,1)S(1)} collective-permute-done((bf16[1,128,256]{2,1,0:T(8,128)(2,1)S(1)}, bf16[1,128,256]{2,1,0:T(8,128)(2,1)S(1)}, u32[]{:S(2)}, u32[]{:S(2)}) %collective-permute-start.4) | collective-permute-done | bytes 65568 | tf_op jit(solution)/shard_map/ppermute | solution.py:238
  13.0 3.1 %collective-permute-done.5 = bf16[1,128,256]{2,1,0:T(8,128)(2,1)S(1)} collective-permute-done((bf16[1,128,256]{2,1,0:T(8,128)(2,1)S(1)}, bf16[1,128,256]{2,1,0:T(8,128)(2,1)S(1)}, u32[]{:S(2)}, u32[]{:S(2)}) %collective-permute-start.5) | collective-permute-done | bytes 65568 | tf_op jit(solution)/shard_map/ppermute | solution.py:238
  18.7 4.6 %copy-done = bf16[1,2048,3072]{2,1,0:T(8,128)(2,1)S(1)} copy-done((bf16[1,2048,3072]{2,1,0:T(8,128)(2,1)S(1)}, bf16[1,2048,3072]{2,1,0:T(8,128)(2,1)}, u32[]{:S(2)}) %copy-start) | copy-done | bytes 12582936
  24.1 3.8 %copy-done.1 = bf16[1,2048,3072]{2,1,0:T(8,128)(2,1)S(1)} copy-done((bf16[1,2048,3072]{2,1,0:T(8,128)(2,1)S(1)}, bf16[1,2048,3072]{2,1,0:T(8,128)(2,1)}, u32[]{:S(2)}) %copy-start.1) | copy-done | bytes 12582936
  38.8 4.8 %collective-permute-start.12 = (bf16[128,1024]{1,0:T(8,128)(2,1)S(1)}, bf16[128,1024]{1,0:T(8,128)(2,1)S(1)}, u32[]{:S(2)}, u32[]{:S(2)}) collective-permute-start(bf16[128,1024]{1,0:T(8,128)(2,1)S(1)} %add_convert_fusion.6), channel_id=1, source_target_pairs={{0,8},{4,12},{8,16},{12,20},{16,24},{20,28},{1,9},{5,13},{9,17},{1... | collective-permute-start | bytes 786440 | tf_op jit(solution)/shard_map/ppermute | solution.py:238
  43.7 2.9 %collective-permute-start.11 = (bf16[128,1024]{1,0:T(8,128)(2,1)S(1)}, bf16[128,1024]{1,0:T(8,128)(2,1)S(1)}, u32[]{:S(2)}, u32[]{:S(2)}) collective-permute-start(bf16[128,1024]{1,0:T(8,128)(2,1)S(1)} %add_convert_fusion.6), channel_id=1, source_target_pairs={{0,12},{4,8},{8,20},{12,16},{16,28},{20,24},{1,13},{5,9},{9,21},{1... | collective-permute-start | bytes 786440 | tf_op jit(solution)/shard_map/ppermute | solution.py:238
  52.3 2.9 %collective-permute-done.10 = bf16[128,1024]{1,0:T(8,128)(2,1)S(1)} collective-permute-done((bf16[128,1024]{1,0:T(8,128)(2,1)S(1)}, bf16[128,1024]{1,0:T(8,128)(2,1)S(1)}, u32[]{:S(2)}, u32[]{:S(2)}) %collective-permute-start.10) | collective-permute-done | bytes 262176 | tf_op jit(solution)/shard_map/ppermute | solution.py:238
  59.9 4.1 %collective-permute-done.13 = bf16[128,1024]{1,0:T(8,128)(2,1)S(1)} collective-permute-done((bf16[128,1024]{1,0:T(8,128)(2,1)S(1)}, bf16[128,1024]{1,0:T(8,128)(2,1)S(1)}, u32[]{:S(2)}, u32[]{:S(2)}) %collective-permute-start.13) | collective-permute-done | bytes 262176 | tf_op jit(solution)/shard_map/ppermute | solution.py:238
  64.1 5.3 %collective-permute-start.15 = (bf16[128,1024]{1,0:T(8,128)(2,1)S(1)}, bf16[128,1024]{1,0:T(8,128)(2,1)S(1)}, u32[]{:S(2)}, u32[]{:S(2)}) collective-permute-start(bf16[128,1024]{1,0:T(8,128)(2,1)S(1)} %add_convert_fusion.5), channel_id=1, source_target_pairs={{0,8},{4,12},{8,16},{12,20},{16,24},{20,28},{1,9},{5,13},{9,17},{1... | collective-permute-start | bytes 786440 | tf_op jit(solution)/shard_map/ppermute | solution.py:238
  69.9 3.5 %collective-permute-start.14 = (bf16[128,1024]{1,0:T(8,128)(2,1)S(1)}, bf16[128,1024]{1,0:T(8,128)(2,1)S(1)}, u32[]{:S(2)}, u32[]{:S(2)}) collective-permute-start(bf16[128,1024]{1,0:T(8,128)(2,1)S(1)} %add_convert_fusion.5), channel_id=1, source_target_pairs={{0,12},{4,8},{8,20},{12,16},{16,28},{20,24},{1,13},{5,9},{9,21},{1... | collective-permute-start | bytes 786440 | tf_op jit(solution)/shard_map/ppermute | solution.py:238
  81.8 5.6 %collective-permute-done.16 = bf16[128,1024]{1,0:T(8,128)(2,1)S(1)} collective-permute-done((bf16[128,1024]{1,0:T(8,128)(2,1)S(1)}, bf16[128,1024]{1,0:T(8,128)(2,1)S(1)}, u32[]{:S(2)}, u32[]{:S(2)}) %collective-permute-start.16) | collective-permute-done | bytes 262176 | tf_op jit(solution)/shard_map/ppermute | solution.py:238
  87.4 4.7 %collective-permute-start.18 = (bf16[128,1024]{1,0:T(8,128)(2,1)S(1)}, bf16[128,1024]{1,0:T(8,128)(2,1)S(1)}, u32[]{:S(2)}, u32[]{:S(2)}) collective-permute-start(bf16[128,1024]{1,0:T(8,128)(2,1)S(1)} %add_convert_fusion.4), channel_id=1, source_target_pairs={{0,8},{4,12},{8,16},{12,20},{16,24},{20,28},{1,9},{5,13},{9,17},{1... | collective-permute-start | bytes 786440 | tf_op jit(solution)/shard_map/ppermute | solution.py:238
  104.0 5.2 %collective-permute-done.19 = bf16[128,1024]{1,0:T(8,128)(2,1)S(1)} collective-permute-done((bf16[128,1024]{1,0:T(8,128)(2,1)S(1)}, bf16[128,1024]{1,0:T(8,128)(2,1)S(1)}, u32[]{:S(2)}, u32[]{:S(2)}) %collective-permute-start.19) | collective-permute-done | bytes 262176 | tf_op jit(solution)/shard_map/ppermute | solution.py:238
  109.3 4.6 %collective-permute-start.21 = (bf16[128,1024]{1,0:T(8,128)(2,1)S(1)}, bf16[128,1024]{1,0:T(8,128)(2,1)S(1)}, u32[]{:S(2)}, u32[]{:S(2)}) collective-permute-start(bf16[128,1024]{1,0:T(8,128)(2,1)S(1)} %add_convert_fusion.3), channel_id=1, source_target_pairs={{0,8},{4,12},{8,16},{12,20},{16,24},{20,28},{1,9},{5,13},{9,17},{1... | collective-permute-start | bytes 786440 | tf_op jit(solution)/shard_map/ppermute | solution.py:238
  122.1 5.0 %collective-permute-done.22 = bf16[128,1024]{1,0:T(8,128)(2,1)S(1)} collective-permute-done((bf16[128,1024]{1,0:T(8,128)(2,1)S(1)}, bf16[128,1024]{1,0:T(8,128)(2,1)S(1)}, u32[]{:S(2)}, u32[]{:S(2)}) %collective-permute-start.22) | collective-permute-done | bytes 262176 | tf_op jit(solution)/shard_map/ppermute | solution.py:238
  127.2 7.5 %collective-permute-start.24 = (bf16[128,1024]{1,0:T(8,128)(2,1)S(1)}, bf16[128,1024]{1,0:T(8,128)(2,1)S(1)}, u32[]{:S(2)}, u32[]{:S(2)}) collective-permute-start(bf16[128,1024]{1,0:T(8,128)(2,1)S(1)} %add_convert_fusion.2), channel_id=1, source_target_pairs={{0,8},{4,12},{8,16},{12,20},{16,24},{20,28},{1,9},{5,13},{9,17},{1... | collective-permute-start | bytes 786440 | tf_op jit(solution)/shard_map/ppermute | solution.py:238
  142.3 5.6 %collective-permute-done.25 = bf16[128,1024]{1,0:T(8,128)(2,1)S(1)} collective-permute-done((bf16[128,1024]{1,0:T(8,128)(2,1)S(1)}, bf16[128,1024]{1,0:T(8,128)(2,1)S(1)}, u32[]{:S(2)}, u32[]{:S(2)}) %collective-permute-start.25) | collective-permute-done | bytes 262176 | tf_op jit(solution)/shard_map/ppermute | solution.py:238
  148.0 4.6 %collective-permute-start.30 = (bf16[128,1024]{1,0:T(8,128)(2,1)S(1)}, bf16[128,1024]{1,0:T(8,128)(2,1)S(1)}, u32[]{:S(2)}, u32[]{:S(2)}) collective-permute-start(bf16[128,1024]{1,0:T(8,128)(2,1)S(1)} %add_convert_fusion.1), channel_id=1, source_target_pairs={{0,8},{4,12},{8,16},{12,20},{16,24},{20,28},{1,9},{5,13},{9,17},{1... | collective-permute-start | bytes 786440 | tf_op jit(solution)/shard_map/ppermute | solution.py:238
  152.6 5.2 %collective-permute-start.29 = (bf16[128,1024]{1,0:T(8,128)(2,1)S(1)}, bf16[128,1024]{1,0:T(8,128)(2,1)S(1)}, u32[]{:S(2)}, u32[]{:S(2)}) collective-permute-start(bf16[128,1024]{1,0:T(8,128)(2,1)S(1)} %add_convert_fusion.1), channel_id=1, source_target_pairs={{0,12},{4,8},{8,20},{12,16},{16,28},{20,24},{1,13},{5,9},{9,21},{1... | collective-permute-start | bytes 786440 | tf_op jit(solution)/shard_map/ppermute | solution.py:238
  157.9 3.6 %collective-permute-done.29.refs_0_ = bf16[128,1024]{1,0:T(8,128)(2,1)S(1)} collective-permute-done((bf16[128,1024]{1,0:T(8,128)(2,1)S(1)}, bf16[128,1024]{1,0:T(8,128)(2,1)S(1)}, u32[]{:S(2)}, u32[]{:S(2)}) %collective-permute-start.29) | collective-permute-done | bytes 262176 | tf_op jit(solution)/shard_map/ppermute | solution.py:238
  165.0 2.9 %collective-permute-done.31 = bf16[128,1024]{1,0:T(8,128)(2,1)S(1)} collective-permute-done((bf16[128,1024]{1,0:T(8,128)(2,1)S(1)}, bf16[128,1024]{1,0:T(8,128)(2,1)S(1)}, u32[]{:S(2)}, u32[]{:S(2)}) %collective-permute-start.31) | collective-permute-done | bytes 262176 | tf_op jit(solution)/shard_map/ppermute | solution.py:238
  169.3 3.8 %collective-permute-done.28 = bf16[3,128,256]{2,1,0:T(8,128)(2,1)S(1)} collective-permute-done((bf16[3,128,256]{2,1,0:T(8,128)(2,1)S(1)}, bf16[3,128,256]{2,1,0:T(8,128)(2,1)S(1)}, u32[]{:S(2)}, u32[]{:S(2)}) %collective-permute-start.28) | collective-permute-done | bytes 196640 | tf_op jit(solution)/shard_map/ppermute | solution.py:238
  174.5 6.5 %collective-permute-done.34 = bf16[1,128,256]{2,1,0:T(8,128)(2,1)S(1)} collective-permute-done((bf16[1,128,256]{2,1,0:T(8,128)(2,1)S(1)}, bf16[1,128,256]{2,1,0:T(8,128)(2,1)S(1)}, u32[]{:S(2)}, u32[]{:S(2)}) %collective-permute-start.34) | collective-permute-done | bytes 65568 | tf_op jit(solution)/shard_map/ppermute | solution.py:238
  (122 shorter events, 71.8 us)
Async XLA Ops:
  0.9 8.6 %collective-permute-start.3 = (bf16[1,128,256]{2,1,0:T(8,128)(2,1)S(1)}, bf16[1,128,256]{2,1,0:T(8,128)(2,1)S(1)}, u32[]{:S(2)}, u32[]{:S(2)}) collective-permute-start(bf16[1,128,256]{2,1,0:T(8,128)(2,1)S(1)} %get-tuple-element.64), channel_id=1, source_target_pairs={{16,0},{20,4},{0,16},{4,20},{17,1},{21,5},{1,17},{5,21},{18,2},{22... | collective-permute-start | bytes 196616 | tf_op jit(solution)/shard_map/ppermute | solution.py:238
  8.2 8.0 %collective-permute-start.5 = (bf16[1,128,256]{2,1,0:T(8,128)(2,1)S(1)}, bf16[1,128,256]{2,1,0:T(8,128)(2,1)S(1)}, u32[]{:S(2)}, u32[]{:S(2)}) collective-permute-start(bf16[1,128,256]{2,1,0:T(8,128)(2,1)S(1)} %get-tuple-element.66), channel_id=1, source_target_pairs={{24,0},{28,4},{8,16},{12,20},{25,1},{29,5},{9,17},{13,21},{26,2},{... | collective-permute-start | bytes 196616 | tf_op jit(solution)/shard_map/ppermute | solution.py:238
  16.2 12.7 %collective-permute-start.6 = (bf16[128,1024]{1,0:T(8,128)(2,1)S(1)}, bf16[128,1024]{1,0:T(8,128)(2,1)S(1)}, u32[]{:S(2)}, u32[]{:S(2)}) collective-permute-start(bf16[128,1024]{1,0:T(8,128)(2,1)S(1)} %pad_maximum_fusion.refs_0_), channel_id=1, source_target_pairs={{0,4},{4,0},{8,12},{12,8},{16,20},{20,16},{24,28},{28,24},{1,5},{5... | collective-permute-start | bytes 786440 | tf_op jit(solution)/shard_map/ppermute | solution.py:238
  33.0 15.1 %collective-permute-start = (bf16[3,128,256]{2,1,0:T(8,128)(2,1)S(1)}, bf16[3,128,256]{2,1,0:T(8,128)(2,1)S(1)}, u32[]{:S(2)}, u32[]{:S(2)}) collective-permute-start(bf16[3,128,256]{2,1,0:T(8,128)(2,1)S(1)} %get-tuple-element.60), channel_id=1, source_target_pairs={{8,0},{12,4},{24,16},{28,20},{9,1},{13,5},{25,17},{29,21},{10,2},{... | collective-permute-start | bytes 589832 | tf_op jit(solution)/shard_map/ppermute | solution.py:238
  34.3 13.8 %collective-permute-start.1 = (bf16[3,128,256]{2,1,0:T(8,128)(2,1)S(1)}, bf16[3,128,256]{2,1,0:T(8,128)(2,1)S(1)}, u32[]{:S(2)}, u32[]{:S(2)}) collective-permute-start(bf16[3,128,256]{2,1,0:T(8,128)(2,1)S(1)} %get-tuple-element.61), channel_id=1, source_target_pairs={{16,0},{20,4},{0,16},{4,20},{17,1},{21,5},{1,17},{5,21},{18,2},{22... | collective-permute-start | bytes 589832 | tf_op jit(solution)/shard_map/ppermute | solution.py:238
  36.2 11.8 %collective-permute-start.2 = (bf16[3,128,256]{2,1,0:T(8,128)(2,1)S(1)}, bf16[3,128,256]{2,1,0:T(8,128)(2,1)S(1)}, u32[]{:S(2)}, u32[]{:S(2)}) collective-permute-start(bf16[3,128,256]{2,1,0:T(8,128)(2,1)S(1)} %get-tuple-element.62), channel_id=1, source_target_pairs={{24,0},{28,4},{8,16},{12,20},{25,1},{29,5},{9,17},{13,21},{26,2},{... | collective-permute-start | bytes 589832 | tf_op jit(solution)/shard_map/ppermute | solution.py:238
  38.8 10.9 %collective-permute-start.12 = (bf16[128,1024]{1,0:T(8,128)(2,1)S(1)}, bf16[128,1024]{1,0:T(8,128)(2,1)S(1)}, u32[]{:S(2)}, u32[]{:S(2)}) collective-permute-start(bf16[128,1024]{1,0:T(8,128)(2,1)S(1)} %add_convert_fusion.6), channel_id=1, source_target_pairs={{0,8},{4,12},{8,16},{12,20},{16,24},{20,28},{1,9},{5,13},{9,17},{1... | collective-permute-start | bytes 786440 | tf_op jit(solution)/shard_map/ppermute | solution.py:238
  43.7 8.7 %collective-permute-start.11 = (bf16[128,1024]{1,0:T(8,128)(2,1)S(1)}, bf16[128,1024]{1,0:T(8,128)(2,1)S(1)}, u32[]{:S(2)}, u32[]{:S(2)}) collective-permute-start(bf16[128,1024]{1,0:T(8,128)(2,1)S(1)} %add_convert_fusion.6), channel_id=1, source_target_pairs={{0,12},{4,8},{8,20},{12,16},{16,28},{20,24},{1,13},{5,9},{9,21},{1... | collective-permute-start | bytes 786440 | tf_op jit(solution)/shard_map/ppermute | solution.py:238
  48.2 7.1 %collective-permute-start.10 = (bf16[128,1024]{1,0:T(8,128)(2,1)S(1)}, bf16[128,1024]{1,0:T(8,128)(2,1)S(1)}, u32[]{:S(2)}, u32[]{:S(2)}) collective-permute-start(bf16[128,1024]{1,0:T(8,128)(2,1)S(1)} %pad_maximum_fusion.3), channel_id=1, source_target_pairs={{0,4},{4,0},{8,12},{12,8},{16,20},{20,16},{24,28},{28,24},{1,5},{5... | collective-permute-start | bytes 786440 | tf_op jit(solution)/shard_map/ppermute | solution.py:238
  64.1 11.6 %collective-permute-start.15 = (bf16[128,1024]{1,0:T(8,128)(2,1)S(1)}, bf16[128,1024]{1,0:T(8,128)(2,1)S(1)}, u32[]{:S(2)}, u32[]{:S(2)}) collective-permute-start(bf16[128,1024]{1,0:T(8,128)(2,1)S(1)} %add_convert_fusion.5), channel_id=1, source_target_pairs={{0,8},{4,12},{8,16},{12,20},{16,24},{20,28},{1,9},{5,13},{9,17},{1... | collective-permute-start | bytes 786440 | tf_op jit(solution)/shard_map/ppermute | solution.py:238
  69.4 9.2 %collective-permute-start.9 = (bf16[128,1024]{1,0:T(8,128)(2,1)S(1)}, bf16[128,1024]{1,0:T(8,128)(2,1)S(1)}, u32[]{:S(2)}, u32[]{:S(2)}) collective-permute-start(bf16[128,1024]{1,0:T(8,128)(2,1)S(1)} %pad_maximum_fusion.2), channel_id=1, source_target_pairs={{0,4},{4,0},{8,12},{12,8},{16,20},{20,16},{24,28},{28,24},{1,5},{5... | collective-permute-start | bytes 786440 | tf_op jit(solution)/shard_map/ppermute | solution.py:238
  69.9 8.7 %collective-permute-start.14 = (bf16[128,1024]{1,0:T(8,128)(2,1)S(1)}, bf16[128,1024]{1,0:T(8,128)(2,1)S(1)}, u32[]{:S(2)}, u32[]{:S(2)}) collective-permute-start(bf16[128,1024]{1,0:T(8,128)(2,1)S(1)} %add_convert_fusion.5), channel_id=1, source_target_pairs={{0,12},{4,8},{8,20},{12,16},{16,28},{20,24},{1,13},{5,9},{9,21},{1... | collective-permute-start | bytes 786440 | tf_op jit(solution)/shard_map/ppermute | solution.py:238
  87.4 9.1 %collective-permute-start.18 = (bf16[128,1024]{1,0:T(8,128)(2,1)S(1)}, bf16[128,1024]{1,0:T(8,128)(2,1)S(1)}, u32[]{:S(2)}, u32[]{:S(2)}) collective-permute-start(bf16[128,1024]{1,0:T(8,128)(2,1)S(1)} %add_convert_fusion.4), channel_id=1, source_target_pairs={{0,8},{4,12},{8,16},{12,20},{16,24},{20,28},{1,9},{5,13},{9,17},{1... | collective-permute-start | bytes 786440 | tf_op jit(solution)/shard_map/ppermute | solution.py:238
  92.2 8.3 %collective-permute-start.8 = (bf16[128,1024]{1,0:T(8,128)(2,1)S(1)}, bf16[128,1024]{1,0:T(8,128)(2,1)S(1)}, u32[]{:S(2)}, u32[]{:S(2)}) collective-permute-start(bf16[128,1024]{1,0:T(8,128)(2,1)S(1)} %pad_maximum_fusion.1), channel_id=1, source_target_pairs={{0,4},{4,0},{8,12},{12,8},{16,20},{20,16},{24,28},{28,24},{1,5},{5... | collective-permute-start | bytes 786440 | tf_op jit(solution)/shard_map/ppermute | solution.py:238
  109.3 8.4 %collective-permute-start.21 = (bf16[128,1024]{1,0:T(8,128)(2,1)S(1)}, bf16[128,1024]{1,0:T(8,128)(2,1)S(1)}, u32[]{:S(2)}, u32[]{:S(2)}) collective-permute-start(bf16[128,1024]{1,0:T(8,128)(2,1)S(1)} %add_convert_fusion.3), channel_id=1, source_target_pairs={{0,8},{4,12},{8,16},{12,20},{16,24},{20,28},{1,9},{5,13},{9,17},{1... | collective-permute-start | bytes 786440 | tf_op jit(solution)/shard_map/ppermute | solution.py:238
  113.9 6.7 %collective-permute-start.20 = (bf16[128,1024]{1,0:T(8,128)(2,1)S(1)}, bf16[128,1024]{1,0:T(8,128)(2,1)S(1)}, u32[]{:S(2)}, u32[]{:S(2)}) collective-permute-start(bf16[128,1024]{1,0:T(8,128)(2,1)S(1)} %add_convert_fusion.3), channel_id=1, source_target_pairs={{0,12},{4,8},{8,20},{12,16},{16,28},{20,24},{1,13},{5,9},{9,21},{1... | collective-permute-start | bytes 786440 | tf_op jit(solution)/shard_map/ppermute | solution.py:238
  127.2 11.4 %collective-permute-start.24 = (bf16[128,1024]{1,0:T(8,128)(2,1)S(1)}, bf16[128,1024]{1,0:T(8,128)(2,1)S(1)}, u32[]{:S(2)}, u32[]{:S(2)}) collective-permute-start(bf16[128,1024]{1,0:T(8,128)(2,1)S(1)} %add_convert_fusion.2), channel_id=1, source_target_pairs={{0,8},{4,12},{8,16},{12,20},{16,24},{20,28},{1,9},{5,13},{9,17},{1... | collective-permute-start | bytes 786440 | tf_op jit(solution)/shard_map/ppermute | solution.py:238
  134.7 6.7 %collective-permute-start.23 = (bf16[128,1024]{1,0:T(8,128)(2,1)S(1)}, bf16[128,1024]{1,0:T(8,128)(2,1)S(1)}, u32[]{:S(2)}, u32[]{:S(2)}) collective-permute-start(bf16[128,1024]{1,0:T(8,128)(2,1)S(1)} %add_convert_fusion.2), channel_id=1, source_target_pairs={{0,12},{4,8},{8,20},{12,16},{16,28},{20,24},{1,13},{5,9},{9,21},{1... | collective-permute-start | bytes 786440 | tf_op jit(solution)/shard_map/ppermute | solution.py:238
  148.0 9.8 %collective-permute-start.30 = (bf16[128,1024]{1,0:T(8,128)(2,1)S(1)}, bf16[128,1024]{1,0:T(8,128)(2,1)S(1)}, u32[]{:S(2)}, u32[]{:S(2)}) collective-permute-start(bf16[128,1024]{1,0:T(8,128)(2,1)S(1)} %add_convert_fusion.1), channel_id=1, source_target_pairs={{0,8},{4,12},{8,16},{12,20},{16,24},{20,28},{1,9},{5,13},{9,17},{1... | collective-permute-start | bytes 786440 | tf_op jit(solution)/shard_map/ppermute | solution.py:238
  152.6 8.9 %collective-permute-start.29 = (bf16[128,1024]{1,0:T(8,128)(2,1)S(1)}, bf16[128,1024]{1,0:T(8,128)(2,1)S(1)}, u32[]{:S(2)}, u32[]{:S(2)}) collective-permute-start(bf16[128,1024]{1,0:T(8,128)(2,1)S(1)} %add_convert_fusion.1), channel_id=1, source_target_pairs={{0,12},{4,8},{8,20},{12,16},{16,28},{20,24},{1,13},{5,9},{9,21},{1... | collective-permute-start | bytes 786440 | tf_op jit(solution)/shard_map/ppermute | solution.py:238
  162.2 10.9 %collective-permute-start.28 = (bf16[3,128,256]{2,1,0:T(8,128)(2,1)S(1)}, bf16[3,128,256]{2,1,0:T(8,128)(2,1)S(1)}, u32[]{:S(2)}, u32[]{:S(2)}) collective-permute-start(bf16[3,128,256]{2,1,0:T(8,128)(2,1)S(1)} %pad_maximum_fusion.7), channel_id=1, source_target_pairs={{24,0},{28,4},{25,1},{29,5},{26,2},{30,6},{27,3},{31,7}} | collective-permute-start | bytes 589832 | tf_op jit(solution)/shard_map/ppermute | solution.py:238
  163.6 10.9 %collective-permute-start.27 = (bf16[3,128,256]{2,1,0:T(8,128)(2,1)S(1)}, bf16[3,128,256]{2,1,0:T(8,128)(2,1)S(1)}, u32[]{:S(2)}, u32[]{:S(2)}) collective-permute-start(bf16[3,128,256]{2,1,0:T(8,128)(2,1)S(1)} %pad_maximum_fusion.6), channel_id=1, source_target_pairs={{24,8},{28,12},{25,9},{29,13},{26,10},{30,14},{27,11},{31,15}} | collective-permute-start | bytes 589832 | tf_op jit(solution)/shard_map/ppermute | solution.py:238
  164.3 10.2 %collective-permute-start.26 = (bf16[3,128,256]{2,1,0:T(8,128)(2,1)S(1)}, bf16[3,128,256]{2,1,0:T(8,128)(2,1)S(1)}, u32[]{:S(2)}, u32[]{:S(2)}) collective-permute-start(bf16[3,128,256]{2,1,0:T(8,128)(2,1)S(1)} %pad_maximum_fusion.5), channel_id=1, source_target_pairs={{24,16},{28,20},{25,17},{29,21},{26,18},{30,22},{27,19},{31,23}} | collective-permute-start | bytes 589832 | tf_op jit(solution)/shard_map/ppermute | solution.py:238
  173.2 7.9 %collective-permute-start.34 = (bf16[1,128,256]{2,1,0:T(8,128)(2,1)S(1)}, bf16[1,128,256]{2,1,0:T(8,128)(2,1)S(1)}, u32[]{:S(2)}, u32[]{:S(2)}) collective-permute-start(bf16[1,128,256]{2,1,0:T(8,128)(2,1)S(1)} %get-tuple-element.147), channel_id=1, source_target_pairs={{24,0},{28,4},{25,1},{29,5},{26,2},{30,6},{27,3},{31,7}} | collective-permute-start | bytes 196616 | tf_op jit(solution)/shard_map/ppermute | solution.py:238
  (18 other events, 88.6 us)

commit v5 on v4

--- a/solution.py
+++ b/solution.py
@@ -237,17 +237,18 @@
     def permute(value, pairs):
         return lax.ppermute(value, axis, pairs)
 
-    def partners(k):
+    def partners(k, sections=range(SECTIONS)):
         return [
             (p * group + q, p * group + (q + k) % group)
-            for p in range(SECTIONS)
+            for p in sections
             for q in range(group)
         ]
 
-    def onward(k):
+    def onward(k, sections):
         return [
             (p * group + q, (p + 1) * group + (q + k) % group)
-            for p in range(SECTIONS - 1)
+            for p in sections
+            if p < SECTIONS - 1
             for q in range(group)
         ]
 
@@ -294,7 +295,7 @@
         mine = lax.optimization_barrier(mine)
         parts = [mine]
         for k in range(1, group):
-            parts.append([permute(v, partners(k)) for v in mine])
+            parts.append([permute(v, partners(k, (0, 2))) for v in mine])
         entry[b] = parts
 
 
@@ -410,6 +411,7 @@
         exits.append(result)
 
     for t in range(periods):
+        live = [p for p in range(SECTIONS) if 0 <= t - p < batches]
         sends, mix = rest(fed, partial, token)
         bases = tail(fed, mix)
         taken = [
@@ -430,7 +432,7 @@
             done.append(total)
             if t + 1 < periods:
                 for k in range(group):
-                    came[k][c] = permute(total, onward(k))
+                    came[k][c] = permute(total, onward(k, live))
         if t == 0:
             late[0] = gated(late[0], done)
             enter(1)

time: 183 us -> 195 us (1.066)
  waiting for transfers between devices: 71.2 us -> 97.6 us
  starting transfers between devices: 80.4 us -> 66.1 us
    ppermute x35, waiting for transfers between devices: 71.2 us -> 97.6 us  [permute(): return lax.ppermute(value, axis, pairs)]
    ppermute x35, starting transfers between devices: 80.4 us -> 66.1 us  [permute(): return lax.ppermute(value, axis, pairs)]
  transfers between devices with their start and end apart: 35 -> 35, of which waited for: 22 -> 18; matrix products, arithmetic and copies ran while one was open for 1% -> 1% of each run, Pallas kernels for 3% -> 3%
where the time goes in v5:
time: 195 us; the launch traced here: 194 us
  waiting for transfers between devices  97.6 us (50%)
  starting transfers between devices  66.1 us (34%)
  Pallas kernels  15.4 us (8%)
  local copies, waits for them, and re-layouts  10.3 us (5%)
  other arithmetic  3.93 us (2%)
    ppermute x35, waiting for transfers between devices, permute(): return lax.ppermute(value, axis, pairs)  97.6 us
    ppermute x35, starting transfers between devices, permute(): return lax.ppermute(value, axis, pairs)  66.1 us
    unnamed x14, local copies, waits for them, and re-layouts  10.2 us
    pallas_call x7, Pallas kernels, rest(): pl.pallas_call(functools.partial(rest_kernel, group, same, t, batches), o...  9.19 us
    pallas_call x7, Pallas kernels, own(): pl.pallas_call(functools.partial(own_kernel, group, same, t, batches), ou...  4.24 us
  transfers between devices with their start and end apart: 35, of which 18 were waited for; matrix products, arithmetic and copies ran while one was open for 1% of the time, Pallas kernels for 3%

profile of v5, /device:TPU:0, one launch (start us, length us, event | category | flops | bytes accessed | tf_op | source)
XLA Modules:
  0.0 194.1 jit_solution(4710753560254383924)
XLA Ops:
  0.9 6.0 %collective-permute-start.3 = (bf16[1,128,256]{2,1,0:T(8,128)(2,1)S(1)}, bf16[1,128,256]{2,1,0:T(8,128)(2,1)S(1)}, u32[]{:S(2)}, u32[]{:S(2)}) collective-permute-start(bf16[1,128,256]{2,1,0:T(8,128)(2,1)S(1)} %get-tuple-element.64), channel_id=1, source_target_pairs={{16,0},{20,4},{0,16},{4,20},{17,1},{21,5},{1,17},{5,21},{18,2},{22... | collective-permute-start | bytes 196616 | tf_op jit(solution)/shard_map/ppermute | solution.py:238
  9.5 3.5 %collective-permute-done.4 = bf16[1,128,256]{2,1,0:T(8,128)(2,1)S(1)} collective-permute-done((bf16[1,128,256]{2,1,0:T(8,128)(2,1)S(1)}, bf16[1,128,256]{2,1,0:T(8,128)(2,1)S(1)}, u32[]{:S(2)}, u32[]{:S(2)}) %collective-permute-start.4) | collective-permute-done | bytes 65568 | tf_op jit(solution)/shard_map/ppermute | solution.py:238
  13.0 3.1 %collective-permute-done.5 = bf16[1,128,256]{2,1,0:T(8,128)(2,1)S(1)} collective-permute-done((bf16[1,128,256]{2,1,0:T(8,128)(2,1)S(1)}, bf16[1,128,256]{2,1,0:T(8,128)(2,1)S(1)}, u32[]{:S(2)}, u32[]{:S(2)}) %collective-permute-start.5) | collective-permute-done | bytes 65568 | tf_op jit(solution)/shard_map/ppermute | solution.py:238
  16.2 3.4 %collective-permute-start.6 = (bf16[128,1024]{1,0:T(8,128)(2,1)S(1)}, bf16[128,1024]{1,0:T(8,128)(2,1)S(1)}, u32[]{:S(2)}, u32[]{:S(2)}) collective-permute-start(bf16[128,1024]{1,0:T(8,128)(2,1)S(1)} %pad_maximum_fusion.refs_0_), channel_id=1, source_target_pairs={{0,4},{4,0},{16,20},{20,16},{1,5},{5,1},{17,21},{21,17},{2,6},{6,2... | collective-permute-start | bytes 786440 | tf_op jit(solution)/shard_map/ppermute | solution.py:238
  20.6 4.6 %copy-done = bf16[1,2048,3072]{2,1,0:T(8,128)(2,1)S(1)} copy-done((bf16[1,2048,3072]{2,1,0:T(8,128)(2,1)S(1)}, bf16[1,2048,3072]{2,1,0:T(8,128)(2,1)}, u32[]{:S(2)}) %copy-start) | copy-done | bytes 12582936
  25.9 3.8 %copy-done.1 = bf16[1,2048,3072]{2,1,0:T(8,128)(2,1)S(1)} copy-done((bf16[1,2048,3072]{2,1,0:T(8,128)(2,1)S(1)}, bf16[1,2048,3072]{2,1,0:T(8,128)(2,1)}, u32[]{:S(2)}) %copy-start.1) | copy-done | bytes 12582936
  40.7 4.8 %collective-permute-start.12 = (bf16[128,1024]{1,0:T(8,128)(2,1)S(1)}, bf16[128,1024]{1,0:T(8,128)(2,1)S(1)}, u32[]{:S(2)}, u32[]{:S(2)}) collective-permute-start(bf16[128,1024]{1,0:T(8,128)(2,1)S(1)} %add_convert_fusion.6), channel_id=1, source_target_pairs={{0,8},{4,12},{1,9},{5,13},{2,10},{6,14},{3,11},{7,15}} | collective-permute-start | bytes 786440 | tf_op jit(solution)/shard_map/ppermute | solution.py:238
  50.0 3.4 %collective-permute-start.10 = (bf16[128,1024]{1,0:T(8,128)(2,1)S(1)}, bf16[128,1024]{1,0:T(8,128)(2,1)S(1)}, u32[]{:S(2)}, u32[]{:S(2)}) collective-permute-start(bf16[128,1024]{1,0:T(8,128)(2,1)S(1)} %pad_maximum_fusion.3), channel_id=1, source_target_pairs={{0,4},{4,0},{16,20},{20,16},{1,5},{5,1},{17,21},{21,17},{2,6},{6,2... | collective-permute-start | bytes 786440 | tf_op jit(solution)/shard_map/ppermute | solution.py:238
  54.6 5.0 %collective-permute-done.10 = bf16[128,1024]{1,0:T(8,128)(2,1)S(1)} collective-permute-done((bf16[128,1024]{1,0:T(8,128)(2,1)S(1)}, bf16[128,1024]{1,0:T(8,128)(2,1)S(1)}, u32[]{:S(2)}, u32[]{:S(2)}) %collective-permute-start.10) | collective-permute-done | bytes 262176 | tf_op jit(solution)/shard_map/ppermute | solution.py:238
  64.4 5.4 %collective-permute-done.13 = bf16[128,1024]{1,0:T(8,128)(2,1)S(1)} collective-permute-done((bf16[128,1024]{1,0:T(8,128)(2,1)S(1)}, bf16[128,1024]{1,0:T(8,128)(2,1)S(1)}, u32[]{:S(2)}, u32[]{:S(2)}) %collective-permute-start.13) | collective-permute-done | bytes 262176 | tf_op jit(solution)/shard_map/ppermute | solution.py:238
  71.2 4.4 %collective-permute-start.9 = (bf16[128,1024]{1,0:T(8,128)(2,1)S(1)}, bf16[128,1024]{1,0:T(8,128)(2,1)S(1)}, u32[]{:S(2)}, u32[]{:S(2)}) collective-permute-start(bf16[128,1024]{1,0:T(8,128)(2,1)S(1)} %pad_maximum_fusion.2), channel_id=1, source_target_pairs={{0,4},{4,0},{16,20},{20,16},{1,5},{5,1},{17,21},{21,17},{2,6},{6,2... | collective-permute-start | bytes 786440 | tf_op jit(solution)/shard_map/ppermute | solution.py:238
  86.5 5.9 %collective-permute-done.16 = bf16[128,1024]{1,0:T(8,128)(2,1)S(1)} collective-permute-done((bf16[128,1024]{1,0:T(8,128)(2,1)S(1)}, bf16[128,1024]{1,0:T(8,128)(2,1)S(1)}, u32[]{:S(2)}, u32[]{:S(2)}) %collective-permute-start.16) | collective-permute-done | bytes 262176 | tf_op jit(solution)/shard_map/ppermute | solution.py:238
  92.4 3.4 %collective-permute-start.18 = (bf16[128,1024]{1,0:T(8,128)(2,1)S(1)}, bf16[128,1024]{1,0:T(8,128)(2,1)S(1)}, u32[]{:S(2)}, u32[]{:S(2)}) collective-permute-start(bf16[128,1024]{1,0:T(8,128)(2,1)S(1)} %add_convert_fusion.4), channel_id=1, source_target_pairs={{0,8},{4,12},{8,16},{12,20},{16,24},{20,28},{1,9},{5,13},{9,17},{1... | collective-permute-start | bytes 786440 | tf_op jit(solution)/shard_map/ppermute | solution.py:238
  95.9 4.4 %collective-permute-start.8 = (bf16[128,1024]{1,0:T(8,128)(2,1)S(1)}, bf16[128,1024]{1,0:T(8,128)(2,1)S(1)}, u32[]{:S(2)}, u32[]{:S(2)}) collective-permute-start(bf16[128,1024]{1,0:T(8,128)(2,1)S(1)} %pad_maximum_fusion.1), channel_id=1, source_target_pairs={{0,4},{4,0},{16,20},{20,16},{1,5},{5,1},{17,21},{21,17},{2,6},{6,2... | collective-permute-start | bytes 786440 | tf_op jit(solution)/shard_map/ppermute | solution.py:238
  102.7 3.5 %collective-permute-done.17 = bf16[128,1024]{1,0:T(8,128)(2,1)S(1)} collective-permute-done((bf16[128,1024]{1,0:T(8,128)(2,1)S(1)}, bf16[128,1024]{1,0:T(8,128)(2,1)S(1)}, u32[]{:S(2)}, u32[]{:S(2)}) %collective-permute-start.17) | collective-permute-done | bytes 262176 | tf_op jit(solution)/shard_map/ppermute | solution.py:238
  109.5 5.4 %collective-permute-done.19 = bf16[128,1024]{1,0:T(8,128)(2,1)S(1)} collective-permute-done((bf16[128,1024]{1,0:T(8,128)(2,1)S(1)}, bf16[128,1024]{1,0:T(8,128)(2,1)S(1)}, u32[]{:S(2)}, u32[]{:S(2)}) %collective-permute-start.19) | collective-permute-done | bytes 262176 | tf_op jit(solution)/shard_map/ppermute | solution.py:238
  115.0 4.2 %collective-permute-start.21 = (bf16[128,1024]{1,0:T(8,128)(2,1)S(1)}, bf16[128,1024]{1,0:T(8,128)(2,1)S(1)}, u32[]{:S(2)}, u32[]{:S(2)}) collective-permute-start(bf16[128,1024]{1,0:T(8,128)(2,1)S(1)} %add_convert_fusion.3), channel_id=1, source_target_pairs={{0,8},{4,12},{8,16},{12,20},{16,24},{20,28},{1,9},{5,13},{9,17},{1... | collective-permute-start | bytes 786440 | tf_op jit(solution)/shard_map/ppermute | solution.py:238
  119.3 3.5 %collective-permute-start.20 = (bf16[128,1024]{1,0:T(8,128)(2,1)S(1)}, bf16[128,1024]{1,0:T(8,128)(2,1)S(1)}, u32[]{:S(2)}, u32[]{:S(2)}) collective-permute-start(bf16[128,1024]{1,0:T(8,128)(2,1)S(1)} %add_convert_fusion.3), channel_id=1, source_target_pairs={{0,12},{4,8},{8,20},{12,16},{16,28},{20,24},{1,13},{5,9},{9,21},{1... | collective-permute-start | bytes 786440 | tf_op jit(solution)/shard_map/ppermute | solution.py:238
  123.2 3.5 %collective-permute-done.20.refs_0_ = bf16[128,1024]{1,0:T(8,128)(2,1)S(1)} collective-permute-done((bf16[128,1024]{1,0:T(8,128)(2,1)S(1)}, bf16[128,1024]{1,0:T(8,128)(2,1)S(1)}, u32[]{:S(2)}, u32[]{:S(2)}) %collective-permute-start.20) | collective-permute-done | bytes 262176 | tf_op jit(solution)/shard_map/ppermute | solution.py:238
  128.3 6.9 %collective-permute-done.22 = bf16[128,1024]{1,0:T(8,128)(2,1)S(1)} collective-permute-done((bf16[128,1024]{1,0:T(8,128)(2,1)S(1)}, bf16[128,1024]{1,0:T(8,128)(2,1)S(1)}, u32[]{:S(2)}, u32[]{:S(2)}) %collective-permute-start.22) | collective-permute-done | bytes 262176 | tf_op jit(solution)/shard_map/ppermute | solution.py:238
  137.2 6.0 %collective-permute-done.25 = bf16[128,1024]{1,0:T(8,128)(2,1)S(1)} collective-permute-done((bf16[128,1024]{1,0:T(8,128)(2,1)S(1)}, bf16[128,1024]{1,0:T(8,128)(2,1)S(1)}, u32[]{:S(2)}, u32[]{:S(2)}) %collective-permute-start.25) | collective-permute-done | bytes 262176 | tf_op jit(solution)/shard_map/ppermute | solution.py:238
  148.1 3.3 %collective-permute-done.31 = bf16[128,1024]{1,0:T(8,128)(2,1)S(1)} collective-permute-done((bf16[128,1024]{1,0:T(8,128)(2,1)S(1)}, bf16[128,1024]{1,0:T(8,128)(2,1)S(1)}, u32[]{:S(2)}, u32[]{:S(2)}) %collective-permute-start.31) | collective-permute-done | bytes 262176 | tf_op jit(solution)/shard_map/ppermute | solution.py:238
  152.9 32.5 %collective-permute-done.28 = bf16[3,128,256]{2,1,0:T(8,128)(2,1)S(1)} collective-permute-done((bf16[3,128,256]{2,1,0:T(8,128)(2,1)S(1)}, bf16[3,128,256]{2,1,0:T(8,128)(2,1)S(1)}, u32[]{:S(2)}, u32[]{:S(2)}) %collective-permute-start.28) | collective-permute-done | bytes 196640 | tf_op jit(solution)/shard_map/ppermute | solution.py:238
  186.8 6.5 %collective-permute-done.34 = bf16[1,128,256]{2,1,0:T(8,128)(2,1)S(1)} collective-permute-done((bf16[1,128,256]{2,1,0:T(8,128)(2,1)S(1)}, bf16[1,128,256]{2,1,0:T(8,128)(2,1)S(1)}, u32[]{:S(2)}, u32[]{:S(2)}) %collective-permute-start.34) | collective-permute-done | bytes 65568 | tf_op jit(solution)/shard_map/ppermute | solution.py:238
  (122 shorter events, 56.9 us)
Async XLA Ops:
  0.9 8.6 %collective-permute-start.3 = (bf16[1,128,256]{2,1,0:T(8,128)(2,1)S(1)}, bf16[1,128,256]{2,1,0:T(8,128)(2,1)S(1)}, u32[]{:S(2)}, u32[]{:S(2)}) collective-permute-start(bf16[1,128,256]{2,1,0:T(8,128)(2,1)S(1)} %get-tuple-element.64), channel_id=1, source_target_pairs={{16,0},{20,4},{0,16},{4,20},{17,1},{21,5},{1,17},{5,21},{18,2},{22... | collective-permute-start | bytes 196616 | tf_op jit(solution)/shard_map/ppermute | solution.py:238
  8.2 8.0 %collective-permute-start.5 = (bf16[1,128,256]{2,1,0:T(8,128)(2,1)S(1)}, bf16[1,128,256]{2,1,0:T(8,128)(2,1)S(1)}, u32[]{:S(2)}, u32[]{:S(2)}) collective-permute-start(bf16[1,128,256]{2,1,0:T(8,128)(2,1)S(1)} %get-tuple-element.66), channel_id=1, source_target_pairs={{24,0},{28,4},{8,16},{12,20},{25,1},{29,5},{9,17},{13,21},{26,2},{... | collective-permute-start | bytes 196616 | tf_op jit(solution)/shard_map/ppermute | solution.py:238
  16.2 14.6 %collective-permute-start.6 = (bf16[128,1024]{1,0:T(8,128)(2,1)S(1)}, bf16[128,1024]{1,0:T(8,128)(2,1)S(1)}, u32[]{:S(2)}, u32[]{:S(2)}) collective-permute-start(bf16[128,1024]{1,0:T(8,128)(2,1)S(1)} %pad_maximum_fusion.refs_0_), channel_id=1, source_target_pairs={{0,4},{4,0},{16,20},{20,16},{1,5},{5,1},{17,21},{21,17},{2,6},{6,2... | collective-permute-start | bytes 786440 | tf_op jit(solution)/shard_map/ppermute | solution.py:238
  34.8 15.1 %collective-permute-start = (bf16[3,128,256]{2,1,0:T(8,128)(2,1)S(1)}, bf16[3,128,256]{2,1,0:T(8,128)(2,1)S(1)}, u32[]{:S(2)}, u32[]{:S(2)}) collective-permute-start(bf16[3,128,256]{2,1,0:T(8,128)(2,1)S(1)} %get-tuple-element.60), channel_id=1, source_target_pairs={{8,0},{12,4},{24,16},{28,20},{9,1},{13,5},{25,17},{29,21},{10,2},{... | collective-permute-start | bytes 589832 | tf_op jit(solution)/shard_map/ppermute | solution.py:238
  36.1 13.8 %collective-permute-start.1 = (bf16[3,128,256]{2,1,0:T(8,128)(2,1)S(1)}, bf16[3,128,256]{2,1,0:T(8,128)(2,1)S(1)}, u32[]{:S(2)}, u32[]{:S(2)}) collective-permute-start(bf16[3,128,256]{2,1,0:T(8,128)(2,1)S(1)} %get-tuple-element.61), channel_id=1, source_target_pairs={{16,0},{20,4},{0,16},{4,20},{17,1},{21,5},{1,17},{5,21},{18,2},{22... | collective-permute-start | bytes 589832 | tf_op jit(solution)/shard_map/ppermute | solution.py:238
  38.1 11.8 %collective-permute-start.2 = (bf16[3,128,256]{2,1,0:T(8,128)(2,1)S(1)}, bf16[3,128,256]{2,1,0:T(8,128)(2,1)S(1)}, u32[]{:S(2)}, u32[]{:S(2)}) collective-permute-start(bf16[3,128,256]{2,1,0:T(8,128)(2,1)S(1)} %get-tuple-element.62), channel_id=1, source_target_pairs={{24,0},{28,4},{8,16},{12,20},{25,1},{29,5},{9,17},{13,21},{26,2},{... | collective-permute-start | bytes 589832 | tf_op jit(solution)/shard_map/ppermute | solution.py:238
  40.7 12.7 %collective-permute-start.12 = (bf16[128,1024]{1,0:T(8,128)(2,1)S(1)}, bf16[128,1024]{1,0:T(8,128)(2,1)S(1)}, u32[]{:S(2)}, u32[]{:S(2)}) collective-permute-start(bf16[128,1024]{1,0:T(8,128)(2,1)S(1)} %add_convert_fusion.6), channel_id=1, source_target_pairs={{0,8},{4,12},{1,9},{5,13},{2,10},{6,14},{3,11},{7,15}} | collective-permute-start | bytes 786440 | tf_op jit(solution)/shard_map/ppermute | solution.py:238
  45.5 9.0 %collective-permute-start.11 = (bf16[128,1024]{1,0:T(8,128)(2,1)S(1)}, bf16[128,1024]{1,0:T(8,128)(2,1)S(1)}, u32[]{:S(2)}, u32[]{:S(2)}) collective-permute-start(bf16[128,1024]{1,0:T(8,128)(2,1)S(1)} %add_convert_fusion.6), channel_id=1, source_target_pairs={{0,12},{4,8},{1,13},{5,9},{2,14},{6,10},{3,15},{7,11}} | collective-permute-start | bytes 786440 | tf_op jit(solution)/shard_map/ppermute | solution.py:238
  50.0 9.6 %collective-permute-start.10 = (bf16[128,1024]{1,0:T(8,128)(2,1)S(1)}, bf16[128,1024]{1,0:T(8,128)(2,1)S(1)}, u32[]{:S(2)}, u32[]{:S(2)}) collective-permute-start(bf16[128,1024]{1,0:T(8,128)(2,1)S(1)} %pad_maximum_fusion.3), channel_id=1, source_target_pairs={{0,4},{4,0},{16,20},{20,16},{1,5},{5,1},{17,21},{21,17},{2,6},{6,2... | collective-permute-start | bytes 786440 | tf_op jit(solution)/shard_map/ppermute | solution.py:238
  61.9 7.9 %collective-permute-start.13 = (bf16[128,1024]{1,0:T(8,128)(2,1)S(1)}, bf16[128,1024]{1,0:T(8,128)(2,1)S(1)}, u32[]{:S(2)}, u32[]{:S(2)}) collective-permute-start(bf16[128,1024]{1,0:T(8,128)(2,1)S(1)} %get-tuple-element.79), channel_id=1, source_target_pairs={{0,4},{4,0},{8,12},{12,8},{16,20},{20,16},{24,28},{28,24},{1,5},{5... | collective-permute-start | bytes 786440 | tf_op jit(solution)/shard_map/ppermute | solution.py:238
  69.9 7.1 %collective-permute-start.15 = (bf16[128,1024]{1,0:T(8,128)(2,1)S(1)}, bf16[128,1024]{1,0:T(8,128)(2,1)S(1)}, u32[]{:S(2)}, u32[]{:S(2)}) collective-permute-start(bf16[128,1024]{1,0:T(8,128)(2,1)S(1)} %add_convert_fusion.5), channel_id=1, source_target_pairs={{0,8},{4,12},{8,16},{12,20},{1,9},{5,13},{9,17},{13,21},{2,10},{6,... | collective-permute-start | bytes 786440 | tf_op jit(solution)/shard_map/ppermute | solution.py:238
  71.2 10.6 %collective-permute-start.9 = (bf16[128,1024]{1,0:T(8,128)(2,1)S(1)}, bf16[128,1024]{1,0:T(8,128)(2,1)S(1)}, u32[]{:S(2)}, u32[]{:S(2)}) collective-permute-start(bf16[128,1024]{1,0:T(8,128)(2,1)S(1)} %pad_maximum_fusion.2), channel_id=1, source_target_pairs={{0,4},{4,0},{16,20},{20,16},{1,5},{5,1},{17,21},{21,17},{2,6},{6,2... | collective-permute-start | bytes 786440 | tf_op jit(solution)/shard_map/ppermute | solution.py:238
  84.2 8.2 %collective-permute-start.16 = (bf16[128,1024]{1,0:T(8,128)(2,1)S(1)}, bf16[128,1024]{1,0:T(8,128)(2,1)S(1)}, u32[]{:S(2)}, u32[]{:S(2)}) collective-permute-start(bf16[128,1024]{1,0:T(8,128)(2,1)S(1)} %get-tuple-element.84), channel_id=1, source_target_pairs={{0,4},{4,0},{8,12},{12,8},{16,20},{20,16},{24,28},{28,24},{1,5},{5... | collective-permute-start | bytes 786440 | tf_op jit(solution)/shard_map/ppermute | solution.py:238
  92.4 9.2 %collective-permute-start.18 = (bf16[128,1024]{1,0:T(8,128)(2,1)S(1)}, bf16[128,1024]{1,0:T(8,128)(2,1)S(1)}, u32[]{:S(2)}, u32[]{:S(2)}) collective-permute-start(bf16[128,1024]{1,0:T(8,128)(2,1)S(1)} %add_convert_fusion.4), channel_id=1, source_target_pairs={{0,8},{4,12},{8,16},{12,20},{16,24},{20,28},{1,9},{5,13},{9,17},{1... | collective-permute-start | bytes 786440 | tf_op jit(solution)/shard_map/ppermute | solution.py:238
  95.9 10.3 %collective-permute-start.8 = (bf16[128,1024]{1,0:T(8,128)(2,1)S(1)}, bf16[128,1024]{1,0:T(8,128)(2,1)S(1)}, u32[]{:S(2)}, u32[]{:S(2)}) collective-permute-start(bf16[128,1024]{1,0:T(8,128)(2,1)S(1)} %pad_maximum_fusion.1), channel_id=1, source_target_pairs={{0,4},{4,0},{16,20},{20,16},{1,5},{5,1},{17,21},{21,17},{2,6},{6,2... | collective-permute-start | bytes 786440 | tf_op jit(solution)/shard_map/ppermute | solution.py:238
  115.0 8.1 %collective-permute-start.21 = (bf16[128,1024]{1,0:T(8,128)(2,1)S(1)}, bf16[128,1024]{1,0:T(8,128)(2,1)S(1)}, u32[]{:S(2)}, u32[]{:S(2)}) collective-permute-start(bf16[128,1024]{1,0:T(8,128)(2,1)S(1)} %add_convert_fusion.3), channel_id=1, source_target_pairs={{0,8},{4,12},{8,16},{12,20},{16,24},{20,28},{1,9},{5,13},{9,17},{1... | collective-permute-start | bytes 786440 | tf_op jit(solution)/shard_map/ppermute | solution.py:238
  119.3 7.4 %collective-permute-start.20 = (bf16[128,1024]{1,0:T(8,128)(2,1)S(1)}, bf16[128,1024]{1,0:T(8,128)(2,1)S(1)}, u32[]{:S(2)}, u32[]{:S(2)}) collective-permute-start(bf16[128,1024]{1,0:T(8,128)(2,1)S(1)} %add_convert_fusion.3), channel_id=1, source_target_pairs={{0,12},{4,8},{8,20},{12,16},{16,28},{20,24},{1,13},{5,9},{9,21},{1... | collective-permute-start | bytes 786440 | tf_op jit(solution)/shard_map/ppermute | solution.py:238
  126.8 8.4 %collective-permute-start.22 = (bf16[128,1024]{1,0:T(8,128)(2,1)S(1)}, bf16[128,1024]{1,0:T(8,128)(2,1)S(1)}, u32[]{:S(2)}, u32[]{:S(2)}) collective-permute-start(bf16[128,1024]{1,0:T(8,128)(2,1)S(1)} %get-tuple-element.94), channel_id=1, source_target_pairs={{0,4},{4,0},{8,12},{12,8},{16,20},{20,16},{24,28},{28,24},{1,5},{5... | collective-permute-start | bytes 786440 | tf_op jit(solution)/shard_map/ppermute | solution.py:238
  145.4 40.0 %collective-permute-start.28 = (bf16[3,128,256]{2,1,0:T(8,128)(2,1)S(1)}, bf16[3,128,256]{2,1,0:T(8,128)(2,1)S(1)}, u32[]{:S(2)}, u32[]{:S(2)}) collective-permute-start(bf16[3,128,256]{2,1,0:T(8,128)(2,1)S(1)} %pad_maximum_fusion.7), channel_id=1, source_target_pairs={{24,0},{28,4},{25,1},{29,5},{26,2},{30,6},{27,3},{31,7}} | collective-permute-start | bytes 589832 | tf_op jit(solution)/shard_map/ppermute | solution.py:238
  146.7 40.0 %collective-permute-start.27 = (bf16[3,128,256]{2,1,0:T(8,128)(2,1)S(1)}, bf16[3,128,256]{2,1,0:T(8,128)(2,1)S(1)}, u32[]{:S(2)}, u32[]{:S(2)}) collective-permute-start(bf16[3,128,256]{2,1,0:T(8,128)(2,1)S(1)} %pad_maximum_fusion.6), channel_id=1, source_target_pairs={{24,8},{28,12},{25,9},{29,13},{26,10},{30,14},{27,11},{31,15}} | collective-permute-start | bytes 589832 | tf_op jit(solution)/shard_map/ppermute | solution.py:238
  147.4 39.3 %collective-permute-start.26 = (bf16[3,128,256]{2,1,0:T(8,128)(2,1)S(1)}, bf16[3,128,256]{2,1,0:T(8,128)(2,1)S(1)}, u32[]{:S(2)}, u32[]{:S(2)}) collective-permute-start(bf16[3,128,256]{2,1,0:T(8,128)(2,1)S(1)} %pad_maximum_fusion.5), channel_id=1, source_target_pairs={{24,16},{28,20},{25,17},{29,21},{26,18},{30,22},{27,19},{31,23}} | collective-permute-start | bytes 589832 | tf_op jit(solution)/shard_map/ppermute | solution.py:238
  151.5 35.3 %collective-permute-start.32 = (bf16[1,128,256]{2,1,0:T(8,128)(2,1)S(1)}, bf16[1,128,256]{2,1,0:T(8,128)(2,1)S(1)}, u32[]{:S(2)}, u32[]{:S(2)}) collective-permute-start(bf16[1,128,256]{2,1,0:T(8,128)(2,1)S(1)} %get-tuple-element.149), channel_id=1, source_target_pairs={{24,16},{28,20},{25,17},{29,21},{26,18},{30,22},{27,19},{31,23}} | collective-permute-start | bytes 196616 | tf_op jit(solution)/shard_map/ppermute | solution.py:238
  152.2 34.6 %collective-permute-start.33 = (bf16[1,128,256]{2,1,0:T(8,128)(2,1)S(1)}, bf16[1,128,256]{2,1,0:T(8,128)(2,1)S(1)}, u32[]{:S(2)}, u32[]{:S(2)}) collective-permute-start(bf16[1,128,256]{2,1,0:T(8,128)(2,1)S(1)} %get-tuple-element.148), channel_id=1, source_target_pairs={{24,8},{28,12},{25,9},{29,13},{26,10},{30,14},{27,11},{31,15}} | collective-permute-start | bytes 196616 | tf_op jit(solution)/shard_map/ppermute | solution.py:238
  185.4 7.9 %collective-permute-start.34 = (bf16[1,128,256]{2,1,0:T(8,128)(2,1)S(1)}, bf16[1,128,256]{2,1,0:T(8,128)(2,1)S(1)}, u32[]{:S(2)}, u32[]{:S(2)}) collective-permute-start(bf16[1,128,256]{2,1,0:T(8,128)(2,1)S(1)} %get-tuple-element.147), channel_id=1, source_target_pairs={{24,0},{28,4},{25,1},{29,5},{26,2},{30,6},{27,3},{31,7}} | collective-permute-start | bytes 196616 | tf_op jit(solution)/shard_map/ppermute | solution.py:238
  (18 other events, 66.2 us)
